TPU v7x, 512 devices: a whole 4x8x8 slice. The times are simulated.
512 devices in a mesh: ens: 4 (over z_lo), replica: 32 (over y_lo, x, core), model: 4 (over z_hi, y_hi).
Axes of the slice: x: 4, y: 8 (y_hi: 2, y_lo: 4; y = y_hi * 4 + y_lo), z: 8 (z_hi: 2, z_lo: 4; z = z_hi * 4 + z_lo), core: 2. Of those that a mesh axis runs over, the one named last changes fastest.
Arguments:
- slope_up: float32 [128, 768, 3072], P(('ens', 'replica'), None, 'model'), parts along dimension 0, may hold values from -1.25 to 1.25
- slope_down: float32 [128, 3072, 768], P(('ens', 'replica'), 'model'), parts along dimension 0, may hold values from -1.25 to 1.25
- slope_norm: float32 [128, 768], P(('ens', 'replica')), parts along dimension 0, may hold values from -12 to 12
- slope_bias: float32 [128, 768], P(('ens', 'replica')), parts along dimension 0, may hold values from -12 to 12
- param_up: float32 [3072, 3072], P(('ens', 'replica'), 'model'), parts along dimension 0, may hold values from -0.4375 to 0.4375
- param_down: float32 [12288, 768], P(('ens', 'model'), 'replica'), parts along dimension 0, may hold values from -0.21875 to 0.21875
- param_norm: float32 [3072], P(('ens', 'replica')), parts along dimension 0, may hold values from 0.25 to 1.75
- param_bias: float32 [3072], P(('ens', 'replica')), parts along dimension 0, may hold values from -3 to 3
Outputs:
- half_up: bfloat16 [3072, 3072], P('ens', 'model'), parts along dimension 0
- half_down: bfloat16 [12288, 768], P(('ens', 'model')), parts along dimension 0
- half_norm: bfloat16 [3072], P('ens'), parts along dimension 0
- half_bias: bfloat16 [3072], P('ens'), parts along dimension 0
- next_up: float32 [3072, 3072], P(('ens', 'replica'), 'model'), parts along dimension 0
- next_down: float32 [12288, 768], P(('ens', 'model'), 'replica'), parts along dimension 0
- next_norm: float32 [3072], P(('ens', 'replica')), parts along dimension 0
- next_bias: float32 [3072], P(('ens', 'replica')), parts along dimension 0
There are 4 independent parts, one for each index of `ens`. A program takes and returns all parts, laid end to end along the dimension named above; each array names one. Nothing has to cross between parts.
All inputs are finite; a program needn't handle non-finite values.
Results may differ from a plain program's by a relative error of at most 0.0004.
Values may be sent and summed in bfloat16 or wider, within the bound.
No kernel may reach another device: no remote copies, remote signals or barrier semaphores. Data moves between devices by JAX's collectives and lax.ppermute only.
A program may use at most 64 MiB of HBM per device.

v0:
```python
import jax
import jax.numpy as jnp
from jax import lax
from jax.sharding import Mesh
from jax.sharding import PartitionSpec as P

REPLICA = ("replica_0", "replica_1", "replica_2")
ENS_REPLICA = ("ens", "replica_0", "replica_1", "replica_2")


learn_rate = 0.4


def split_up(shard, dim, count):
    lengths = shard.shape
    tiles = shard.reshape(*lengths[:dim], count, lengths[dim] // count, *lengths[dim + 1 :])
    return jnp.moveaxis(tiles, dim, 0)


def sum_at_owner(shard, axis, dim):
    count = lax.axis_size(axis)
    tiles = lax.all_to_all(split_up(shard, dim, count), axis, 0, 0, tiled=True)
    return jnp.sum(tiles, axis=0)


def sum_by_axis(shard, axes, dim):
    far, near = axes
    tiles = split_up(shard, dim, lax.axis_size(far))
    nearer = sum_at_owner(tiles, near, dim + 1)
    arrived = lax.all_to_all(nearer, far, split_axis=0, concat_axis=0, tiled=True)
    return arrived.sum(axis=0)


def from_everyone(shard, axis):
    count = lax.axis_size(axis)
    return lax.all_to_all(
        jnp.broadcast_to(shard[None], (count, *shard.shape)), axis, 0, 0, tiled=True
    )


def taken_together(shard, axis):
    return from_everyone(shard, axis).sum(axis=0)


def together(arrays, axis):
    ends = [0]
    for a in arrays:
        ends.append(ends[-1] + a.size)
    total = taken_together(jnp.concatenate([a.ravel() for a in arrays]), axis)
    return tuple((total[b:e].reshape(a.shape) for a, b, e in zip(arrays, ends, ends[1:])))


def gather_turned(arrays, axis, dims):
    turned = [jnp.moveaxis(a, dim, 0) for a, dim in zip(arrays, dims)]
    both = jnp.concatenate([t.reshape(len(t), -1) for t in turned], axis=1)
    whole, at, outs = (lax.all_gather(both, axis, axis=0, tiled=True), 0, [])
    for t, dim in zip(turned, dims):
        section = whole[:, at : at + t[0].size].reshape(-1, *t.shape[1:])
        outs.append(jnp.moveaxis(section, 0, dim))
        at += t[0].size
    return tuple(outs)


def on_device(
    slope_up, slope_down, slope_norm, slope_bias, param_up, param_down, param_norm, param_bias
):
    mean_up, mean_down, mean_norm, mean_bias = (
        sum_by_axis(slope_up[0], (("replica_0", "replica_1"), "replica_2"), 0),
        sum_by_axis(slope_down[0], (("replica_0", "replica_1"), "replica_2"), 1),
        sum_by_axis(slope_norm[0], (("replica_0", "replica_1"), "replica_2"), 0),
        sum_by_axis(slope_bias[0], (("replica_0", "replica_1"), "replica_2"), 0),
    )
    mean_rate = lax.axis_size(REPLICA) ** (-0.5)
    mean_up = mean_up * mean_rate
    mean_down = mean_down * mean_rate
    mean_norm = mean_norm * mean_rate
    mean_bias = mean_bias * mean_rate
    own_up, own_down, slope_up_norm, slope_down_norm = together(
        (
            jnp.sum(param_up * param_up, axis=1, keepdims=True),
            jnp.sum(param_down * param_down, axis=0, keepdims=True),
            jnp.sum(mean_up * mean_up, axis=1, keepdims=True),
            jnp.sum(mean_down * mean_down, axis=0, keepdims=True),
        ),
        "model",
    )
    mean_up = mean_up * (jnp.sqrt(own_up) * lax.rsqrt(slope_up_norm + 1e-06))
    mean_down = mean_down * (jnp.sqrt(own_down) * lax.rsqrt(slope_down_norm + 1e-06))
    next_up = param_up - learn_rate * mean_up
    next_down = param_down - learn_rate * mean_down
    next_norm = param_norm - learn_rate * mean_norm
    next_bias = param_bias - learn_rate * mean_bias
    half_up, half_down, half_norm, half_bias = gather_turned(
        (
            next_up.astype(jnp.bfloat16),
            next_down.astype(jnp.bfloat16),
            next_norm.astype(jnp.bfloat16),
            next_bias.astype(jnp.bfloat16),
        ),
        REPLICA,
        (0, 1, 0, 0),
    )
    return (half_up, half_down, half_norm, half_bias, next_up, next_down, next_norm, next_bias)


def solution(mesh):
    split = Mesh(
        mesh.devices.reshape(mesh.shape["ens"], 4, 4, 2, mesh.shape["model"]),
        ("ens", "replica_0", "replica_1", "replica_2", "model"),
    )
    placed = (
        P(ENS_REPLICA, None, "model"),
        P(ENS_REPLICA, "model", None),
        P(ENS_REPLICA, None),
        P(ENS_REPLICA, None),
        P(ENS_REPLICA, "model"),
        P(("ens", "model"), REPLICA),
        P(ENS_REPLICA),
        P(ENS_REPLICA),
    )
    return jax.shard_map(
        on_device,
        mesh=split,
        in_specs=placed,
        out_specs=(
            P("ens", "model"),
            P(("ens", "model"), None),
            P("ens"),
            P("ens"),
            P(ENS_REPLICA, "model"),
            P(("ens", "model"), REPLICA),
            P(ENS_REPLICA),
            P(ENS_REPLICA),
        ),
        check_vma=False,
    )
```

profile of v0, /device:TPU:1, one launch (start us, length us, event | category | flops | bytes accessed | tf_op | source)
XLA Modules:
  0.0 228.4 jit_solution(1284755570534542590)
XLA Ops:
  7.2 0.7 reduce.3
  7.9 0.1 reshape_reshape_squeeze.10
  8.0 0.7 reshape.64
  8.6 10.0 %all-to-all-start.5 = ((f32[2,1,384]{2,1,0:T(1,128)}), f32[2,1,384]{2,1,0:T(1,128)S(1)}, u32[]{:S(2)}, u32[]{:S(2)}) async-start(f32[2,1,384]{2,1,0:T(1,128)} %reshape.64), calls=%async_computation.5 | async-start | bytes 6144 | tf_op jit(solution)/shard_map/all_to_all | solution.py:22
  18.7 0.7 reduce.4
  19.4 0.1 reshape_reshape_squeeze.11
  19.5 0.7 reshape.66
  20.2 0.0 all-to-all-done.5
  20.2 3.2 %all-to-all-start.7 = ((f32[2,1,384]{2,1,0:T(1,128)}), f32[2,1,384]{2,1,0:T(1,128)S(1)}, u32[]{:S(2)}, u32[]{:S(2)}) async-start(f32[2,1,384]{2,1,0:T(1,128)} %reshape.66), calls=%async_computation.7 | async-start | bytes 6144 | tf_op jit(solution)/shard_map/all_to_all | solution.py:22
  23.4 0.5 broadcast.24
  23.9 0.7 reduce.9
  24.6 0.1 reshape.65
  24.7 1.8 copy.47
  26.5 3.0 %copy.48 = f32[1,768,768]{1,2,0:T(8,128)} copy(f32[1,768,768]{2,1,0:T(8,128)} %param.9) | data formatting | bytes 4718592 | tf_op args[1]
  29.6 3.3 %copy.49 = f32[2,16,768,24]{2,3,1,0:T(8,128)} copy(f32[2,16,768,24]{2,3,0,1:T(8,128)} %bitcast.23) | data formatting | bytes 4718592 | tf_op jit(solution)/shard_map/transpose | solution.py:17
  32.8 0.6 reduce_sum.126
  33.4 0.0 all-to-all-done.7
  33.4 0.0 copy-start
  33.4 6.3 %all_to_all.54 = f32[2,16,24,768]{3,2,1,0:T(8,128)} all-to-all(f32[2,16,24,768]{3,2,1,0:T(8,128)S(1)} %copy.47), channel_id=1, replica_groups=mesh['ens'=4,'replica_0'=4,'replica_1'=4,'replica_2'=2,'model'=4] {'repl..., dimensions={0} | all-to-all | bytes 4718592 | tf_op jit(solution)/shard_map/all_to_all | solution.py:22
  39.7 0.0 copy-done
  39.7 5.6 %all_to_all.55 = f32[2,16,768,24]{2,3,1,0:T(8,128)S(1)} all-to-all(f32[2,16,768,24]{2,3,1,0:T(8,128)S(1)} %copy-done), channel_id=1, replica_groups=mesh['ens'=4,'replica_0'=4,'replica_1'=4,'replica_2'=2,'model'=4] {'repl..., dimensions={0} | all-to-all | bytes 4718592 | tf_op jit(solution)/shard_map/all_to_all | solution.py:22
  45.4 3.5 %all-to-all-start.6 = ((f32[16,1,24]{2,1,0:T(1,128)}), f32[16,1,24]{2,1,0:T(1,128)S(1)}, u32[]{:S(2)}, u32[]{:S(2)}) async-start(f32[16,1,24]{2,1,0:T(1,128)} %bitcast.9), calls=%async_computation.6 | async-start | bytes 16384 | tf_op jit(solution)/shard_map/all_to_all | solution.py:30
  48.8 0.7 reduce.10
  49.5 0.1 reshape.67
  49.6 0.6 reduce_sum.128
  50.2 5.3 %all-to-all-done.6 = f32[16,1,24]{2,1,0:T(1,128)S(1)} async-done(((f32[16,1,24]{2,1,0:T(1,128)}), f32[16,1,24]{2,1,0:T(1,128)S(1)}, u32[]{:S(2)}, u32[]{:S(2)}) %all-to-all-start.6) | async-done | bytes 1568 | tf_op jit(solution)/shard_map/all_to_all | solution.py:30
  55.5 3.5 %all-to-all-start.8 = ((f32[16,1,24]{2,1,0:T(1,128)}), f32[16,1,24]{2,1,0:T(1,128)S(1)}, u32[]{:S(2)}, u32[]{:S(2)}) async-start(f32[16,1,24]{2,1,0:T(1,128)} %bitcast.12), calls=%async_computation.8 | async-start | bytes 16384 | tf_op jit(solution)/shard_map/all_to_all | solution.py:30
  59.0 3.0 %reduce_sum.117 = f32[16,24,768]{2,1,0:T(8,128)} reduce(f32[2,16,24,768]{3,2,1,0:T(8,128)} %all_to_all.54, f32[]{:T(128)} %constant.5.clone.1), dimensions={0}, to_apply=%region_0.0 | reduce | flops 294912 | bytes 3538948 | tf_op jit(solution)/shard_map/reduce_sum | solution.py:23
  61.9 3.7 %all-to-all-done.8 = f32[16,1,24]{2,1,0:T(1,128)S(1)} async-done(((f32[16,1,24]{2,1,0:T(1,128)}), f32[16,1,24]{2,1,0:T(1,128)S(1)}, u32[]{:S(2)}, u32[]{:S(2)}) %all-to-all-start.8) | async-done | bytes 1568 | tf_op jit(solution)/shard_map/all_to_all | solution.py:30
  65.7 3.7 %all-to-all-start.1 = ((f32[16,24,768]{2,1,0:T(8,128)}), f32[16,24,768]{2,1,0:T(8,128)S(1)}, u32[]{:S(2)}, u32[]{:S(2)}) async-start(f32[16,24,768]{2,1,0:T(8,128)} %reduce_sum.117), calls=%async_computation.1 | async-start | bytes 2359296 | tf_op jit(solution)/shard_map/all_to_all | solution.py:30
  69.4 1.3 reduce_sum.122
  70.6 0.0 copy-start.1
  70.7 0.0 copy-start.3
  70.7 23.0 %all-to-all-done.1 = f32[16,24,768]{2,1,0:T(8,128)S(1)} async-done(((f32[16,24,768]{2,1,0:T(8,128)}), f32[16,24,768]{2,1,0:T(8,128)S(1)}, u32[]{:S(2)}, u32[]{:S(2)}) %all-to-all-start.1) | async-done | bytes 1179680 | tf_op jit(solution)/shard_map/all_to_all | solution.py:30
  93.7 8.4 %all-to-all-start.3 = ((f32[16,768,24]{1,2,0:T(8,128)}), f32[16,768,24]{1,2,0:T(8,128)S(1)}, u32[]{:S(2)}, u32[]{:S(2)}) async-start(f32[16,768,24]{1,2,0:T(8,128)} %reduce_sum.122), calls=%async_computation.3 | async-start | bytes 2359296 | tf_op jit(solution)/shard_map/all_to_all | solution.py:30
  102.1 0.0 copy-done.2
  102.1 0.1 multiply_reduce_fusion.3
  102.2 0.0 copy-done.1
  102.2 0.1 multiply_reduce_fusion.2
  102.4 0.0 copy-done.3
  102.4 0.5 convert_bitcast_fusion.2
  102.9 0.1 reduce_sum.118
  103.0 0.1 multiply_reduce_fusion.1
  103.1 23.3 %all-to-all-done.3 = f32[16,768,24]{1,2,0:T(8,128)S(1)} async-done(((f32[16,768,24]{1,2,0:T(8,128)}), f32[16,768,24]{1,2,0:T(8,128)S(1)}, u32[]{:S(2)}, u32[]{:S(2)}) %all-to-all-start.3) | async-done | bytes 1179680 | tf_op jit(solution)/shard_map/all_to_all | solution.py:30
  126.4 0.1 reduce_sum.123
  126.5 0.1 multiply_reduce_fusion
  126.6 0.1 pad_maximum_fusion
  126.7 0.6 broadcast_in_dim.2
  127.3 10.9 %all-to-all-start.4 = ((f32[4,1,96]{2,1,0:T(1,128)}), f32[4,1,96]{2,1,0:T(1,128)S(1)}, u32[]{:S(2)}, u32[]{:S(2)}) async-start(f32[4,1,96]{2,1,0:T(1,128)} %broadcast_in_dim.2), calls=%async_computation.4 | async-start | bytes 4096 | tf_op jit(solution)/shard_map/all_to_all | solution.py:36
  138.2 0.0 all-gather.2.cloned.1.call-start
  138.2 0.0 copy-done.4
  138.2 0.5 convert_bitcast_fusion.1
  138.7 0.1 copy.54
  138.8 0.1 copy.55
  138.9 10.6 %all-to-all-done.4 = f32[4,1,96]{2,1,0:T(1,128)S(1)} async-done(((f32[4,1,96]{2,1,0:T(1,128)}), f32[4,1,96]{2,1,0:T(1,128)S(1)}, u32[]{:S(2)}, u32[]{:S(2)}) %all-to-all-start.4) | async-done | bytes 1568 | tf_op jit(solution)/shard_map/all_to_all | solution.py:36
  149.5 0.1 multiply_multiply_fusion
  149.6 0.7 convert_bitcast_fusion
  150.3 0.7 fusion
  151.0 0.7 concatenate.7
  151.7 0.0 all-gather.2.cloned.1.call-update
  151.8 63.6 %all-gather.2.cloned.1.call-done = bf16[768,1538]{1,0:T(8,128)(2,1)} async-done(((bf16[24,1538]{1,0:T(8,128)(2,1)}), bf16[768,1538]{1,0:T(8,128)(2,1)}) %all-gather.2.cloned.1.call-update) | async-done | bytes 2362384 | tf_op jit(solution)/shard_map/all_gather | solution.py:56
  215.4 2.8 %slice_bitcast_fusion = (bf16[768,768]{0,1:T(8,128)(2,1)S(1)}, bf16[768,768]{1,0:T(8,128)(2,1)}) fusion(bf16[768,1538]{1,0:T(8,128)(2,1)} %all-gather.2.cloned.1.call-done), kind=kLoop, calls=%fused_computation | loop fusion | bytes 4718592 | tf_op jit(solution)/shard_map/transpose | solution.py:59
  218.2 1.4 copy.56
  219.6 1.9 slice_reduce_fusion
  (7 shorter events, 0.1 us)
Async XLA Ops:
  8.6 11.5 %all-to-all-start.5 = ((f32[2,1,384]{2,1,0:T(1,128)}), f32[2,1,384]{2,1,0:T(1,128)S(1)}, u32[]{:S(2)}, u32[]{:S(2)}) async-start(f32[2,1,384]{2,1,0:T(1,128)} %reshape.64), calls=%async_computation.5 | async-start | bytes 6144 | tf_op jit(solution)/shard_map/all_to_all | solution.py:22
  20.2 13.3 %all-to-all-start.7 = ((f32[2,1,384]{2,1,0:T(1,128)}), f32[2,1,384]{2,1,0:T(1,128)S(1)}, u32[]{:S(2)}, u32[]{:S(2)}) async-start(f32[2,1,384]{2,1,0:T(1,128)} %reshape.66), calls=%async_computation.7 | async-start | bytes 6144 | tf_op jit(solution)/shard_map/all_to_all | solution.py:22
  33.4 6.3 %copy-start = (f32[2,16,768,24]{2,3,1,0:T(8,128)S(1)}, f32[2,16,768,24]{2,3,1,0:T(8,128)}, u32[]{:S(2)}) copy-start(f32[2,16,768,24]{2,3,1,0:T(8,128)} %copy.49) | copy-start | bytes 7077892
  45.4 10.2 %all-to-all-start.6 = ((f32[16,1,24]{2,1,0:T(1,128)}), f32[16,1,24]{2,1,0:T(1,128)S(1)}, u32[]{:S(2)}, u32[]{:S(2)}) async-start(f32[16,1,24]{2,1,0:T(1,128)} %bitcast.9), calls=%async_computation.6 | async-start | bytes 16384 | tf_op jit(solution)/shard_map/all_to_all | solution.py:30
  55.5 10.2 %all-to-all-start.8 = ((f32[16,1,24]{2,1,0:T(1,128)}), f32[16,1,24]{2,1,0:T(1,128)S(1)}, u32[]{:S(2)}, u32[]{:S(2)}) async-start(f32[16,1,24]{2,1,0:T(1,128)} %bitcast.12), calls=%async_computation.8 | async-start | bytes 16384 | tf_op jit(solution)/shard_map/all_to_all | solution.py:30
  65.7 28.0 %all-to-all-start.1 = ((f32[16,24,768]{2,1,0:T(8,128)}), f32[16,24,768]{2,1,0:T(8,128)S(1)}, u32[]{:S(2)}, u32[]{:S(2)}) async-start(f32[16,24,768]{2,1,0:T(8,128)} %reduce_sum.117), calls=%async_computation.1 | async-start | bytes 2359296 | tf_op jit(solution)/shard_map/all_to_all | solution.py:30
  70.6 31.4 %copy-start.2 = (f32[24,768]{1,0:T(8,128)S(1)}, f32[24,768]{1,0:T(8,128)}, u32[]{:S(2)}) copy-start(f32[24,768]{1,0:T(8,128)} %param.12) | copy-start | bytes 221188
  70.6 31.5 %copy-start.1 = (f32[768,24]{0,1:T(8,128)S(1)}, f32[768,24]{0,1:T(8,128)}, u32[]{:S(2)}) copy-start(f32[768,24]{0,1:T(8,128)} %param.13) | copy-start | bytes 221188
  70.7 31.7 %copy-start.3 = (f32[24]{0:T(128)S(1)}, f32[24]{0:T(128)}, u32[]{:S(2)}) copy-start(f32[24]{0:T(128)} %param.14) | copy-start | bytes 292
  70.7 67.6 %copy-start.4 = (f32[24]{0:T(128)S(1)}, f32[24]{0:T(128)}, u32[]{:S(2)}) copy-start(f32[24]{0:T(128)} %param.15) | copy-start | bytes 292
  93.7 32.8 %all-to-all-start.3 = ((f32[16,768,24]{1,2,0:T(8,128)}), f32[16,768,24]{1,2,0:T(8,128)S(1)}, u32[]{:S(2)}, u32[]{:S(2)}) async-start(f32[16,768,24]{1,2,0:T(8,128)} %reduce_sum.122), calls=%async_computation.3 | async-start | bytes 2359296 | tf_op jit(solution)/shard_map/all_to_all | solution.py:30
  127.3 22.2 %all-to-all-start.4 = ((f32[4,1,96]{2,1,0:T(1,128)}), f32[4,1,96]{2,1,0:T(1,128)S(1)}, u32[]{:S(2)}, u32[]{:S(2)}) async-start(f32[4,1,96]{2,1,0:T(1,128)} %broadcast_in_dim.2), calls=%async_computation.4 | async-start | bytes 4096 | tf_op jit(solution)/shard_map/all_to_all | solution.py:36
  138.2 77.2 %all-gather.2.cloned.1.call-start = ((), (), s32[]{:S(2)}) async-start(), calls=%async_computation.9 | async-start | bytes 2635776 | tf_op jit(solution)/shard_map/all_gather | solution.py:56
Sparse Core Ops, SparseCore 0:
  151.9 63.4 all-gather.1
where the time goes:
time: 229 us; the launch traced here: 228 us
  waiting for transfers between devices  130 us (57%)
  starting transfers between devices  43.3 us (19%)
  local copies, waits for them, and re-layouts  18 us (8%)
  between operations  14.2 us (6%)
  blocking collectives  11.9 us (5%)
  other arithmetic  11.5 us (5%)
    all_gather x1, waiting for transfers between devices, gather_turned(): whole, at, outs = (lax.all_gather(both, axis, axis=0, tiled=True), 0, [])  63.6 us
    all_to_all x4, waiting for transfers between devices, sum_by_axis(): lax.all_to_all(nearer, far, split_axis=0, concat_axis=0, tiled=True)  55.4 us
    all_to_all x4, starting transfers between devices, sum_by_axis(): lax.all_to_all(nearer, far, split_axis=0, concat_axis=0, tiled=True)  19 us
    all_to_all x2, starting transfers between devices, sum_at_owner(): tiles = lax.all_to_all(split_up(shard, dim, count), axis, 0, 0, tiled=True)  13.3 us
    all_to_all x2, blocking collectives, sum_at_owner(): tiles = lax.all_to_all(split_up(shard, dim, count), axis, 0, 0, tiled=True)  11.9 us
    all_to_all x1, starting transfers between devices, from_everyone(): lax.all_to_all(jnp.broadcast_to(shard[None], (count, *shard.shape)), axis...  10.9 us
    all_to_all x1, waiting for transfers between devices, from_everyone(): lax.all_to_all(jnp.broadcast_to(shard[None], (count, *shard.shape)), axis...  10.6 us
    unnamed x16, local copies, waits for them, and re-layouts  6 us
  transfers between devices with their start and end apart: 8, of which 6 were waited for; matrix products, arithmetic and copies ran while one was open for 8% of the time, Pallas kernels for 0%

commit v1 on v0

v1 whole, which is shorter than its diff:
```python
import jax
import jax.numpy as jnp
from jax import lax
from jax.sharding import Mesh
from jax.sharding import PartitionSpec as P

REPLICA = ("y", "x", "core")
ENS_REPLICA = ("ens", "y", "x", "core")
PLANE = ("y", "x")
MODEL = ("mz", "my")
SWAP = [(0, 1), (1, 0)]

learn_rate = 0.4
f32 = jnp.float32
SPAN = 173.25


def core_sum(grad):
    core = lax.axis_index("core")
    tiles = grad.reshape(16, 2, 24, 768)
    mine = lax.dynamic_index_in_dim(tiles, core, 1, keepdims=False)
    other = lax.dynamic_index_in_dim(tiles, 1 - core, 1, keepdims=False)
    return mine + lax.ppermute(other, "core", SWAP)


def encode(part):
    top = jnp.max(jnp.abs(part), axis=2, keepdims=True)
    top = lax.reduce_precision(jnp.maximum(top, 1e-30) * (1 + 2.0**-7), 8, 7)
    code = jnp.exp(jnp.abs(part) * (SPAN / top) - SPAN / 2)
    code = jnp.where(part < 0, -code, code)
    return jnp.concatenate([code, jnp.broadcast_to(top, (16, 24, 128))], axis=2).astype(jnp.bfloat16)


def decode(message):
    code = message[:, :, :768].astype(f32)
    top = message[:, :, 768:769].astype(f32)
    size = (jnp.log(jnp.abs(code)) + SPAN / 2) * (top * (1 / SPAN))
    return jnp.where(code < 0, -size, size)


def plane_sum(part):
    return jnp.sum(decode(lax.all_to_all(encode(part), PLANE, 0, 0, tiled=True)), axis=0) * 32**-0.5


def model_sum(a):
    a = a + lax.ppermute(a, "mz", SWAP)
    return a + lax.ppermute(a, "my", SWAP)


def step(param, mean):
    sizes = jnp.stack([jnp.sum(param * param, axis=1), jnp.sum(mean * mean, axis=1)])
    sizes = model_sum(sizes)
    ratio = jnp.sqrt(sizes[0]) * lax.rsqrt(sizes[1] + 1e-06)
    return param - learn_rate * (mean * ratio[:, None])


def gather(rows):
    core = lax.axis_index("core")
    plane = lax.all_to_all(jnp.broadcast_to(rows[None], (16, 24, 768)), PLANE, 0, 0, tiled=True)
    got = lax.ppermute(plane, "core", SWAP)
    return jnp.stack([jnp.where(core == 0, plane, got), jnp.where(core == 0, got, plane)], axis=1)


def small_sums(slope_norm, slope_bias, param_norm, param_bias):
    own = jnp.concatenate([slope_norm.reshape(6, 128), slope_bias.reshape(6, 128),
                           jnp.concatenate([param_norm, param_bias, jnp.zeros(80, f32)]).reshape(1, 128)])
    every = lax.all_to_all(jnp.broadcast_to(own[None], (32, 13, 128)), REPLICA, 0, 0, tiled=True)
    sums = jnp.sum(every[:, :12], axis=0) * 32**-0.5
    params = every[:, 12]
    norm = params[:, :24].reshape(768) - learn_rate * sums[:6].reshape(768)
    bias = params[:, 24:48].reshape(768) - learn_rate * sums[6:].reshape(768)
    return norm, bias


def on_device(
    slope_up, slope_down, slope_norm, slope_bias, param_up, param_down, param_norm, param_bias
):
    norm, bias = small_sums(slope_norm[0], slope_bias[0], param_norm, param_bias)
    up = core_sum(slope_up[0])
    down = core_sum(slope_down[0].T)
    mean_up = plane_sum(up)
    mean_down = plane_sum(down)
    next_up = step(param_up, mean_up)
    half_up = gather(next_up.astype(jnp.bfloat16)).reshape(768, 768)
    turned = step(param_down.T, mean_down)
    half_down = gather(turned.astype(jnp.bfloat16)).reshape(768, 768).T
    r = lax.axis_index(REPLICA)
    next_norm = lax.dynamic_slice_in_dim(norm, 24 * r, 24)
    next_bias = lax.dynamic_slice_in_dim(bias, 24 * r, 24)
    bf = jnp.bfloat16
    return half_up, half_down, norm.astype(bf), bias.astype(bf), next_up, turned.T, next_norm, next_bias


def solution(mesh):
    split = Mesh(
        mesh.devices.reshape(mesh.shape["ens"], 4, 4, 2, 2, 2),
        ("ens", "y", "x", "core", "mz", "my"),
    )
    return jax.shard_map(
        on_device,
        mesh=split,
        in_specs=(
            P(ENS_REPLICA, None, MODEL),
            P(ENS_REPLICA, MODEL, None),
            P(ENS_REPLICA, None),
            P(ENS_REPLICA, None),
            P(ENS_REPLICA, MODEL),
            P(("ens", *MODEL), REPLICA),
            P(ENS_REPLICA),
            P(ENS_REPLICA),
        ),
        out_specs=(
            P("ens", MODEL),
            P(("ens", *MODEL), None),
            P("ens"),
            P("ens"),
            P(ENS_REPLICA, MODEL),
            P(("ens", *MODEL), REPLICA),
            P(ENS_REPLICA),
            P(ENS_REPLICA),
        ),
        check_vma=False,
    )
```

time: 229 us -> 139 us (0.61)
  waiting for transfers between devices: 130 us -> 35.9 us
  starting transfers between devices: 43.3 us -> 77.7 us
  between operations: 14.2 us -> 1.1 us
  blocking collectives: 11.9 us -> 0 us
  local copies, waits for them, and re-layouts: 18 us -> 9.89 us
    all_gather x1 -> x0, waiting for transfers between devices: 63.6 us -> none  [gather_turned(): whole, at, outs = (lax.all_gather(both, axis, axis=0, tiled=True), 0, [])]
    ppermute x0 -> x8, starting transfers between devices: none -> 48.3 us  [the longest x2 16.5 us: model_sum(): a = a + lax.ppermute(a, 'mz', SWAP)]
    all_to_all x7 -> x5, waiting for transfers between devices: 65.9 us -> 25.1 us  [the longest x2 19.5 us: plane_sum(): lax.all_to_all(encode(part), PLANE, 0, 0, tiled=True)]
    all_to_all x7 -> x5, starting transfers between devices: 43.3 us -> 29.4 us  [the longest x2 11.1 us: gather(): lax.all_to_all(jnp.broadcast_to(rows[None], (16, 24, 768)), PLANE, 0, 0,...]
    all_to_all x2 -> x0, blocking collectives: 11.9 us -> none  [sum_at_owner(): tiles = lax.all_to_all(split_up(shard, dim, count), axis, 0, 0, tiled=True)]
    ppermute x0 -> x8, waiting for transfers between devices: none -> 10.7 us  [the longest x2 9.46 us: model_sum(): return a + lax.ppermute(a, 'my', SWAP)]
    transpose x5 -> x0, local copies, waits for them, and re-layouts: 7.91 us -> none  [the longest x4 5.11 us: split_up(): return jnp.moveaxis(tiles, dim, 0)]
    reduce_sum x13 -> x7, other arithmetic: 6.14 us -> 2.4 us  [the longest x2 1.89 us: plane_sum(): jnp.sum(decode(lax.all_to_all(encode(part), PLANE, 0, 0, tiled=True)), ax...]
  transfers between devices with their start and end apart: 8 -> 13, of which waited for: 6 -> 7; matrix products, arithmetic and copies ran while one was open for 8% -> 12% of each run, Pallas kernels for 0% -> 0%
where the time goes in v1:
time: 139 us; the launch traced here: 138 us
  starting transfers between devices  77.7 us (56%)
  waiting for transfers between devices  35.9 us (26%)
  other arithmetic  13 us (9%)
  local copies, waits for them, and re-layouts  9.89 us (7%)
    all_to_all x2, waiting for transfers between devices, plane_sum(): lax.all_to_all(encode(part), PLANE, 0, 0, tiled=True)  19.5 us
    ppermute x2, starting transfers between devices, model_sum(): a = a + lax.ppermute(a, 'mz', SWAP)  16.5 us
    ppermute x2, starting transfers between devices, gather(): got = lax.ppermute(plane, 'core', SWAP)  14.2 us
    all_to_all x2, starting transfers between devices, gather(): lax.all_to_all(jnp.broadcast_to(rows[None], (16, 24, 768)), PLANE, 0, 0,...  11.1 us
    ppermute x2, starting transfers between devices, core_sum(): return mine + lax.ppermute(other, 'core', SWAP)  10.8 us
    all_to_all x2, starting transfers between devices, plane_sum(): lax.all_to_all(encode(part), PLANE, 0, 0, tiled=True)  9.69 us
    ppermute x2, waiting for transfers between devices, model_sum(): return a + lax.ppermute(a, 'my', SWAP)  9.46 us
    all_to_all x1, starting transfers between devices, small_sums(): lax.all_to_all(jnp.broadcast_to(own[None], (32, 13, 128)), REPLICA, 0, 0,...  8.65 us
  transfers between devices with their start and end apart: 13, of which 7 were waited for; matrix products, arithmetic and copies ran while one was open for 12% of the time, Pallas kernels for 0%

profile of v1, /device:TPU:1, one launch (start us, length us, event | category | flops | bytes accessed | tf_op | source)
XLA Modules:
  0.0 137.6 jit_solution(12352596702403181111)
XLA Ops:
  0.6 2.0 %copy.28 = f32[1,768,768]{1,2,0:T(8,128)S(1)} copy(f32[1,768,768]{2,1,0:T(8,128)} %param.9) | data formatting | bytes 4718592 | tf_op args[1]
  2.7 0.0 copy-start
  2.7 1.1 dynamic-slice_bitcast_fusion
  3.8 8.9 %collective-permute-start.4 = (f32[16,24,768]{2,1,0:T(8,128)}, f32[16,24,768]{2,1,0:T(8,128)}, u32[]{:S(2)}, u32[]{:S(2)}) collective-permute-start(f32[16,24,768]{2,1,0:T(8,128)} %dynamic-slice_bitcast_fusion), channel_id=1, source_target_pairs={{0,4},{4,0},{1,5},{5,1},{2,6},{6,2},{3,7},{7,3},{8,12},{12,8},{9,1... | collective-permute-start | bytes 3538952 | tf_op jit(solution)/shard_map/ppermute | solution.py:23
  12.7 1.1 dynamic-slice_bitcast_fusion.1
  13.8 1.9 %collective-permute-start = (f32[16,24,768]{2,1,0:T(8,128)}, f32[16,24,768]{2,1,0:T(8,128)S(1)}, u32[]{:S(2)}, u32[]{:S(2)}) collective-permute-start(f32[16,24,768]{2,1,0:T(8,128)} %dynamic-slice_bitcast_fusion.1), channel_id=1, source_target_pairs={{0,4},{4,0},{1,5},{5,1},{2,6},{6,2},{3,7},{7,3},{8,12},{12,8},{9,1... | collective-permute-start | bytes 3538952 | tf_op jit(solution)/shard_map/ppermute | solution.py:23
  15.7 1.5 %abs_reduce_fusion = f32[16,24]{1,0:T(8,128)S(1)} fusion(f32[16,24,768]{2,1,0:T(8,128)} %collective-permute-done.4, f32[16,2,24,768]{3,2,1,0:T(8,128)S(1)} %bitcast.69, s32[]{:T(128)S(6)} %select_n.47), kind=kLoop, calls=%fused_computation.24 | loop fusion | flops 884352 | bytes 2360836 | tf_op jit(solution)/shard_map/reduce_max | solution.py:27
  17.3 1.7 %fusion.8 = bf16[16,24,768]{2,1,0:T(8,128)(2,1)S(1)} fusion(f32[16,24]{1,0:T(8,128)S(1)} %get-tuple-element.46, f32[16,24,768]{2,1,0:T(8,128)} %collective-permute-done.4, f32[16,2,24,768]{3,2,1,0:T(8,128)S(1)} %bitcast.70, s32[]{:T(128)S(6)} %select_n.47), kind=kLoop, calls=%fused_computation.16 | loop fusion | flops 2359296 | bytes 2950660 | tf_op jit(solution)/shard_map/convert
  19.0 0.1 broadcast_in_dim.14
  19.1 0.0 copy-start.1
  19.1 0.9 pad_maximum_fusion.3
  20.0 4.4 %all-to-all-start.2 = ((bf16[16,24,896]{2,1,0:T(8,128)(2,1)}), bf16[16,24,896]{2,1,0:T(8,128)(2,1)}, u32[]{:S(2)}, u32[]{:S(2)}) async-start(bf16[16,24,896]{2,1,0:T(8,128)(2,1)} %pad_maximum_fusion.3), calls=%async_computation.2 | async-start | bytes 1376256 | tf_op jit(solution)/shard_map/all_to_all | solution.py:42
  24.5 0.3 abs_reduce_fusion.1
  24.7 0.5 fusion.6
  25.2 0.1 broadcast_in_dim.12
  25.3 0.0 copy-start.4
  25.3 0.0 copy-start.6
  25.4 0.0 copy-start.7
  25.4 0.0 copy-start.3
  25.4 0.9 pad_maximum_fusion.2
  26.3 15.2 %all-to-all-done.2 = bf16[16,24,896]{2,1,0:T(8,128)(2,1)} async-done(((bf16[16,24,896]{2,1,0:T(8,128)(2,1)}), bf16[16,24,896]{2,1,0:T(8,128)(2,1)}, u32[]{:S(2)}, u32[]{:S(2)}) %all-to-all-start.2) | async-done | bytes 688160 | tf_op jit(solution)/shard_map/all_to_all | solution.py:42
  41.5 5.3 %all-to-all-start = ((bf16[16,24,896]{2,1,0:T(8,128)(2,1)}), bf16[16,24,896]{2,1,0:T(8,128)(2,1)S(1)}, u32[]{:S(2)}, u32[]{:S(2)}) async-start(bf16[16,24,896]{2,1,0:T(8,128)(2,1)} %pad_maximum_fusion.2), calls=%async_computation | async-start | bytes 1376256 | tf_op jit(solution)/shard_map/all_to_all | solution.py:42
  46.8 0.1 maximum_bitcast_fusion
  46.9 0.1 fusion.10
  47.1 0.1 multiply_reduce_fusion.4
  47.2 1.0 multiply_reduce_fusion
  48.2 1.5 %fusion.9 = f32[24,768]{1,0:T(8,128)S(1)} fusion(bf16[16,24,896]{2,1,0:T(8,128)(2,1)} %all-to-all-done.2, f32[16,24]{1,0:T(8,128)S(1)} %multiply_reduce_fusion), kind=kLoop, calls=%fused_computation.17 | loop fusion | flops 2340864 | bytes 665088 | tf_op jit(solution)/shard_map/reduce_sum | solution.py:42
  49.7 0.1 multiply_reduce_fusion.2
  49.8 8.2 %collective-permute-start.5 = (f32[2,24]{1,0:T(2,128)S(1)}, f32[2,24]{1,0:T(2,128)S(1)}, u32[]{:S(2)}, u32[]{:S(2)}) collective-permute-start(f32[2,24]{1,0:T(2,128)S(1)} %pad_maximum_fusion.6), channel_id=1, source_target_pairs={{0,2},{2,0},{1,3},{3,1},{4,6},{6,4},{5,7},{7,5},{8,10},{10,8},{9,1... | collective-permute-start | bytes 584 | tf_op jit(solution)/shard_map/ppermute | solution.py:46
  58.1 4.3 %all-to-all-done = bf16[16,24,896]{2,1,0:T(8,128)(2,1)S(1)} async-done(((bf16[16,24,896]{2,1,0:T(8,128)(2,1)}), bf16[16,24,896]{2,1,0:T(8,128)(2,1)S(1)}, u32[]{:S(2)}, u32[]{:S(2)}) %all-to-all-start) | async-done | bytes 688160 | tf_op jit(solution)/shard_map/all_to_all | solution.py:42
  62.4 0.7 broadcast_in_dim.17
  63.1 8.6 %all-to-all-start.4 = ((f32[32,13,128]{2,1,0:T(8,128)}), f32[32,13,128]{2,1,0:T(8,128)S(1)}, u32[]{:S(2)}, u32[]{:S(2)}) async-start(f32[32,13,128]{2,1,0:T(8,128)} %broadcast_in_dim.17), calls=%async_computation.4 | async-start | bytes 524288 | tf_op jit(solution)/shard_map/all_to_all | solution.py:67
  71.8 0.1 multiply_reduce_fusion.1
  71.9 2.4 %collective-permute-start.6 = (f32[2,24]{1,0:T(2,128)S(1)}, f32[2,24]{1,0:T(2,128)S(1)}, u32[]{:S(2)}, u32[]{:S(2)}) collective-permute-start(f32[2,24]{1,0:T(2,128)S(1)} %fusion.20), channel_id=1, source_target_pairs={{0,1},{1,0},{2,3},{3,2},{4,5},{5,4},{6,7},{7,6},{8,9},{9,8},{10,11... | collective-permute-start | bytes 584 | tf_op jit(solution)/shard_map/ppermute | solution.py:47
  74.3 0.4 fusion.7
  74.8 5.7 %collective-permute-done.6 = f32[2,24]{1,0:T(2,128)S(1)} collective-permute-done((f32[2,24]{1,0:T(2,128)S(1)}, f32[2,24]{1,0:T(2,128)S(1)}, u32[]{:S(2)}, u32[]{:S(2)}) %collective-permute-start.6) | collective-permute-done | bytes 224 | tf_op jit(solution)/shard_map/ppermute | solution.py:47
  80.5 0.1 fusion.11
  80.6 2.3 %all-to-all-done.4 = f32[32,13,128]{2,1,0:T(8,128)S(1)} async-done(((f32[32,13,128]{2,1,0:T(8,128)}), f32[32,13,128]{2,1,0:T(8,128)S(1)}, u32[]{:S(2)}, u32[]{:S(2)}) %all-to-all-start.4) | async-done | bytes 213024 | tf_op jit(solution)/shard_map/all_to_all | solution.py:67
  82.9 0.9 broadcast_in_dim.15
  83.7 4.4 %all-to-all-start.3 = ((bf16[16,24,768]{2,1,0:T(8,128)(2,1)}), bf16[16,24,768]{2,1,0:T(8,128)(2,1)S(1)}, u32[]{:S(2)}, u32[]{:S(2)}) async-start(bf16[16,24,768]{2,1,0:T(8,128)(2,1)} %broadcast_in_dim.15), calls=%async_computation.3 | async-start | bytes 1179648 | tf_op jit(solution)/shard_map/all_to_all | solution.py:59
  88.2 0.1 multiply_reduce_fusion.3
  88.3 8.3 %collective-permute-start.1 = (f32[2,24]{1,0:T(2,128)S(1)}, f32[2,24]{1,0:T(2,128)S(1)}, u32[]{:S(2)}, u32[]{:S(2)}) collective-permute-start(f32[2,24]{1,0:T(2,128)S(1)} %pad_maximum_fusion.5), channel_id=1, source_target_pairs={{0,2},{2,0},{1,3},{3,1},{4,6},{6,4},{5,7},{7,5},{8,10},{10,8},{9,1... | collective-permute-start | bytes 584 | tf_op jit(solution)/shard_map/ppermute | solution.py:46
  96.6 1.2 collective-permute-done.1
  97.8 4.5 %collective-permute-start.2 = (f32[2,24]{1,0:T(2,128)S(1)}, f32[2,24]{1,0:T(2,128)S(1)}, u32[]{:S(2)}, u32[]{:S(2)}) collective-permute-start(f32[2,24]{1,0:T(2,128)S(1)} %fusion.21), channel_id=1, source_target_pairs={{0,1},{1,0},{2,3},{3,2},{4,5},{5,4},{6,7},{7,6},{8,9},{9,8},{10,11... | collective-permute-start | bytes 584 | tf_op jit(solution)/shard_map/ppermute | solution.py:47
  102.3 3.8 %collective-permute-done.2 = f32[2,24]{1,0:T(2,128)S(1)} collective-permute-done((f32[2,24]{1,0:T(2,128)S(1)}, f32[2,24]{1,0:T(2,128)S(1)}, u32[]{:S(2)}, u32[]{:S(2)}) %collective-permute-start.2) | collective-permute-done | bytes 224 | tf_op jit(solution)/shard_map/ppermute | solution.py:47
  106.1 0.7 fusion.26
  106.8 0.9 broadcast_in_dim.13
  107.7 6.7 %all-to-all-start.1 = ((bf16[16,24,768]{2,1,0:T(8,128)(2,1)}), bf16[16,24,768]{2,1,0:T(8,128)(2,1)S(1)}, u32[]{:S(2)}, u32[]{:S(2)}) async-start(bf16[16,24,768]{2,1,0:T(8,128)(2,1)} %broadcast_in_dim.13), calls=%async_computation.1 | async-start | bytes 1179648 | tf_op jit(solution)/shard_map/all_to_all | solution.py:59
  114.4 0.1 fusion.27
  114.4 0.1 reshape.109
  114.5 0.1 reshape.110
  114.7 6.3 %collective-permute-start.7 = (bf16[16,24,768]{2,1,0:T(8,128)(2,1)S(1)}, bf16[16,24,768]{2,1,0:T(8,128)(2,1)S(1)}, u32[]{:S(2)}, u32[]{:S(2)}) collective-permute-start(bf16[16,24,768]{2,1,0:T(8,128)(2,1)S(1)} %all-to-all-done.3), channel_id=1, source_target_pairs={{0,4},{4,0},{1,5},{5,1},{2,6},{6,2},{3,7},{7,3},{8,12},{12,8},{9,1... | collective-permute-start | bytes 1769480 | tf_op jit(solution)/shard_map/ppermute | solution.py:60
  121.0 0.6 fusion.22
  121.6 0.6 dynamic_slice.23
  122.1 0.6 dynamic_slice.24
  122.7 3.3 %all-to-all-done.1 = bf16[16,24,768]{2,1,0:T(8,128)(2,1)S(1)} async-done(((bf16[16,24,768]{2,1,0:T(8,128)(2,1)}), bf16[16,24,768]{2,1,0:T(8,128)(2,1)S(1)}, u32[]{:S(2)}, u32[]{:S(2)}) %all-to-all-start.1) | async-done | bytes 589856 | tf_op jit(solution)/shard_map/all_to_all | solution.py:59
  126.1 7.9 %collective-permute-start.3 = (bf16[16,24,768]{2,1,0:T(8,128)(2,1)S(1)}, bf16[16,24,768]{2,1,0:T(8,128)(2,1)S(1)}, u32[]{:S(2)}, u32[]{:S(2)}) collective-permute-start(bf16[16,24,768]{2,1,0:T(8,128)(2,1)S(1)} %all-to-all-done.1), channel_id=1, source_target_pairs={{0,4},{4,0},{1,5},{5,1},{2,6},{6,2},{3,7},{7,3},{8,12},{12,8},{9,1... | collective-permute-start | bytes 1769480 | tf_op jit(solution)/shard_map/ppermute | solution.py:60
  133.9 0.7 bitcast_subtract_fusion
  134.7 0.1 select_bitcast_fusion.1
  134.7 0.1 pad_maximum_fusion.1
  134.9 0.1 copy.29
  134.9 1.5 %copy.30 = bf16[768,768]{1,0:T(8,128)(2,1)} copy(bf16[768,768]{0,1:T(8,128)(2,1)S(1)} %bitcast.74) | data formatting | bytes 2359296
  136.4 0.1 select_bitcast_fusion.3
  136.5 1.1 pad_maximum_fusion
  (33 shorter events, 0.2 us)
Async XLA Ops:
  2.7 10.0 %copy-start = (f32[1,768,768]{2,1,0:T(8,128)S(1)}, f32[1,768,768]{2,1,0:T(8,128)}, u32[]{:S(2)}) copy-start(f32[1,768,768]{2,1,0:T(8,128)} %param.8) | copy-start | bytes 7077892
  3.8 11.9 %collective-permute-start.4 = (f32[16,24,768]{2,1,0:T(8,128)}, f32[16,24,768]{2,1,0:T(8,128)}, u32[]{:S(2)}, u32[]{:S(2)}) collective-permute-start(f32[16,24,768]{2,1,0:T(8,128)} %dynamic-slice_bitcast_fusion), channel_id=1, source_target_pairs={{0,4},{4,0},{1,5},{5,1},{2,6},{6,2},{3,7},{7,3},{8,12},{12,8},{9,1... | collective-permute-start | bytes 3538952 | tf_op jit(solution)/shard_map/ppermute | solution.py:23
  13.8 10.7 %collective-permute-start = (f32[16,24,768]{2,1,0:T(8,128)}, f32[16,24,768]{2,1,0:T(8,128)S(1)}, u32[]{:S(2)}, u32[]{:S(2)}) collective-permute-start(f32[16,24,768]{2,1,0:T(8,128)} %dynamic-slice_bitcast_fusion.1), channel_id=1, source_target_pairs={{0,4},{4,0},{1,5},{5,1},{2,6},{6,2},{3,7},{7,3},{8,12},{12,8},{9,1... | collective-permute-start | bytes 3538952 | tf_op jit(solution)/shard_map/ppermute | solution.py:23
  19.1 5.3 %copy-start.1 = (f32[1,768,768]{2,1,0:T(8,128)S(1)}, f32[1,768,768]{2,1,0:T(8,128)}, u32[]{:S(2)}) copy-start(f32[1,768,768]{2,1,0:T(8,128)} %param.8) | copy-start | bytes 7077892
  20.0 21.4 %all-to-all-start.2 = ((bf16[16,24,896]{2,1,0:T(8,128)(2,1)}), bf16[16,24,896]{2,1,0:T(8,128)(2,1)}, u32[]{:S(2)}, u32[]{:S(2)}) async-start(bf16[16,24,896]{2,1,0:T(8,128)(2,1)} %pad_maximum_fusion.3), calls=%async_computation.2 | async-start | bytes 1376256 | tf_op jit(solution)/shard_map/all_to_all | solution.py:42
  25.3 21.4 %copy-start.4 = (f32[1,768]{1,0:T(1,128)S(1)}, f32[1,768]{1,0:T(1,128)}, u32[]{:S(2)}) copy-start(f32[1,768]{1,0:T(1,128)} %param.10) | copy-start | bytes 9220
  25.3 21.5 %copy-start.5 = (f32[1,768]{1,0:T(1,128)S(1)}, f32[1,768]{1,0:T(1,128)}, u32[]{:S(2)}) copy-start(f32[1,768]{1,0:T(1,128)} %param.11) | copy-start | bytes 9220
  25.3 21.5 %copy-start.6 = (f32[24]{0:T(128)S(1)}, f32[24]{0:T(128)}, u32[]{:S(2)}) copy-start(f32[24]{0:T(128)} %param.15) | copy-start | bytes 292
  25.4 21.5 %copy-start.7 = (f32[24]{0:T(128)S(1)}, f32[24]{0:T(128)}, u32[]{:S(2)}) copy-start(f32[24]{0:T(128)} %param.14) | copy-start | bytes 292
  25.4 21.6 %copy-start.2 = (f32[768,24]{0,1:T(8,128)S(1)}, f32[768,24]{0,1:T(8,128)}, u32[]{:S(2)}) copy-start(f32[768,24]{0,1:T(8,128)} %param.13) | copy-start | bytes 221188
  25.4 21.7 %copy-start.3 = (f32[24,768]{1,0:T(8,128)S(1)}, f32[24,768]{1,0:T(8,128)}, u32[]{:S(2)}) copy-start(f32[24,768]{1,0:T(8,128)} %param.12) | copy-start | bytes 221188
  41.5 20.9 %all-to-all-start = ((bf16[16,24,896]{2,1,0:T(8,128)(2,1)}), bf16[16,24,896]{2,1,0:T(8,128)(2,1)S(1)}, u32[]{:S(2)}, u32[]{:S(2)}) async-start(bf16[16,24,896]{2,1,0:T(8,128)(2,1)} %pad_maximum_fusion.2), calls=%async_computation | async-start | bytes 1376256 | tf_op jit(solution)/shard_map/all_to_all | solution.py:42
  49.8 22.1 %collective-permute-start.5 = (f32[2,24]{1,0:T(2,128)S(1)}, f32[2,24]{1,0:T(2,128)S(1)}, u32[]{:S(2)}, u32[]{:S(2)}) collective-permute-start(f32[2,24]{1,0:T(2,128)S(1)} %pad_maximum_fusion.6), channel_id=1, source_target_pairs={{0,2},{2,0},{1,3},{3,1},{4,6},{6,4},{5,7},{7,5},{8,10},{10,8},{9,1... | collective-permute-start | bytes 584 | tf_op jit(solution)/shard_map/ppermute | solution.py:46
  63.1 19.8 %all-to-all-start.4 = ((f32[32,13,128]{2,1,0:T(8,128)}), f32[32,13,128]{2,1,0:T(8,128)S(1)}, u32[]{:S(2)}, u32[]{:S(2)}) async-start(f32[32,13,128]{2,1,0:T(8,128)} %broadcast_in_dim.17), calls=%async_computation.4 | async-start | bytes 524288 | tf_op jit(solution)/shard_map/all_to_all | solution.py:67
  71.9 8.5 %collective-permute-start.6 = (f32[2,24]{1,0:T(2,128)S(1)}, f32[2,24]{1,0:T(2,128)S(1)}, u32[]{:S(2)}, u32[]{:S(2)}) collective-permute-start(f32[2,24]{1,0:T(2,128)S(1)} %fusion.20), channel_id=1, source_target_pairs={{0,1},{1,0},{2,3},{3,2},{4,5},{5,4},{6,7},{7,6},{8,9},{9,8},{10,11... | collective-permute-start | bytes 584 | tf_op jit(solution)/shard_map/ppermute | solution.py:47
  83.7 23.1 %all-to-all-start.3 = ((bf16[16,24,768]{2,1,0:T(8,128)(2,1)}), bf16[16,24,768]{2,1,0:T(8,128)(2,1)S(1)}, u32[]{:S(2)}, u32[]{:S(2)}) async-start(bf16[16,24,768]{2,1,0:T(8,128)(2,1)} %broadcast_in_dim.15), calls=%async_computation.3 | async-start | bytes 1179648 | tf_op jit(solution)/shard_map/all_to_all | solution.py:59
  88.3 9.5 %collective-permute-start.1 = (f32[2,24]{1,0:T(2,128)S(1)}, f32[2,24]{1,0:T(2,128)S(1)}, u32[]{:S(2)}, u32[]{:S(2)}) collective-permute-start(f32[2,24]{1,0:T(2,128)S(1)} %pad_maximum_fusion.5), channel_id=1, source_target_pairs={{0,2},{2,0},{1,3},{3,1},{4,6},{6,4},{5,7},{7,5},{8,10},{10,8},{9,1... | collective-permute-start | bytes 584 | tf_op jit(solution)/shard_map/ppermute | solution.py:46
  97.8 8.2 %collective-permute-start.2 = (f32[2,24]{1,0:T(2,128)S(1)}, f32[2,24]{1,0:T(2,128)S(1)}, u32[]{:S(2)}, u32[]{:S(2)}) collective-permute-start(f32[2,24]{1,0:T(2,128)S(1)} %fusion.21), channel_id=1, source_target_pairs={{0,1},{1,0},{2,3},{3,2},{4,5},{5,4},{6,7},{7,6},{8,9},{9,8},{10,11... | collective-permute-start | bytes 584 | tf_op jit(solution)/shard_map/ppermute | solution.py:47
  107.7 18.4 %all-to-all-start.1 = ((bf16[16,24,768]{2,1,0:T(8,128)(2,1)}), bf16[16,24,768]{2,1,0:T(8,128)(2,1)S(1)}, u32[]{:S(2)}, u32[]{:S(2)}) async-start(bf16[16,24,768]{2,1,0:T(8,128)(2,1)} %broadcast_in_dim.13), calls=%async_computation.1 | async-start | bytes 1179648 | tf_op jit(solution)/shard_map/all_to_all | solution.py:59
  114.7 20.0 %collective-permute-start.7 = (bf16[16,24,768]{2,1,0:T(8,128)(2,1)S(1)}, bf16[16,24,768]{2,1,0:T(8,128)(2,1)S(1)}, u32[]{:S(2)}, u32[]{:S(2)}) collective-permute-start(bf16[16,24,768]{2,1,0:T(8,128)(2,1)S(1)} %all-to-all-done.3), channel_id=1, source_target_pairs={{0,4},{4,0},{1,5},{5,1},{2,6},{6,2},{3,7},{7,3},{8,12},{12,8},{9,1... | collective-permute-start | bytes 1769480 | tf_op jit(solution)/shard_map/ppermute | solution.py:60
  126.1 10.3 %collective-permute-start.3 = (bf16[16,24,768]{2,1,0:T(8,128)(2,1)S(1)}, bf16[16,24,768]{2,1,0:T(8,128)(2,1)S(1)}, u32[]{:S(2)}, u32[]{:S(2)}) collective-permute-start(bf16[16,24,768]{2,1,0:T(8,128)(2,1)S(1)} %all-to-all-done.1), channel_id=1, source_target_pairs={{0,4},{4,0},{1,5},{5,1},{2,6},{6,2},{3,7},{7,3},{8,12},{12,8},{9,1... | collective-permute-start | bytes 1769480 | tf_op jit(solution)/shard_map/ppermute | solution.py:60

commit v2 on v1

v2 whole, which is shorter than its diff:
```python
import jax
import jax.numpy as jnp
from jax import lax
from jax.experimental import pallas as pl
from jax.experimental.pallas import tpu as pltpu
from jax.sharding import Mesh
from jax.sharding import PartitionSpec as P


ENS_REPLICA = ("ens", "y", "x", "core")
PLANE = ("y", "x")
MODEL = ("mz", "my")
SWAP = [(0, 1), (1, 0)]

learn_rate = 0.4
f32 = jnp.float32
bf16 = jnp.bfloat16
SPAN = 173.25
GROUP = 4
VMEM = pl.BlockSpec(memory_space=pltpu.VMEM)
PARAMS = pltpu.CompilerParams(vmem_limit_bytes=12 << 20)


def pieces(a):
    high = a.astype(bf16).astype(f32)
    rest = a - high
    middle = rest.astype(bf16).astype(f32)
    return high, middle, rest - middle


def pick_kernel(core_ref, tiles_ref, vector_ref, param_ref, out_ref):
    i = pl.program_id(0)

    @pl.when(i < 4)
    def _():
        out_ref[...] = tiles_ref[0, :, 0]

    @pl.when(i == 4)
    def _():
        out_ref[0, 0:8, :] = jnp.broadcast_to(vector_ref[...], (8, 768))
        out_ref[0, 8:16, 0:128] = jnp.broadcast_to(param_ref[...], (8, 128))


def pick(core, grad, vector, param):
    return pl.pallas_call(
        pick_kernel,
        grid_spec=pltpu.PrefetchScalarGridSpec(
            num_scalar_prefetch=1,
            grid=(5,),
            in_specs=[
                pl.BlockSpec((1, GROUP, 1, 24, 768), lambda i, c: (jnp.minimum(i, 3), 0, 1 - c[0], 0, 0)),
                pl.BlockSpec((1, 768), lambda i, c: (0, 0)),
                pl.BlockSpec((1, 128), lambda i, c: (0, 0)),
            ],
            out_specs=pl.BlockSpec((GROUP, 24, 768), lambda i, c: (i, 0, 0)),
        ),
        out_shape=jax.ShapeDtypeStruct((17, 24, 768), f32),
        compiler_params=PARAMS,
        name="pick",
    )(core, grad.reshape(4, GROUP, 2, 24, 768), vector, param)


def encode_kernel(core_ref, tiles_ref, got_ref, small_ref, vector_ref, param_ref, out_ref):
    core = core_ref[0]
    total = vector_ref[...] + small_ref[0, 0:1, :]
    wide = [jnp.concatenate([total[:, 96 * k : 96 * k + 96], jnp.zeros((1, 32), f32)], axis=1) for k in range(8)]
    mine = jnp.broadcast_to(param_ref[...], (8, 128))
    theirs = jnp.broadcast_to(small_ref[0, 8:9, 0:128], (8, 128))
    parts = pieces(jnp.concatenate(wide, axis=0))
    first = pieces(jnp.where(core == 0, mine, theirs))
    second = pieces(jnp.where(core == 0, theirs, mine))
    row = lax.broadcasted_iota(jnp.int32, (8, 128), 0)
    listed = jnp.zeros((8, 128), f32)
    for k, a in enumerate((*first, *second)):
        listed = jnp.where(row == k, a, listed)
    lane = lax.broadcasted_iota(jnp.int32, (8, 128), 1)
    beside = jnp.concatenate([jnp.where(lane >= 100, listed, parts[0]), parts[1], parts[2]], axis=0)
    lane = lax.broadcasted_iota(jnp.int32, (24, 128), 1)
    for o in range(GROUP):
        part = tiles_ref[0, o, 0] + got_ref[o]
        size = jnp.abs(part)
        top = jnp.max(size, axis=1, keepdims=True)
        top = (jnp.maximum(top, 1e-30) * (1 + 2.0**-7)).astype(bf16).astype(f32)
        code = jnp.exp(size * (SPAN / top) - SPAN / 2)
        code = jnp.where(part < 0, -code, code)
        out_ref[o, :, 0:768] = code.astype(bf16)
        out_ref[o, :, 768:896] = jnp.where(lane == 96, top, beside).astype(bf16)


def encode(core, grad, got, vector, param):
    return pl.pallas_call(
        encode_kernel,
        grid_spec=pltpu.PrefetchScalarGridSpec(
            num_scalar_prefetch=1,
            grid=(4,),
            in_specs=[
                pl.BlockSpec((1, GROUP, 1, 24, 768), lambda i, c: (i, 0, c[0], 0, 0)),
                pl.BlockSpec((GROUP, 24, 768), lambda i, c: (i, 0, 0)),
                pl.BlockSpec((1, 24, 768), lambda i, c: (16, 0, 0)),
                pl.BlockSpec((1, 768), lambda i, c: (0, 0)),
                pl.BlockSpec((1, 128), lambda i, c: (0, 0)),
            ],
            out_specs=pl.BlockSpec((GROUP, 24, 896), lambda i, c: (i, 0, 0)),
        ),
        out_shape=jax.ShapeDtypeStruct((16, 24, 896), bf16),
        compiler_params=PARAMS,
        name="encode",
    )(core, grad.reshape(4, GROUP, 2, 24, 768), got, got, vector, param)


def decode_kernel(message_ref, param_ref, mean_ref, sizes_ref, vector_ref, params_ref):
    def add(o, carry):
        total, beside = carry
        code = message_ref[o, :, 0:768].astype(f32)
        side = message_ref[o, :, 768:896].astype(f32)
        params_ref[o] = side[0:8, :]
        size = (jnp.log(jnp.abs(code)) + SPAN / 2) * (side[:, 96:97] * (1 / SPAN))
        return total + jnp.where(code < 0, -size, size), beside + side

    start = (jnp.zeros((24, 768), f32), jnp.zeros((24, 128), f32))
    total, beside = lax.fori_loop(0, 16, add, start)
    mean = total * 32**-0.5
    param = param_ref[...]
    mean_ref[...] = mean
    vector_ref[...] = beside[0:8] + beside[8:16] + beside[16:24]
    own = jnp.sum(param * param, axis=1, keepdims=True)
    size = jnp.sum(mean * mean, axis=1, keepdims=True)
    lane = lax.broadcasted_iota(jnp.int32, (24, 128), 1)
    sizes_ref[...] = jnp.where(lane < 64, own, size)


def decode(message, param):
    return pl.pallas_call(
        decode_kernel,
        out_shape=(
            jax.ShapeDtypeStruct((24, 768), f32),
            jax.ShapeDtypeStruct((24, 128), f32),
            jax.ShapeDtypeStruct((8, 128), f32),
            jax.ShapeDtypeStruct((16, 8, 128), f32),
        ),
        in_specs=[VMEM] * 2,
        out_specs=(VMEM,) * 4,
        compiler_params=PARAMS,
        name="decode",
    )(message, param)


def step_kernel(param_ref, mean_ref, near_ref, far_ref, next_ref, copies_ref):
    sizes = near_ref[...] + far_ref[...]
    ratio = jnp.sqrt(sizes[:, 0:1]) * lax.rsqrt(sizes[:, 64:65] + 1e-06)
    after = param_ref[...] - learn_rate * (mean_ref[...] * ratio)
    next_ref[...] = after
    half = after.astype(bf16)
    for o in range(16):
        copies_ref[o] = half


def step(param, mean, near, far):
    return pl.pallas_call(
        step_kernel,
        out_shape=(jax.ShapeDtypeStruct((24, 768), f32), jax.ShapeDtypeStruct((16, 24, 768), bf16)),
        in_specs=[VMEM] * 4,
        out_specs=(VMEM, VMEM),
        compiler_params=PARAMS,
        name="step",
    )(param, mean, near, far)


def merge_kernel(core_ref, plane_ref, got_ref, out_ref):
    core = core_ref[0]
    out_ref[0, :, pl.ds(core, 1)] = plane_ref[...][:, None]
    out_ref[0, :, pl.ds(1 - core, 1)] = got_ref[...][:, None]


def merge(core, plane, got):
    whole = pl.pallas_call(
        merge_kernel,
        grid_spec=pltpu.PrefetchScalarGridSpec(
            num_scalar_prefetch=1,
            grid=(4,),
            in_specs=[pl.BlockSpec((GROUP, 24, 768), lambda i, c: (i, 0, 0))] * 2,
            out_specs=pl.BlockSpec((1, GROUP, 2, 24, 768), lambda i, c: (i, 0, 0, 0, 0)),
        ),
        out_shape=jax.ShapeDtypeStruct((4, GROUP, 2, 24, 768), bf16),
        compiler_params=PARAMS,
        name="merge",
    )(core, plane, got)
    return whole.reshape(768, 768)


def vector_step(beside, params):
    total = beside[:, 0:96].reshape(768)
    first = params[:, 0:1, 100:124] + params[:, 1:2, 100:124] + params[:, 2:3, 100:124]
    second = params[:, 3:4, 100:124] + params[:, 4:5, 100:124] + params[:, 5:6, 100:124]
    param = jnp.concatenate([first, second], axis=1).reshape(768)
    return param - learn_rate * (total * 32**-0.5)


def on_device(
    slope_up, slope_down, slope_norm, slope_bias, param_up, param_down, param_norm, param_bias
):
    core = lax.axis_index("core").astype(jnp.int32)
    cores = core.reshape(1)
    padded = jnp.pad(jnp.stack([param_norm, param_bias]), ((0, 0), (100, 4)))
    streams = {
        "up": (slope_up[0], param_up, slope_norm, padded[0:1]),
        "down": (slope_down[0].T, param_down.T, slope_bias, padded[1:2]),
    }
    messages, vectors, copies, after, halves = {}, {}, {}, {}, {}
    for s, (grad, _, vector, small) in streams.items():
        got = lax.ppermute(pick(cores, grad, vector, small), "core", SWAP)
        messages[s] = encode(cores, grad, got, vector, small)
    for s, (_, param, _, _) in streams.items():
        arrived = lax.all_to_all(messages[s], PLANE, 0, 0, tiled=True)
        mean, sizes, beside, params = decode(arrived, param)
        near = sizes + lax.ppermute(sizes, "mz", SWAP)
        far = lax.ppermute(near, "my", SWAP)
        after[s], copies[s] = step(param, mean, near, far)
        vectors[s] = vector_step(beside, params)
    for s in streams:
        plane = lax.all_to_all(copies[s], PLANE, 0, 0, tiled=True)
        got = lax.ppermute(plane, "core", SWAP)
        halves[s] = merge(cores, plane, got)
    at = 24 * lax.axis_index(("y", "x", "core"))
    own_norm = lax.dynamic_slice_in_dim(vectors["up"], at, 24)
    own_bias = lax.dynamic_slice_in_dim(vectors["down"], at, 24)
    return (
        halves["up"], halves["down"].T, vectors["up"].astype(bf16), vectors["down"].astype(bf16),
        after["up"], after["down"].T, own_norm, own_bias,
    )


def solution(mesh):
    split = Mesh(
        mesh.devices.reshape(mesh.shape["ens"], 4, 4, 2, 2, 2),
        ("ens", "y", "x", "core", "mz", "my"),
    )

    return jax.shard_map(
        on_device,
        mesh=split,
        in_specs=(
            P(ENS_REPLICA, None, MODEL),
            P(ENS_REPLICA, MODEL, None),
            P(ENS_REPLICA, None),
            P(ENS_REPLICA, None),
            P(ENS_REPLICA, MODEL),
            P(("ens", *MODEL), ("y", "x", "core")),
            P(ENS_REPLICA),
            P(ENS_REPLICA),
        ),
        out_specs=(
            P("ens", MODEL),
            P(("ens", *MODEL), None),
            P("ens"),
            P("ens"),
            P(ENS_REPLICA, MODEL),
            P(("ens", *MODEL), ("y", "x", "core")),
            P(ENS_REPLICA),
            P(ENS_REPLICA),
        ),
        check_vma=False,
    )
```

time: 139 us -> 125 us (0.90)
  Pallas kernels: 0 us -> 11.9 us
  waiting for transfers between devices: 35.9 us -> 24 us
  other arithmetic: 13 us -> 1.73 us
  local copies, waits for them, and re-layouts: 9.89 us -> 6.67 us
  starting transfers between devices: 77.7 us -> 79.4 us
    all_to_all x5 -> x4, waiting for transfers between devices: 25.1 us -> 9.56 us  [the longest x2 7.89 us: on_device(): arrived = lax.all_to_all(messages[s], PLANE, 0, 0, tiled=True)]
    pallas_call x0 -> x10, Pallas kernels: none -> 11.9 us  [the longest x2 4.09 us: encode(): pl.pallas_call(encode_kernel, grid_spec=pltpu.PrefetchScalarGridSpec(num_...]
    ppermute x8, starting transfers between devices: 48.3 us -> 56.5 us  [the longest x2 19.9 us: on_device(): got = lax.ppermute(plane, 'core', SWAP)]
    all_to_all x5 -> x4, starting transfers between devices: 29.4 us -> 22.9 us  [the longest x2 13.9 us: on_device(): plane = lax.all_to_all(copies[s], PLANE, 0, 0, tiled=True)]
    ppermute x8, waiting for transfers between devices: 10.7 us -> 14.4 us  [the longest x2 7.17 us: on_device(): far = lax.ppermute(near, 'my', SWAP)]
    another operation x8 -> x1, other arithmetic: 3.59 us -> 0.75 us  [on_device(): padded = jnp.pad(jnp.stack([param_norm, param_bias]), ((0, 0), (100, 4)))]
    broadcast_in_dim x6 -> x0, local copies, waits for them, and re-layouts: 2.66 us -> none  [the longest x2 1.71 us: gather(): jnp.broadcast_to(rows[None], (16, 24, 768))]
    reduce_sum x7 -> x0, other arithmetic: 2.4 us -> none  [the longest x2 1.89 us: plane_sum(): jnp.sum(decode(lax.all_to_all(encode(part), PLANE, 0, 0, tiled=True)), ax...]
  transfers between devices with their start and end apart: 13 -> 12, of which waited for: 7 -> 8; matrix products, arithmetic and copies ran while one was open for 12% -> 3% of each run, Pallas kernels for 0% -> 6%
where the time goes in v2:
time: 125 us
  starting transfers between devices  79.4 us (64%)
  waiting for transfers between devices  24 us (19%)
  Pallas kernels  11.9 us (10%)
  local copies, waits for them, and re-layouts  6.67 us (5%)
  other arithmetic  1.73 us (1%)
    ppermute x2, starting transfers between devices, on_device(): got = lax.ppermute(plane, 'core', SWAP)  19.9 us
    ppermute x2, starting transfers between devices, on_device(): near = sizes + lax.ppermute(sizes, 'mz', SWAP)  16.1 us
    all_to_all x2, starting transfers between devices, on_device(): plane = lax.all_to_all(copies[s], PLANE, 0, 0, tiled=True)  13.9 us
    ppermute x2, starting transfers between devices, on_device(): got = lax.ppermute(pick(cores, grad, vector, small), 'core', SWAP)  11 us
    ppermute x2, starting transfers between devices, on_device(): far = lax.ppermute(near, 'my', SWAP)  9.49 us
    all_to_all x2, starting transfers between devices, on_device(): arrived = lax.all_to_all(messages[s], PLANE, 0, 0, tiled=True)  9.01 us
    all_to_all x2, waiting for transfers between devices, on_device(): arrived = lax.all_to_all(messages[s], PLANE, 0, 0, tiled=True)  7.89 us
    ppermute x2, waiting for transfers between devices, on_device(): far = lax.ppermute(near, 'my', SWAP)  7.17 us
  transfers between devices with their start and end apart: 12, of which 8 were waited for; matrix products, arithmetic and copies ran while one was open for 3% of the time, Pallas kernels for 6%

profile of v2, /device:TPU:1, one launch (start us, length us, event | category | flops | bytes accessed | tf_op | source)
XLA Modules:
  0.0 124.6 jit_solution(2206873022930152472)
XLA Ops:
  0.6 0.7 select_maximum_fusion
  1.4 0.0 copy-start.3
  1.4 2.0 %copy.16 = f32[768,768]{1,0:T(8,128)S(1)} copy(f32[768,768]{0,1:T(8,128)} %bitcast.20) | data formatting | bytes 4718592 | tf_op jit(solution)/shard_map/transpose | solution.py:207
  3.5 0.0 copy-done.3
  3.5 0.6 pick.3
  4.0 8.7 %collective-permute-start.4 = (f32[17,24,768]{2,1,0:T(8,128)S(1)}, f32[17,24,768]{2,1,0:T(8,128)S(1)}, u32[]{:S(2)}, u32[]{:S(2)}) collective-permute-start(f32[17,24,768]{2,1,0:T(8,128)S(1)} %pick.3), channel_id=1, source_target_pairs={{0,4},{4,0},{1,5},{5,1},{2,6},{6,2},{3,7},{7,3},{8,12},{12,8},{9,1... | collective-permute-start | bytes 3760136 | tf_op jit(solution)/shard_map/ppermute | solution.py:211
  12.8 2.6 %collective-permute-done.4.got_ref.small_ref = f32[17,24,768]{2,1,0:T(8,128)S(1)} collective-permute-done((f32[17,24,768]{2,1,0:T(8,128)S(1)}, f32[17,24,768]{2,1,0:T(8,128)S(1)}, u32[]{:S(2)}, u32[]{:S(2)}) %collective-permute-start.4) | collective-permute-done | bytes 1253408 | tf_op jit(solution)/shard_map/ppermute | solution.py:211
  15.3 2.0 %encode.3 = bf16[16,24,896]{2,1,0:T(8,128)(2,1)} custom-call(s32[1]{0:T(128)} %bitcast.core_ref, f32[4,4,2,24,768]{4,3,2,1,0:T(8,128)S(1)} %bitcast.14, f32[17,24,768]{2,1,0:T(8,128)S(1)} %collective-permute-done.4.got_ref.small_ref, f32[17,24,768]{2,1,0:T(8,128)S(1)} %collective-permute-done.4.got_ref.small_ref, f32[1,768]{1,0:T(1,128)S(1)} %copy-done.3, ...), custom_call_target="tpu_custom_call" | custom-call | tf_op jit(solution)/shard_map/encode/pallas_call | solution.py:91
  17.4 0.0 copy-start.4
  17.4 3.7 %all-to-all-start.2 = ((bf16[16,24,896]{2,1,0:T(8,128)(2,1)}), bf16[16,24,896]{2,1,0:T(8,128)(2,1)S(1)}, u32[]{:S(2)}, u32[]{:S(2)}) async-start(bf16[16,24,896]{2,1,0:T(8,128)(2,1)} %encode.3), calls=%async_computation.2 | async-start | bytes 1376256 | tf_op jit(solution)/shard_map/all_to_all | solution.py:214
  21.1 0.0 copy-done.4
  21.1 0.0 copy-start
  21.1 1.7 %copy-done = f32[1,768,768]{2,1,0:T(8,128)S(1)} copy-done((f32[1,768,768]{2,1,0:T(8,128)S(1)}, f32[1,768,768]{2,1,0:T(8,128)}, u32[]{:S(2)}) %copy-start) | copy-done | bytes 2359320
  22.8 0.5 pick.2
  23.3 2.3 %collective-permute-start = (f32[17,24,768]{2,1,0:T(8,128)S(1)}, f32[17,24,768]{2,1,0:T(8,128)S(1)}, u32[]{:S(2)}, u32[]{:S(2)}) collective-permute-start(f32[17,24,768]{2,1,0:T(8,128)S(1)} %pick.2), channel_id=1, source_target_pairs={{0,4},{4,0},{1,5},{5,1},{2,6},{6,2},{3,7},{7,3},{8,12},{12,8},{9,1... | collective-permute-start | bytes 3760136 | tf_op jit(solution)/shard_map/ppermute | solution.py:211
  25.6 2.6 %collective-permute-done.got_ref.small_ref = f32[17,24,768]{2,1,0:T(8,128)S(1)} collective-permute-done((f32[17,24,768]{2,1,0:T(8,128)S(1)}, f32[17,24,768]{2,1,0:T(8,128)S(1)}, u32[]{:S(2)}, u32[]{:S(2)}) %collective-permute-start) | collective-permute-done | bytes 1253408 | tf_op jit(solution)/shard_map/ppermute | solution.py:211
  28.2 2.1 %encode.2 = bf16[16,24,896]{2,1,0:T(8,128)(2,1)} custom-call(s32[1]{0:T(128)} %bitcast.core_ref, f32[4,4,2,24,768]{4,3,2,1,0:T(8,128)S(1)} %bitcast.16, f32[17,24,768]{2,1,0:T(8,128)S(1)} %collective-permute-done.got_ref.small_ref, f32[17,24,768]{2,1,0:T(8,128)S(1)} %collective-permute-done.got_ref.small_ref, f32[1,768]{1,0:T(1,128)S(1)} %copy-done.4, ...), custom_call_target="tpu_custom_call" | custom-call | tf_op jit(solution)/shard_map/encode/pallas_call | solution.py:91
  30.2 0.0 copy-start.1
  30.2 7.9 %all-to-all-done.2.message_ref = bf16[16,24,896]{2,1,0:T(8,128)(2,1)S(1)} async-done(((bf16[16,24,896]{2,1,0:T(8,128)(2,1)}), bf16[16,24,896]{2,1,0:T(8,128)(2,1)S(1)}, u32[]{:S(2)}, u32[]{:S(2)}) %all-to-all-start.2) | async-done | bytes 688160 | tf_op jit(solution)/shard_map/all_to_all | solution.py:214
  38.1 5.3 %all-to-all-start = ((bf16[16,24,896]{2,1,0:T(8,128)(2,1)}), bf16[16,24,896]{2,1,0:T(8,128)(2,1)S(1)}, u32[]{:S(2)}, u32[]{:S(2)}) async-start(bf16[16,24,896]{2,1,0:T(8,128)(2,1)} %encode.2), calls=%async_computation | async-start | bytes 1376256 | tf_op jit(solution)/shard_map/all_to_all | solution.py:214
  43.4 0.0 copy-start.2
  43.4 0.0 copy-done.1
  43.4 1.5 %decode.3 = (f32[24,768]{1,0:T(8,128)S(1)}, f32[24,128]{1,0:T(8,128)S(1)}, f32[8,128]{1,0:T(8,128)S(1)}, f32[16,8,128]{2,1,0:T(8,128)S(1)}) custom-call(bf16[16,24,896]{2,1,0:T(8,128)(2,1)S(1)} %all-to-all-done.2.message_ref, f32[24,768]{1,0:T(8,128)S(1)} %bitcast.18), custom_call_target="tpu_custom_call" | custom-call | tf_op jit(solution)/shard_map/decode/pallas_call | solution.py:133
  44.9 8.8 %collective-permute-start.5 = (f32[24,128]{1,0:T(8,128)S(1)}, f32[24,128]{1,0:T(8,128)S(1)}, u32[]{:S(2)}, u32[]{:S(2)}) collective-permute-start(f32[24,128]{1,0:T(8,128)S(1)} %get-tuple-element.24), channel_id=1, source_target_pairs={{0,2},{2,0},{1,3},{3,1},{4,6},{6,4},{5,7},{7,5},{8,10},{10,8},{9,1... | collective-permute-start | bytes 36872 | tf_op jit(solution)/shard_map/ppermute | solution.py:216
  53.7 1.1 collective-permute-done.5
  54.8 4.7 %collective-permute-start.6 = (f32[24,128]{1,0:T(8,128)S(1)}, f32[24,128]{1,0:T(8,128)S(1)}, u32[]{:S(2)}, u32[]{:S(2)}) collective-permute-start(f32[24,128]{1,0:T(8,128)S(1)} %add.43.near_ref), channel_id=1, source_target_pairs={{0,1},{1,0},{2,3},{3,2},{4,5},{5,4},{6,7},{7,6},{8,9},{9,8},{10,11... | collective-permute-start | bytes 36872 | tf_op jit(solution)/shard_map/ppermute | solution.py:217
  59.6 3.6 %collective-permute-done.6.far_ref = f32[24,128]{1,0:T(8,128)S(1)} collective-permute-done((f32[24,128]{1,0:T(8,128)S(1)}, f32[24,128]{1,0:T(8,128)S(1)}, u32[]{:S(2)}, u32[]{:S(2)}) %collective-permute-start.6) | collective-permute-done | bytes 12320 | tf_op jit(solution)/shard_map/ppermute | solution.py:217
  63.2 1.0 step.3
  64.2 0.0 all-to-all-done.message_ref
  64.2 7.0 %all-to-all-start.3 = ((bf16[16,24,768]{2,1,0:T(8,128)(2,1)}), bf16[16,24,768]{2,1,0:T(8,128)(2,1)S(1)}, u32[]{:S(2)}, u32[]{:S(2)}) async-start(bf16[16,24,768]{2,1,0:T(8,128)(2,1)} %get-tuple-element.25), calls=%async_computation.3 | async-start | bytes 1179648 | tf_op jit(solution)/shard_map/all_to_all | solution.py:221
  71.1 0.0 copy-done.2
  71.2 1.5 %decode.2 = (f32[24,768]{1,0:T(8,128)S(1)}, f32[24,128]{1,0:T(8,128)S(1)}, f32[8,128]{1,0:T(8,128)S(1)}, f32[16,8,128]{2,1,0:T(8,128)S(1)}) custom-call(bf16[16,24,896]{2,1,0:T(8,128)(2,1)S(1)} %all-to-all-done.message_ref, f32[24,768]{1,0:T(8,128)S(1)} %copy-done.2), custom_call_target="tpu_custom_call" | custom-call | tf_op jit(solution)/shard_map/decode/pallas_call | solution.py:133
  72.6 7.3 %collective-permute-start.1 = (f32[24,128]{1,0:T(8,128)S(1)}, f32[24,128]{1,0:T(8,128)S(1)}, u32[]{:S(2)}, u32[]{:S(2)}) collective-permute-start(f32[24,128]{1,0:T(8,128)S(1)} %get-tuple-element.21), channel_id=1, source_target_pairs={{0,2},{2,0},{1,3},{3,1},{4,6},{6,4},{5,7},{7,5},{8,10},{10,8},{9,1... | collective-permute-start | bytes 36872 | tf_op jit(solution)/shard_map/ppermute | solution.py:216
  79.9 1.1 collective-permute-done.1
  81.0 4.7 %collective-permute-start.2 = (f32[24,128]{1,0:T(8,128)S(1)}, f32[24,128]{1,0:T(8,128)S(1)}, u32[]{:S(2)}, u32[]{:S(2)}) collective-permute-start(f32[24,128]{1,0:T(8,128)S(1)} %add.42.near_ref), channel_id=1, source_target_pairs={{0,1},{1,0},{2,3},{3,2},{4,5},{5,4},{6,7},{7,6},{8,9},{9,8},{10,11... | collective-permute-start | bytes 36872 | tf_op jit(solution)/shard_map/ppermute | solution.py:217
  85.7 3.6 %collective-permute-done.2.far_ref = f32[24,128]{1,0:T(8,128)S(1)} collective-permute-done((f32[24,128]{1,0:T(8,128)S(1)}, f32[24,128]{1,0:T(8,128)S(1)}, u32[]{:S(2)}, u32[]{:S(2)}) %collective-permute-start.2) | collective-permute-done | bytes 12320 | tf_op jit(solution)/shard_map/ppermute | solution.py:217
  89.3 1.0 step.2
  90.3 0.0 all-to-all-done.3.plane_ref
  90.3 7.0 %all-to-all-start.1 = ((bf16[16,24,768]{2,1,0:T(8,128)(2,1)}), bf16[16,24,768]{2,1,0:T(8,128)(2,1)S(1)}, u32[]{:S(2)}, u32[]{:S(2)}) async-start(bf16[16,24,768]{2,1,0:T(8,128)(2,1)} %get-tuple-element.22), calls=%async_computation.1 | async-start | bytes 1179648 | tf_op jit(solution)/shard_map/all_to_all | solution.py:221
  97.3 0.2 slice_add_fusion.1
  97.5 0.1 reshape.46
  97.6 0.2 slice_add_fusion.3
  97.8 0.1 reshape.45
  97.9 9.4 %collective-permute-start.7 = (bf16[16,24,768]{2,1,0:T(8,128)(2,1)S(1)}, bf16[16,24,768]{2,1,0:T(8,128)(2,1)S(1)}, u32[]{:S(2)}, u32[]{:S(2)}) collective-permute-start(bf16[16,24,768]{2,1,0:T(8,128)(2,1)S(1)} %all-to-all-done.3.plane_ref), channel_id=1, source_target_pairs={{0,4},{4,0},{1,5},{5,1},{2,6},{6,2},{3,7},{7,3},{8,12},{12,8},{9,1... | collective-permute-start | bytes 1769480 | tf_op jit(solution)/shard_map/ppermute | solution.py:222
  107.3 1.7 %all-to-all-done.1.plane_ref = bf16[16,24,768]{2,1,0:T(8,128)(2,1)S(1)} async-done(((bf16[16,24,768]{2,1,0:T(8,128)(2,1)}), bf16[16,24,768]{2,1,0:T(8,128)(2,1)S(1)}, u32[]{:S(2)}, u32[]{:S(2)}) %all-to-all-start.1) | async-done | bytes 589856 | tf_op jit(solution)/shard_map/all_to_all | solution.py:221
  109.0 10.5 %collective-permute-start.3 = (bf16[16,24,768]{2,1,0:T(8,128)(2,1)S(1)}, bf16[16,24,768]{2,1,0:T(8,128)(2,1)S(1)}, u32[]{:S(2)}, u32[]{:S(2)}) collective-permute-start(bf16[16,24,768]{2,1,0:T(8,128)(2,1)S(1)} %all-to-all-done.1.plane_ref), channel_id=1, source_target_pairs={{0,4},{4,0},{1,5},{5,1},{2,6},{6,2},{3,7},{7,3},{8,12},{12,8},{9,1... | collective-permute-start | bytes 1769480 | tf_op jit(solution)/shard_map/ppermute | solution.py:222
  119.5 0.1 mul.26
  119.6 0.1 mul.24
  119.6 0.6 fusion
  120.2 0.6 dynamic_slice.7
  120.8 0.6 dynamic_slice.6
  121.4 0.0 collective-permute-done.7.got_ref
  121.4 0.1 merge.3
  121.5 1.5 %copy.17 = bf16[768,768]{0,1:T(8,128)(2,1)} copy(bf16[768,768]{1,0:T(8,128)(2,1)S(1)} %bitcast.17) | data formatting | bytes 2359296 | tf_op jit(solution)/shard_map/reshape | solution.py:188
  123.0 0.0 collective-permute-done.3.got_ref
  123.0 1.6 %merge.2 = bf16[4,4,2,24,768]{4,3,2,1,0:T(8,128)(2,1)} custom-call(s32[1]{0:T(128)} %bitcast.core_ref, bf16[16,24,768]{2,1,0:T(8,128)(2,1)S(1)} %all-to-all-done.1.plane_ref, bf16[16,24,768]{2,1,0:T(8,128)(2,1)S(1)} %collective-permute-done.3.got_ref), custom_call_target="tpu_custom_call" | custom-call | tf_op jit(solution)/shard_map/merge/pallas_call | solution.py:176
  (7 shorter events, 0.1 us)
Async XLA Ops:
  1.4 2.1 %copy-start.3 = (f32[1,768]{1,0:T(1,128)S(1)}, f32[1,768]{1,0:T(1,128)}, u32[]{:S(2)}) copy-start(f32[1,768]{1,0:T(1,128)} %vector_ref.7) | copy-start | bytes 9220
  4.0 11.3 %collective-permute-start.4 = (f32[17,24,768]{2,1,0:T(8,128)S(1)}, f32[17,24,768]{2,1,0:T(8,128)S(1)}, u32[]{:S(2)}, u32[]{:S(2)}) collective-permute-start(f32[17,24,768]{2,1,0:T(8,128)S(1)} %pick.3), channel_id=1, source_target_pairs={{0,4},{4,0},{1,5},{5,1},{2,6},{6,2},{3,7},{7,3},{8,12},{12,8},{9,1... | collective-permute-start | bytes 3760136 | tf_op jit(solution)/shard_map/ppermute | solution.py:211
  17.4 3.7 %copy-start.4 = (f32[1,768]{1,0:T(1,128)S(1)}, f32[1,768]{1,0:T(1,128)}, u32[]{:S(2)}) copy-start(f32[1,768]{1,0:T(1,128)} %vector_ref.5) | copy-start | bytes 9220
  17.4 20.7 %all-to-all-start.2 = ((bf16[16,24,896]{2,1,0:T(8,128)(2,1)}), bf16[16,24,896]{2,1,0:T(8,128)(2,1)S(1)}, u32[]{:S(2)}, u32[]{:S(2)}) async-start(bf16[16,24,896]{2,1,0:T(8,128)(2,1)} %encode.3), calls=%async_computation.2 | async-start | bytes 1376256 | tf_op jit(solution)/shard_map/all_to_all | solution.py:214
  21.1 1.7 %copy-start = (f32[1,768,768]{2,1,0:T(8,128)S(1)}, f32[1,768,768]{2,1,0:T(8,128)}, u32[]{:S(2)}) copy-start(f32[1,768,768]{2,1,0:T(8,128)} %param.8) | copy-start | bytes 7077892
  23.3 4.8 %collective-permute-start = (f32[17,24,768]{2,1,0:T(8,128)S(1)}, f32[17,24,768]{2,1,0:T(8,128)S(1)}, u32[]{:S(2)}, u32[]{:S(2)}) collective-permute-start(f32[17,24,768]{2,1,0:T(8,128)S(1)} %pick.2), channel_id=1, source_target_pairs={{0,4},{4,0},{1,5},{5,1},{2,6},{6,2},{3,7},{7,3},{8,12},{12,8},{9,1... | collective-permute-start | bytes 3760136 | tf_op jit(solution)/shard_map/ppermute | solution.py:211
  30.2 13.2 %copy-start.1 = (f32[768,24]{0,1:T(8,128)S(1)}, f32[768,24]{0,1:T(8,128)}, u32[]{:S(2)}) copy-start(f32[768,24]{0,1:T(8,128)} %param.13) | copy-start | bytes 221188
  38.1 26.1 %all-to-all-start = ((bf16[16,24,896]{2,1,0:T(8,128)(2,1)}), bf16[16,24,896]{2,1,0:T(8,128)(2,1)S(1)}, u32[]{:S(2)}, u32[]{:S(2)}) async-start(bf16[16,24,896]{2,1,0:T(8,128)(2,1)} %encode.2), calls=%async_computation | async-start | bytes 1376256 | tf_op jit(solution)/shard_map/all_to_all | solution.py:214
  43.4 27.7 %copy-start.2 = (f32[24,768]{1,0:T(8,128)S(1)}, f32[24,768]{1,0:T(8,128)}, u32[]{:S(2)}) copy-start(f32[24,768]{1,0:T(8,128)} %param_ref.3) | copy-start | bytes 221188
  44.9 9.9 %collective-permute-start.5 = (f32[24,128]{1,0:T(8,128)S(1)}, f32[24,128]{1,0:T(8,128)S(1)}, u32[]{:S(2)}, u32[]{:S(2)}) collective-permute-start(f32[24,128]{1,0:T(8,128)S(1)} %get-tuple-element.24), channel_id=1, source_target_pairs={{0,2},{2,0},{1,3},{3,1},{4,6},{6,4},{5,7},{7,5},{8,10},{10,8},{9,1... | collective-permute-start | bytes 36872 | tf_op jit(solution)/shard_map/ppermute | solution.py:216
  54.8 8.3 %collective-permute-start.6 = (f32[24,128]{1,0:T(8,128)S(1)}, f32[24,128]{1,0:T(8,128)S(1)}, u32[]{:S(2)}, u32[]{:S(2)}) collective-permute-start(f32[24,128]{1,0:T(8,128)S(1)} %add.43.near_ref), channel_id=1, source_target_pairs={{0,1},{1,0},{2,3},{3,2},{4,5},{5,4},{6,7},{7,6},{8,9},{9,8},{10,11... | collective-permute-start | bytes 36872 | tf_op jit(solution)/shard_map/ppermute | solution.py:217
  64.2 26.2 %all-to-all-start.3 = ((bf16[16,24,768]{2,1,0:T(8,128)(2,1)}), bf16[16,24,768]{2,1,0:T(8,128)(2,1)S(1)}, u32[]{:S(2)}, u32[]{:S(2)}) async-start(bf16[16,24,768]{2,1,0:T(8,128)(2,1)} %get-tuple-element.25), calls=%async_computation.3 | async-start | bytes 1179648 | tf_op jit(solution)/shard_map/all_to_all | solution.py:221
  72.6 8.3 %collective-permute-start.1 = (f32[24,128]{1,0:T(8,128)S(1)}, f32[24,128]{1,0:T(8,128)S(1)}, u32[]{:S(2)}, u32[]{:S(2)}) collective-permute-start(f32[24,128]{1,0:T(8,128)S(1)} %get-tuple-element.21), channel_id=1, source_target_pairs={{0,2},{2,0},{1,3},{3,1},{4,6},{6,4},{5,7},{7,5},{8,10},{10,8},{9,1... | collective-permute-start | bytes 36872 | tf_op jit(solution)/shard_map/ppermute | solution.py:216
  81.0 8.3 %collective-permute-start.2 = (f32[24,128]{1,0:T(8,128)S(1)}, f32[24,128]{1,0:T(8,128)S(1)}, u32[]{:S(2)}, u32[]{:S(2)}) collective-permute-start(f32[24,128]{1,0:T(8,128)S(1)} %add.42.near_ref), channel_id=1, source_target_pairs={{0,1},{1,0},{2,3},{3,2},{4,5},{5,4},{6,7},{7,6},{8,9},{9,8},{10,11... | collective-permute-start | bytes 36872 | tf_op jit(solution)/shard_map/ppermute | solution.py:217
  90.3 18.6 %all-to-all-start.1 = ((bf16[16,24,768]{2,1,0:T(8,128)(2,1)}), bf16[16,24,768]{2,1,0:T(8,128)(2,1)S(1)}, u32[]{:S(2)}, u32[]{:S(2)}) async-start(bf16[16,24,768]{2,1,0:T(8,128)(2,1)} %get-tuple-element.22), calls=%async_computation.1 | async-start | bytes 1179648 | tf_op jit(solution)/shard_map/all_to_all | solution.py:221
  97.9 23.5 %collective-permute-start.7 = (bf16[16,24,768]{2,1,0:T(8,128)(2,1)S(1)}, bf16[16,24,768]{2,1,0:T(8,128)(2,1)S(1)}, u32[]{:S(2)}, u32[]{:S(2)}) collective-permute-start(bf16[16,24,768]{2,1,0:T(8,128)(2,1)S(1)} %all-to-all-done.3.plane_ref), channel_id=1, source_target_pairs={{0,4},{4,0},{1,5},{5,1},{2,6},{6,2},{3,7},{7,3},{8,12},{12,8},{9,1... | collective-permute-start | bytes 1769480 | tf_op jit(solution)/shard_map/ppermute | solution.py:222
  109.0 14.0 %collective-permute-start.3 = (bf16[16,24,768]{2,1,0:T(8,128)(2,1)S(1)}, bf16[16,24,768]{2,1,0:T(8,128)(2,1)S(1)}, u32[]{:S(2)}, u32[]{:S(2)}) collective-permute-start(bf16[16,24,768]{2,1,0:T(8,128)(2,1)S(1)} %all-to-all-done.1.plane_ref), channel_id=1, source_target_pairs={{0,4},{4,0},{1,5},{5,1},{2,6},{6,2},{3,7},{7,3},{8,12},{12,8},{9,1... | collective-permute-start | bytes 1769480 | tf_op jit(solution)/shard_map/ppermute | solution.py:222

commit v3 on v2

v3 whole, which is shorter than its diff:
```python
import jax
import jax.numpy as jnp
from jax import lax
from jax.experimental import pallas as pl
from jax.experimental.pallas import tpu as pltpu
from jax.sharding import Mesh
from jax.sharding import PartitionSpec as P

ENS_REPLICA = ("ens", "y", "x", "core")
MODEL = ("mz", "my")
SWAP = [(0, 1), (1, 0)]

learn_rate = 0.4
f32 = jnp.float32
bf16 = jnp.bfloat16
SPAN = 173.25
VMEM = pl.BlockSpec(memory_space=pltpu.VMEM)
PARAMS = pltpu.CompilerParams(vmem_limit_bytes=12 << 20)


def shape(*dims, dtype=f32):
    return jax.ShapeDtypeStruct(dims, dtype)


def call(kernel, out_shape, count):
    return pl.pallas_call(
        kernel,
        in_specs=[VMEM] * count,
        out_specs=jax.tree.map(lambda _: VMEM, out_shape),
        out_shape=out_shape,
        compiler_params=PARAMS,
    )


def pieces(a):
    high = a.astype(bf16).astype(f32)
    rest = a - high
    middle = rest.astype(bf16).astype(f32)
    return high, middle, rest - middle


def encode_rows(part, beside):
    size = jnp.abs(part)
    top = jnp.max(size, axis=1, keepdims=True)
    top = (jnp.maximum(top, 1e-30) * (1 + 2.0**-7)).astype(bf16).astype(f32)
    code = jnp.exp(size * (SPAN / top) - SPAN / 2)
    code = jnp.where(part < 0, -code, code)
    lane = lax.broadcasted_iota(jnp.int32, (24, 128), 1)
    return code.astype(bf16), jnp.where(lane == 96, top, beside).astype(bf16)


def decode_rows(code, side):
    code = code.astype(f32)
    size = (jnp.log(jnp.abs(code)) + SPAN / 2) * (side[:, 96:97] * (1 / SPAN))
    return jnp.where(code < 0, -size, size)


def placed(param):
    wide = jnp.concatenate([jnp.zeros((1, 100), f32), param, jnp.zeros((1, 4), f32)], axis=1)
    return jnp.broadcast_to(wide, (8, 128))


def pick_kernel(core_ref, tiles_ref, vector_ref, param_ref, out_ref):
    i = pl.program_id(0)

    @pl.when(i < 4)
    def _():
        out_ref[...] = tiles_ref[0, :, 0]

    @pl.when(i == 4)
    def _():
        out_ref[0, 0:8, :] = jnp.broadcast_to(vector_ref[...], (8, 768))
        out_ref[0, 8:16, 0:128] = placed(param_ref[...])


def pick(core, grad, vector, param):
    return pl.pallas_call(
        pick_kernel,
        grid_spec=pltpu.PrefetchScalarGridSpec(
            num_scalar_prefetch=1,
            grid=(5,),
            in_specs=[
                pl.BlockSpec((1, 4, 1, 24, 768), lambda i, c: (jnp.minimum(i, 3), 0, 1 - c[0], 0, 0)),
                pl.BlockSpec((1, 768), lambda i, c: (0, 0)),
                pl.BlockSpec((1, 24), lambda i, c: (0, 0)),
            ],
            out_specs=pl.BlockSpec((4, 24, 768), lambda i, c: (i, 0, 0)),
        ),
        out_shape=shape(17, 24, 768),
        compiler_params=PARAMS,
        name="pick",
    )(core, grad.reshape(4, 4, 2, 24, 768), vector, param)


def encode_kernel(core_ref, tiles_ref, got_ref, small_ref, vector_ref, param_ref, *refs):
    out_ref = refs[-1]
    core = core_ref[0]
    total = vector_ref[...] + small_ref[0, 0:1, :]
    wide = [jnp.concatenate([total[:, 96 * k : 96 * k + 96], jnp.zeros((1, 32), f32)], axis=1) for k in range(8)]
    mine = placed(param_ref[...])
    theirs = jnp.broadcast_to(small_ref[0, 8:9, 0:128], (8, 128))
    parts = pieces(jnp.concatenate(wide, axis=0))
    first = pieces(jnp.where(core == 0, mine, theirs))
    second = pieces(jnp.where(core == 0, theirs, mine))
    row = lax.broadcasted_iota(jnp.int32, (8, 128), 0)
    listed = jnp.zeros((8, 128), f32)
    for k, a in enumerate((*first, *second)):
        listed = jnp.where(row == k, a, listed)
    lane = lax.broadcasted_iota(jnp.int32, (8, 128), 1)
    beside = jnp.concatenate([jnp.where(lane >= 100, listed, parts[0]), parts[1], parts[2]], axis=0)
    for x in range(4):
        out_ref[x, :, 0:768], out_ref[x, :, 768:896] = encode_rows(tiles_ref[0, x, 0] + got_ref[x], beside)


def encode(core, grad, got, vector, param, message=None):
    t = int(message is not None)
    return pl.pallas_call(
        encode_kernel,
        grid_spec=pltpu.PrefetchScalarGridSpec(
            num_scalar_prefetch=1,
            grid=(4,),
            in_specs=[
                pl.BlockSpec((1, 4, 1, 24, 768), lambda i, c: (i, 0, c[0], 0, 0)),
                pl.BlockSpec((4, 24, 768), lambda i, c: (i, 0, 0)),
                pl.BlockSpec((1, 24, 768), lambda i, c: (16, 0, 0)),
                pl.BlockSpec((1, 768), lambda i, c: (0, 0)),
                pl.BlockSpec((1, 24), lambda i, c: (0, 0)),
            ] + [pl.BlockSpec(memory_space=pl.ANY)] * t,
            out_specs=pl.BlockSpec((4, 24, 896), lambda i, c: (0, 2 * i + t, 0)),
        ),
        out_shape=shape(4, 192, 896, dtype=bf16),
        input_output_aliases={6: 0} if t else {},
        compiler_params=PARAMS,
        name="encode",
    )(core, grad.reshape(4, 4, 2, 24, 768), got, got, vector, param, *([message] * t))


def recode_kernel(message_ref, out_ref):
    lane = lax.broadcasted_iota(jnp.int32, (24, 128), 1)
    to, at = (lax.broadcasted_iota(jnp.int32, (24, 24), d) for d in (0, 1))
    for t in range(2):
        vector = jnp.zeros((8, 128), f32)
        listed = jnp.zeros((24, 128), f32)
        for x in range(4):
            side = message_ref[x, 24 * t : 24 * t + 24, 768:896]
            wide = side.astype(f32)
            vector = vector + (wide[0:8] + wide[8:16] + wide[16:24])
            chosen = ((to == at + 6 * x) & (at < 6)).astype(bf16)
            listed = listed + jnp.dot(chosen, side, preferred_element_type=f32)
        beside = jnp.where(lane >= 100, listed, jnp.concatenate(pieces(vector), axis=0))
        for y in range(4):
            rows = slice(48 * y + 24 * t, 48 * y + 24 * t + 24)
            part = jnp.zeros((24, 768), f32)
            for x in range(4):
                part = part + decode_rows(message_ref[x, rows, 0:768], message_ref[x, rows, 768:896].astype(f32))
            to_y = slice(24 * t, 24 * t + 24)
            out_ref[y, to_y, 0:768], out_ref[y, to_y, 768:896] = encode_rows(part, beside)


def decode_kernel(message_ref, up_ref, down_ref, mean_ref, sizes_ref, vector_ref, params_ref):
    lane = lax.broadcasted_iota(jnp.int32, (24, 128), 1)
    for t, param_ref in enumerate((up_ref, down_ref)):
        rows = slice(24 * t, 24 * t + 24)
        total = jnp.zeros((24, 768), f32)
        beside = jnp.zeros((24, 128), f32)
        for y in range(4):
            side = message_ref[y, rows, 768:896].astype(f32)
            params_ref[t, y] = side
            beside = beside + side
            total = total + decode_rows(message_ref[y, rows, 0:768], side)
        mean = total * 32**-0.5
        mean_ref[rows] = mean
        vector_ref[t] = beside[0:8] + beside[8:16] + beside[16:24]
        param = param_ref[...]
        own = jnp.sum(param * param, axis=1, keepdims=True)
        size = jnp.sum(mean * mean, axis=1, keepdims=True)
        both = jnp.where(lane < 64, own, size)
        for m in range(4):
            sizes_ref[m, rows] = both


def step_kernel(up_ref, down_ref, mean_ref, sizes_ref, next_up_ref, next_down_ref, copies_ref):
    for t, (param_ref, next_ref) in enumerate(((up_ref, next_up_ref), (down_ref, next_down_ref))):
        rows = slice(24 * t, 24 * t + 24)
        sizes = (sizes_ref[0, rows] + sizes_ref[1, rows]) + (sizes_ref[2, rows] + sizes_ref[3, rows])
        ratio = jnp.sqrt(sizes[:, 0:1]) * lax.rsqrt(sizes[:, 64:65] + 1e-06)
        after = param_ref[...] - learn_rate * (mean_ref[rows] * ratio)
        next_ref[...] = after
        half = after.astype(bf16)
        for y in range(4):
            copies_ref[y, rows] = half


def merge_kernel(core_ref, plane_ref, got_ref, up_ref, down_ref):
    core = core_ref[0]
    for ref, at in ((plane_ref, core), (got_ref, 1 - core)):
        for x in range(4):
            up_ref[0, x, pl.ds(at, 1)] = ref[x, :, 0:24]
            down_ref[0, x, pl.ds(at, 1)] = ref[x, :, 24:48]


def merge(core, plane, got):
    out = pl.BlockSpec((1, 4, 2, 24, 768), lambda i, c: (i, 0, 0, 0, 0))
    up, down = pl.pallas_call(
        merge_kernel,
        grid_spec=pltpu.PrefetchScalarGridSpec(
            num_scalar_prefetch=1,
            grid=(4,),
            in_specs=[pl.BlockSpec((4, 1, 48, 768), lambda i, c: (0, i, 0, 0))] * 2,
            out_specs=(out, out),
        ),
        out_shape=(shape(4, 4, 2, 24, 768, dtype=bf16),) * 2,
        compiler_params=PARAMS,
        name="merge",
    )(core, plane, got)
    return up.reshape(768, 768), down.reshape(768, 768)


def vector_kernel(vectors_ref, params_ref, out_ref):
    for t in range(2):
        total = jnp.concatenate([vectors_ref[t, k : k + 1, 0:96] for k in range(8)], axis=1)
        listed = []
        for y in range(4):
            for k in range(0, 24, 3):
                param = params_ref[t, y, k : k + 1] + params_ref[t, y, k + 1 : k + 2] + params_ref[t, y, k + 2 : k + 3]
                listed.append(param[:, 100:124])
        out_ref[t : t + 1] = jnp.concatenate(listed, axis=1) - learn_rate * (total * 32**-0.5)


def exchange(a, axis):
    return lax.all_to_all(a, axis, 0, 0, tiled=True)


def on_device(
    slope_up, slope_down, slope_norm, slope_bias, param_up, param_down, param_norm, param_bias
):
    cores = lax.axis_index("core").astype(jnp.int32).reshape(1)
    turned = param_down.T
    message = None
    for grad, vector, param in ((slope_up[0], slope_norm, param_norm), (slope_down[0].T, slope_bias, param_bias)):
        param = param.reshape(1, 24)
        got = lax.ppermute(pick(cores, grad, vector, param), "core", SWAP)
        message = encode(cores, grad, got, vector, param, message)
    recoded = call(recode_kernel, shape(4, 48, 896, dtype=bf16), 1)(exchange(message, "x"))
    outs = (shape(48, 768), shape(4, 48, 128), shape(2, 8, 128), shape(2, 4, 24, 128))
    mean, sizes, vectors, params = call(decode_kernel, outs, 3)(exchange(recoded, "y"), param_up, turned)
    outs = (shape(24, 768), shape(24, 768), shape(4, 48, 768, dtype=bf16))
    next_up, next_down, copies = call(step_kernel, outs, 4)(param_up, turned, mean, exchange(sizes, MODEL))
    rows = exchange(copies, "y")
    norm, bias = call(vector_kernel, shape(2, 768), 2)(vectors, params)
    at = 24 * lax.axis_index(("y", "x", "core"))
    small = (
        norm.astype(bf16), bias.astype(bf16),
        lax.dynamic_slice_in_dim(norm, at, 24), lax.dynamic_slice_in_dim(bias, at, 24),
    )
    plane = exchange(jnp.broadcast_to(rows[None], (4, 4, 48, 768)), "x")
    plane, half_norm, half_bias, next_norm, next_bias = lax.optimization_barrier((plane, *small))
    half_up, half_down = merge(cores, plane, lax.ppermute(plane, "core", SWAP))
    return half_up, half_down.T, half_norm, half_bias, next_up, next_down.T, next_norm, next_bias


def solution(mesh):
    split = Mesh(
        mesh.devices.reshape(mesh.shape["ens"], 4, 4, 2, 2, 2),
        ("ens", "y", "x", "core", "mz", "my"),
    )
    return jax.shard_map(
        on_device,
        mesh=split,
        in_specs=(
            P(ENS_REPLICA, None, MODEL),
            P(ENS_REPLICA, MODEL, None),
            P(ENS_REPLICA, None),
            P(ENS_REPLICA, None),
            P(ENS_REPLICA, MODEL),
            P(("ens", *MODEL), ("y", "x", "core")),
            P(ENS_REPLICA),
            P(ENS_REPLICA),
        ),
        out_specs=(
            P("ens", MODEL),
            P(("ens", *MODEL), None),
            P("ens"),
            P("ens"),
            P(ENS_REPLICA, MODEL),
            P(("ens", *MODEL), ("y", "x", "core")),
            P(ENS_REPLICA),
            P(ENS_REPLICA),
        ),
        check_vma=False,
    )
```

time: 125 us -> 121 us (0.968)
  blocking collectives: 0 us -> 65.1 us
  starting transfers between devices: 79.4 us -> 21.3 us
  waiting for transfers between devices: 24 us -> 13.5 us
  local copies, waits for them, and re-layouts: 6.67 us -> 8.82 us
  other arithmetic: 1.73 us -> 0 us
    all_to_all x0 -> x4, blocking collectives: none -> 65.1 us  [exchange(): return lax.all_to_all(a, axis, 0, 0, tiled=True)]
    ppermute x8 -> x3, starting transfers between devices: 56.5 us -> 17.8 us  [the longest x2 10.8 us: on_device(): got = lax.ppermute(pick(cores, grad, vector, param), 'core', SWAP)]
    all_to_all x4 -> x1, starting transfers between devices: 22.9 us -> 3.53 us  [exchange(): return lax.all_to_all(a, axis, 0, 0, tiled=True)]
    ppermute x8 -> x3, waiting for transfers between devices: 14.4 us -> 2.54 us  [the longest x1 2.45 us: on_device(): half_up, half_down = merge(cores, plane, lax.ppermute(plane, 'core', SWAP))]
    pallas_call x4, Pallas kernels: 4.99 us -> 2.6 us  [the longest x1 1.3 us: on_device(): call(recode_kernel, shape(4, 48, 896, dtype=bf16), 1)]
    pallas_call x2, Pallas kernels: 1.08 us -> 2.83 us  [pick(): pl.pallas_call(pick_kernel, grid_spec=pltpu.PrefetchScalarGridSpec(num_sc...]
    unnamed x10 -> x20, local copies, waits for them, and re-layouts: 1.68 us -> 3.04 us
    all_to_all x4 -> x1, waiting for transfers between devices: 9.56 us -> 10.9 us  [exchange(): return lax.all_to_all(a, axis, 0, 0, tiled=True)]
  transfers between devices with their start and end apart: 12 -> 4, of which waited for: 8 -> 3; matrix products, arithmetic and copies ran while one was open for 3% -> 3% of each run, Pallas kernels for 6% -> 3%
where the time goes in v3:
time: 121 us
  blocking collectives  65.1 us (54%)
  starting transfers between devices  21.3 us (18%)
  waiting for transfers between devices  13.5 us (11%)
  Pallas kernels  11 us (9%)
  local copies, waits for them, and re-layouts  8.82 us (7%)
    all_to_all x4, blocking collectives, exchange(): return lax.all_to_all(a, axis, 0, 0, tiled=True)  65.1 us
    all_to_all x1, waiting for transfers between devices, exchange(): return lax.all_to_all(a, axis, 0, 0, tiled=True)  10.9 us
    ppermute x2, starting transfers between devices, on_device(): got = lax.ppermute(pick(cores, grad, vector, param), 'core', SWAP)  10.8 us
    ppermute x1, starting transfers between devices, on_device(): half_up, half_down = merge(cores, plane, lax.ppermute(plane, 'core', SWAP))  7.01 us
    pallas_call x2, Pallas kernels, encode(): pl.pallas_call(encode_kernel, grid_spec=pltpu.PrefetchScalarGridSpec(num_...  3.83 us
    all_to_all x1, starting transfers between devices, exchange(): return lax.all_to_all(a, axis, 0, 0, tiled=True)  3.53 us
    unnamed x20, local copies, waits for them, and re-layouts  3.04 us
    pallas_call x2, Pallas kernels, pick(): pl.pallas_call(pick_kernel, grid_spec=pltpu.PrefetchScalarGridSpec(num_sc...  2.83 us
  transfers between devices with their start and end apart: 4, of which 3 were waited for; matrix products, arithmetic and copies ran while one was open for 3% of the time, Pallas kernels for 3%

profile of v3, /device:TPU:1, one launch (start us, length us, event | category | flops | bytes accessed | tf_op | source)
XLA Modules:
  0.0 120.5 jit_solution(2384467858579238773)
XLA Ops:
  0.6 0.0 copy-start
  0.6 1.7 %copy-done = f32[1,768,768]{2,1,0:T(8,128)S(1)} copy-done((f32[1,768,768]{2,1,0:T(8,128)S(1)}, f32[1,768,768]{2,1,0:T(8,128)}, u32[]{:S(2)}) %copy-start) | copy-done | bytes 2359320
  2.3 0.0 copy-start.5
  2.3 0.7 copy-done.5
  3.0 0.0 copy-start.8
  3.0 0.7 copy-done.8
  3.6 2.3 %pick.3 = f32[17,24,768]{2,1,0:T(8,128)} custom-call(s32[1]{0:T(128)} %bitcast.core_ref, f32[4,4,2,24,768]{4,3,2,1,0:T(8,128)S(1)} %bitcast.19, f32[1,768]{1,0:T(1,128)S(1)} %copy-done.5, f32[1,24]{1,0:T(1,128)S(1)} %bitcast.26), custom_call_target="tpu_custom_call" | custom-call | tf_op jit(solution)/shard_map/pick/pallas_call | solution.py:77
  5.9 8.7 %collective-permute-start.1 = (f32[17,24,768]{2,1,0:T(8,128)}, f32[17,24,768]{2,1,0:T(8,128)}, u32[]{:S(2)}, u32[]{:S(2)}) collective-permute-start(f32[17,24,768]{2,1,0:T(8,128)} %pick.3), channel_id=1, source_target_pairs={{0,4},{4,0},{1,5},{5,1},{2,6},{6,2},{3,7},{7,3},{8,12},{12,8},{9,1... | collective-permute-start | bytes 3760136 | tf_op jit(solution)/shard_map/ppermute | solution.py:242
  14.7 0.0 copy-start.4
  14.7 0.0 copy-start.7
  14.7 2.0 %copy.17 = f32[768,768]{1,0:T(8,128)S(1)} copy(f32[768,768]{0,1:T(8,128)} %bitcast.28) | data formatting | bytes 4718592 | tf_op jit(solution)/shard_map/transpose | solution.py:240
  16.7 0.0 copy-done.4
  16.7 0.0 copy-done.7
  16.8 0.0 copy-start.1
  16.8 0.0 copy-start.6
  16.8 0.0 copy-start.9
  16.8 0.6 pick.2
  17.4 2.1 %collective-permute-start = (f32[17,24,768]{2,1,0:T(8,128)S(1)}, f32[17,24,768]{2,1,0:T(8,128)S(1)}, u32[]{:S(2)}, u32[]{:S(2)}) collective-permute-start(f32[17,24,768]{2,1,0:T(8,128)S(1)} %pick.2), channel_id=1, source_target_pairs={{0,4},{4,0},{1,5},{5,1},{2,6},{6,2},{3,7},{7,3},{8,12},{12,8},{9,1... | collective-permute-start | bytes 3760136 | tf_op jit(solution)/shard_map/ppermute | solution.py:242
  19.4 0.0 collective-permute-done.1.got_ref.small_ref
  19.4 0.0 copy-done.1
  19.4 0.0 copy-done.6
  19.5 0.0 copy-done.9
  19.5 2.8 %encode.2.refs_0_ = bf16[4,192,896]{2,1,0:T(8,128)(2,1)S(1)} custom-call(s32[1]{0:T(128)} %bitcast.core_ref, f32[4,4,2,24,768]{4,3,2,1,0:T(8,128)S(1)} %bitcast.20, f32[17,24,768]{2,1,0:T(8,128)} %collective-permute-done.1.got_ref.small_ref, f32[17,24,768]{2,1,0:T(8,128)} %collective-permute-done.1.got_ref.small_ref, f32[1,768]{1,0:T(1,128)S(1)} %copy-done.6, ...), custom_call_target="tpu_custom_call" | custom-call | tf_op jit(solution)/shard_map/encode/pallas_call | solution.py:117
  22.3 0.1 collective-permute-done.got_ref.small_ref
  22.3 1.0 encode.3
  23.4 20.4 %all_to_all.25.message_ref = bf16[4,192,896]{2,1,0:T(8,128)(2,1)S(1)} all-to-all(bf16[4,192,896]{2,1,0:T(8,128)(2,1)S(1)} %encode.3), channel_id=1, replica_groups=mesh['ens'=4,'y'=4,'x'=4,'core'=2,'mz'=2,'my'=2] {'x'}, dimensions={0} | all-to-all | bytes 2752512 | tf_op jit(solution)/shard_map/all_to_all | solution.py:231
  43.8 0.0 copy-start.2
  43.8 0.0 copy-start.3
  43.8 1.3 %shard_map.143 = bf16[4,48,896]{2,1,0:T(8,128)(2,1)S(1)} custom-call(bf16[4,192,896]{2,1,0:T(8,128)(2,1)S(1)} %all_to_all.25.message_ref), custom_call_target="tpu_custom_call" | custom-call | tf_op jit(solution)/shard_map/pallas_call | solution.py:244
  45.1 11.5 %all_to_all.26.message_ref = bf16[4,48,896]{2,1,0:T(8,128)(2,1)S(1)} all-to-all(bf16[4,48,896]{2,1,0:T(8,128)(2,1)S(1)} %shard_map.143), channel_id=1, replica_groups=mesh['ens'=4,'y'=4,'x'=4,'core'=2,'mz'=2,'my'=2] {'y'}, dimensions={0} | all-to-all | bytes 688128 | tf_op jit(solution)/shard_map/all_to_all | solution.py:231
  56.6 0.0 copy-done.2
  56.6 0.0 copy-done.3
  56.6 0.3 shard_map.144
  56.9 23.0 %all_to_all.27.sizes_ref = f32[4,48,128]{2,1,0:T(8,128)S(1)} all-to-all(f32[4,48,128]{2,1,0:T(8,128)S(1)} %get-tuple-element.23), channel_id=1, replica_groups=mesh['ens'=4,'y'=4,'x'=4,'core'=2,'mz'=2,'my'=2] {'mz','my'}, dimensions={0} | all-to-all | bytes 196608 | tf_op jit(solution)/shard_map/all_to_all | solution.py:231
  79.9 0.8 shard_map.145
  80.7 10.2 %all_to_all.28 = bf16[4,48,768]{2,1,0:T(8,128)(2,1)S(1)} all-to-all(bf16[4,48,768]{2,1,0:T(8,128)(2,1)S(1)} %get-tuple-element.24), channel_id=1, replica_groups=mesh['ens'=4,'y'=4,'x'=4,'core'=2,'mz'=2,'my'=2] {'y'}, dimensions={0} | all-to-all | bytes 589824 | tf_op jit(solution)/shard_map/all_to_all | solution.py:231
  90.9 1.1 broadcast_in_dim.2
  92.0 3.5 %all-to-all-start.4 = ((bf16[4,4,48,768]{3,2,1,0:T(8,128)(2,1)}), bf16[4,4,48,768]{3,2,1,0:T(8,128)(2,1)S(1)}, u32[]{:S(2)}, u32[]{:S(2)}) async-start(bf16[4,4,48,768]{3,2,1,0:T(8,128)(2,1)} %broadcast_in_dim.2), calls=%async_computation.4 | async-start | bytes 2359296 | tf_op jit(solution)/shard_map/all_to_all | solution.py:231
  95.6 0.1 shard_map.146
  95.7 0.6 dynamic-slice_bitcast_fusion
  96.3 0.6 convert_reduce_fusion
  96.9 10.9 %all-to-all-done.4.plane_ref = bf16[4,4,48,768]{3,2,1,0:T(8,128)(2,1)S(1)} async-done(((bf16[4,4,48,768]{3,2,1,0:T(8,128)(2,1)}), bf16[4,4,48,768]{3,2,1,0:T(8,128)(2,1)S(1)}, u32[]{:S(2)}, u32[]{:S(2)}) %all-to-all-start.4) | async-done | bytes 1179680 | tf_op jit(solution)/shard_map/all_to_all | solution.py:231
  107.9 7.0 %collective-permute-start.2 = (bf16[4,4,48,768]{3,2,1,0:T(8,128)(2,1)S(1)}, bf16[4,4,48,768]{3,2,1,0:T(8,128)(2,1)S(1)}, u32[]{:S(2)}, u32[]{:S(2)}) collective-permute-start(bf16[4,4,48,768]{3,2,1,0:T(8,128)(2,1)S(1)} %all-to-all-done.4.plane_ref), channel_id=1, source_target_pairs={{0,4},{4,0},{1,5},{5,1},{2,6},{6,2},{3,7},{7,3},{8,12},{12,8},{9,1... | collective-permute-start | bytes 3538952 | tf_op jit(solution)/shard_map/ppermute | solution.py:258
  114.9 2.5 %collective-permute-done.2.got_ref = bf16[4,4,48,768]{3,2,1,0:T(8,128)(2,1)S(1)} collective-permute-done((bf16[4,4,48,768]{3,2,1,0:T(8,128)(2,1)S(1)}, bf16[4,4,48,768]{3,2,1,0:T(8,128)(2,1)S(1)}, u32[]{:S(2)}, u32[]{:S(2)}) %collective-permute-start.2) | collective-permute-done | bytes 1179680 | tf_op jit(solution)/shard_map/ppermute | solution.py:258
  117.3 1.7 %merge.1 = (bf16[4,4,2,24,768]{4,3,2,1,0:T(8,128)(2,1)}, bf16[4,4,2,24,768]{4,3,2,1,0:T(8,128)(2,1)S(1)}) custom-call(s32[1]{0:T(128)} %bitcast.core_ref, bf16[4,4,48,768]{3,2,1,0:T(8,128)(2,1)S(1)} %all-to-all-done.4.plane_ref, bf16[4,4,48,768]{3,2,1,0:T(8,128)(2,1)S(1)} %collective-permute-done.2.got_ref), custom_call_target="tpu_custom_call" | custom-call | tf_op jit(solution)/shard_map/merge/pallas_call | solution.py:204
  119.1 1.4 %copy.18 = bf16[768,768]{0,1:T(8,128)(2,1)} copy(bf16[768,768]{1,0:T(8,128)(2,1)S(1)} %bitcast.21) | data formatting | bytes 2359296 | tf_op jit(solution)/shard_map/reshape | solution.py:216
  (1 shorter events, 0.0 us)
Async XLA Ops:
  0.6 1.7 %copy-start = (f32[1,768,768]{2,1,0:T(8,128)S(1)}, f32[1,768,768]{2,1,0:T(8,128)}, u32[]{:S(2)}) copy-start(f32[1,768,768]{2,1,0:T(8,128)} %param.8) | copy-start | bytes 7077892
  2.3 0.7 copy-start.5
  3.0 0.7 copy-start.8
  5.9 13.5 %collective-permute-start.1 = (f32[17,24,768]{2,1,0:T(8,128)}, f32[17,24,768]{2,1,0:T(8,128)}, u32[]{:S(2)}, u32[]{:S(2)}) collective-permute-start(f32[17,24,768]{2,1,0:T(8,128)} %pick.3), channel_id=1, source_target_pairs={{0,4},{4,0},{1,5},{5,1},{2,6},{6,2},{3,7},{7,3},{8,12},{12,8},{9,1... | collective-permute-start | bytes 3760136 | tf_op jit(solution)/shard_map/ppermute | solution.py:242
  14.7 2.1 %copy-start.4 = (f32[1,768]{1,0:T(1,128)S(1)}, f32[1,768]{1,0:T(1,128)}, u32[]{:S(2)}) copy-start(f32[1,768]{1,0:T(1,128)} %vector_ref.7) | copy-start | bytes 9220
  14.7 2.1 %copy-start.7 = (f32[24]{0:T(128)S(1)}, f32[24]{0:T(128)}, u32[]{:S(2)}) copy-start(f32[24]{0:T(128)} %param.15) | copy-start | bytes 292
  16.8 2.7 %copy-start.1 = (f32[1,768,768]{2,1,0:T(8,128)S(1)}, f32[1,768,768]{2,1,0:T(8,128)}, u32[]{:S(2)}) copy-start(f32[1,768,768]{2,1,0:T(8,128)} %param.8) | copy-start | bytes 7077892
  16.8 2.7 %copy-start.6 = (f32[1,768]{1,0:T(1,128)S(1)}, f32[1,768]{1,0:T(1,128)}, u32[]{:S(2)}) copy-start(f32[1,768]{1,0:T(1,128)} %vector_ref.6) | copy-start | bytes 9220
  16.8 2.7 %copy-start.9 = (f32[24]{0:T(128)S(1)}, f32[24]{0:T(128)}, u32[]{:S(2)}) copy-start(f32[24]{0:T(128)} %param.14) | copy-start | bytes 292
  17.4 5.0 %collective-permute-start = (f32[17,24,768]{2,1,0:T(8,128)S(1)}, f32[17,24,768]{2,1,0:T(8,128)S(1)}, u32[]{:S(2)}, u32[]{:S(2)}) collective-permute-start(f32[17,24,768]{2,1,0:T(8,128)S(1)} %pick.2), channel_id=1, source_target_pairs={{0,4},{4,0},{1,5},{5,1},{2,6},{6,2},{3,7},{7,3},{8,12},{12,8},{9,1... | collective-permute-start | bytes 3760136 | tf_op jit(solution)/shard_map/ppermute | solution.py:242
  43.8 12.8 %copy-start.2 = (f32[24,768]{1,0:T(8,128)S(1)}, f32[24,768]{1,0:T(8,128)}, u32[]{:S(2)}) copy-start(f32[24,768]{1,0:T(8,128)} %up_ref.3) | copy-start | bytes 221188
  43.8 12.8 %copy-start.3 = (f32[768,24]{0,1:T(8,128)S(1)}, f32[768,24]{0,1:T(8,128)}, u32[]{:S(2)}) copy-start(f32[768,24]{0,1:T(8,128)} %param.13) | copy-start | bytes 221188
  92.0 15.8 %all-to-all-start.4 = ((bf16[4,4,48,768]{3,2,1,0:T(8,128)(2,1)}), bf16[4,4,48,768]{3,2,1,0:T(8,128)(2,1)S(1)}, u32[]{:S(2)}, u32[]{:S(2)}) async-start(bf16[4,4,48,768]{3,2,1,0:T(8,128)(2,1)} %broadcast_in_dim.2), calls=%async_computation.4 | async-start | bytes 2359296 | tf_op jit(solution)/shard_map/all_to_all | solution.py:231
  107.9 9.5 %collective-permute-start.2 = (bf16[4,4,48,768]{3,2,1,0:T(8,128)(2,1)S(1)}, bf16[4,4,48,768]{3,2,1,0:T(8,128)(2,1)S(1)}, u32[]{:S(2)}, u32[]{:S(2)}) collective-permute-start(bf16[4,4,48,768]{3,2,1,0:T(8,128)(2,1)S(1)} %all-to-all-done.4.plane_ref), channel_id=1, source_target_pairs={{0,4},{4,0},{1,5},{5,1},{2,6},{6,2},{3,7},{7,3},{8,12},{12,8},{9,1... | collective-permute-start | bytes 3538952 | tf_op jit(solution)/shard_map/ppermute | solution.py:258

commit v4 on v3

--- a/solution.py
+++ b/solution.py
@@ -16,6 +16,10 @@
 SPAN = 173.25
 VMEM = pl.BlockSpec(memory_space=pltpu.VMEM)
 PARAMS = pltpu.CompilerParams(vmem_limit_bytes=12 << 20)
+
+
+def in_hbm(*arrays):
+    return [pltpu.with_memory_space_constraint(a, pltpu.HBM) for a in arrays]
 
 
 def shape(*dims, dtype=f32):
@@ -63,33 +67,33 @@
 def pick_kernel(core_ref, tiles_ref, vector_ref, param_ref, out_ref):
     i = pl.program_id(0)
 
-    @pl.when(i < 4)
+    @pl.when(i < 2)
     def _():
-        out_ref[...] = tiles_ref[0, :, 0]
-
-    @pl.when(i == 4)
+        out_ref[...] = tiles_ref[:, 0]
+
+    @pl.when(i == 2)
     def _():
         out_ref[0, 0:8, :] = jnp.broadcast_to(vector_ref[...], (8, 768))
         out_ref[0, 8:16, 0:128] = placed(param_ref[...])
 
 
-def pick(core, grad, vector, param):
+def pick(core, tiles, vector, param):
     return pl.pallas_call(
         pick_kernel,
         grid_spec=pltpu.PrefetchScalarGridSpec(
             num_scalar_prefetch=1,
-            grid=(5,),
+            grid=(3,),
             in_specs=[
-                pl.BlockSpec((1, 4, 1, 24, 768), lambda i, c: (jnp.minimum(i, 3), 0, 1 - c[0], 0, 0)),
+                pl.BlockSpec((8, 1, 24, 768), lambda i, c: (jnp.minimum(i, 1), 1 - c[0], 0, 0)),
                 pl.BlockSpec((1, 768), lambda i, c: (0, 0)),
                 pl.BlockSpec((1, 24), lambda i, c: (0, 0)),
             ],
-            out_specs=pl.BlockSpec((4, 24, 768), lambda i, c: (i, 0, 0)),
-        ),
-        out_shape=shape(17, 24, 768),
+            out_specs=pl.BlockSpec((8, 24, 768), lambda i, c: (i, 0, 0)),
+        ),
+        out_shape=pltpu.VMEM((17, 24, 768), f32),
         compiler_params=PARAMS,
         name="pick",
-    )(core, grad.reshape(4, 4, 2, 24, 768), vector, param)
+    )(core, tiles, vector, param)
 
 
 def encode_kernel(core_ref, tiles_ref, got_ref, small_ref, vector_ref, param_ref, *refs):
@@ -192,28 +196,34 @@
 
 
 def merge_kernel(core_ref, plane_ref, got_ref, up_ref, down_ref):
-    core = core_ref[0]
-    for ref, at in ((plane_ref, core), (got_ref, 1 - core)):
+    even = core_ref[0] == 0
+    columns = []
+    for y in range(2):
         for x in range(4):
-            up_ref[0, x, pl.ds(at, 1)] = ref[x, :, 0:24]
-            down_ref[0, x, pl.ds(at, 1)] = ref[x, :, 24:48]
+            mine, other = plane_ref[x, y], got_ref[x, y]
+            for c, pair in enumerate((jnp.where(even, mine, other), jnp.where(even, other, mine))):
+                up_ref[y, x, c] = pair[0:24]
+                columns.append(pair.astype(f32)[24:48])
+    down_ref[...] = jnp.concatenate(columns, axis=0).T.astype(bf16)
 
 
 def merge(core, plane, got):
-    out = pl.BlockSpec((1, 4, 2, 24, 768), lambda i, c: (i, 0, 0, 0, 0))
     up, down = pl.pallas_call(
         merge_kernel,
         grid_spec=pltpu.PrefetchScalarGridSpec(
             num_scalar_prefetch=1,
-            grid=(4,),
-            in_specs=[pl.BlockSpec((4, 1, 48, 768), lambda i, c: (0, i, 0, 0))] * 2,
-            out_specs=(out, out),
-        ),
-        out_shape=(shape(4, 4, 2, 24, 768, dtype=bf16),) * 2,
+            grid=(2,),
+            in_specs=[pl.BlockSpec((4, 2, 48, 768), lambda i, c: (0, i, 0, 0))] * 2,
+            out_specs=(
+                pl.BlockSpec((2, 4, 2, 24, 768), lambda i, c: (i, 0, 0, 0, 0)),
+                pl.BlockSpec((768, 384), lambda i, c: (0, i)),
+            ),
+        ),
+        out_shape=(shape(4, 4, 2, 24, 768, dtype=bf16), shape(768, 768, dtype=bf16)),
         compiler_params=PARAMS,
         name="merge",
     )(core, plane, got)
-    return up.reshape(768, 768), down.reshape(768, 768)
+    return up.reshape(768, 768), down
 
 
 def vector_kernel(vectors_ref, params_ref, out_ref):
@@ -239,7 +249,8 @@
     message = None
     for grad, vector, param in ((slope_up[0], slope_norm, param_norm), (slope_down[0].T, slope_bias, param_bias)):
         param = param.reshape(1, 24)
-        got = lax.ppermute(pick(cores, grad, vector, param), "core", SWAP)
+        first = (grad.reshape(16, 2, 24, 768), vector, param)
+        got = lax.ppermute(pick(cores, *(first if message is not None else in_hbm(*first))), "core", SWAP)
         message = encode(cores, grad, got, vector, param, message)
     recoded = call(recode_kernel, shape(4, 48, 896, dtype=bf16), 1)(exchange(message, "x"))
     outs = (shape(48, 768), shape(4, 48, 128), shape(2, 8, 128), shape(2, 4, 24, 128))
@@ -249,14 +260,12 @@
     rows = exchange(copies, "y")
     norm, bias = call(vector_kernel, shape(2, 768), 2)(vectors, params)
     at = 24 * lax.axis_index(("y", "x", "core"))
-    small = (
-        norm.astype(bf16), bias.astype(bf16),
+    plane = exchange(jnp.broadcast_to(rows[None], (4, 4, 48, 768)), "x")
+    half_up, half_down = merge(cores, plane, lax.ppermute(plane, "core", SWAP))
+    return (
+        half_up, half_down, norm.astype(bf16), bias.astype(bf16), next_up, next_down.T,
         lax.dynamic_slice_in_dim(norm, at, 24), lax.dynamic_slice_in_dim(bias, at, 24),
     )
-    plane = exchange(jnp.broadcast_to(rows[None], (4, 4, 48, 768)), "x")
-    plane, half_norm, half_bias, next_norm, next_bias = lax.optimization_barrier((plane, *small))
-    half_up, half_down = merge(cores, plane, lax.ppermute(plane, "core", SWAP))
-    return half_up, half_down.T, half_norm, half_bias, next_up, next_down.T, next_norm, next_bias
 
 
 def solution(mesh):

time: 121 us -> 115 us (0.950)
  blocking collectives: 65.1 us -> 80.1 us
  waiting for transfers between devices: 13.5 us -> 1.16 us
  local copies, waits for them, and re-layouts: 8.82 us -> 3.37 us
  starting transfers between devices: 21.3 us -> 17.5 us
    all_to_all x4 -> x5, blocking collectives: 65.1 us -> 80.1 us  [exchange(): return lax.all_to_all(a, axis, 0, 0, tiled=True)]
    all_to_all x1 -> x0, waiting for transfers between devices: 10.9 us -> none  [exchange(): return lax.all_to_all(a, axis, 0, 0, tiled=True)]
    all_to_all x1 -> x0, starting transfers between devices: 3.53 us -> none  [exchange(): return lax.all_to_all(a, axis, 0, 0, tiled=True)]
    unnamed x20 -> x14, local copies, waits for them, and re-layouts: 3.04 us -> 0.04 us
    reshape x1 -> x0, local copies, waits for them, and re-layouts: 1.44 us -> none  [merge(): return (up.reshape(768, 768), down.reshape(768, 768))]
    ppermute x1, waiting for transfers between devices: 2.45 us -> 1.07 us  [on_device(): half_up, half_down = merge(cores, plane, lax.ppermute(plane, 'core', SWAP))]
  transfers between devices with their start and end apart: 4 -> 3, of which waited for: 3 -> 2; matrix products, arithmetic and copies ran while one was open for 3% -> 3% of each run, Pallas kernels for 3% -> 3%
where the time goes in v4:
time: 115 us; the launch traced here: 114 us
  blocking collectives  80.1 us (70%)
  starting transfers between devices  17.5 us (15%)
  Pallas kernels  11.4 us (10%)
  local copies, waits for them, and re-layouts  3.37 us (3%)
  waiting for transfers between devices  1.16 us (1%)
    all_to_all x5, blocking collectives, exchange(): return lax.all_to_all(a, axis, 0, 0, tiled=True)  80.1 us
    ppermute x2, starting transfers between devices, on_device(): lax.ppermute(pick(cores, *(first if message is not None else in_hbm(*firs...  10.8 us
    ppermute x1, starting transfers between devices, on_device(): half_up, half_down = merge(cores, plane, lax.ppermute(plane, 'core', SWAP))  6.72 us
    pallas_call x2, Pallas kernels, encode(): pl.pallas_call(encode_kernel, grid_spec=pltpu.PrefetchScalarGridSpec(num_...  3.83 us
    pallas_call x2, Pallas kernels, pick(): pl.pallas_call(pick_kernel, grid_spec=pltpu.PrefetchScalarGridSpec(num_sc...  3.13 us
  transfers between devices with their start and end apart: 3, of which 2 were waited for; matrix products, arithmetic and copies ran while one was open for 3% of the time, Pallas kernels for 3%

profile of v4, /device:TPU:1, one launch (start us, length us, event | category | flops | bytes accessed | tf_op | source)
XLA Modules:
  0.0 114.4 jit_solution(13185458509822058459)
XLA Ops:
  0.6 2.7 %pick.3 = f32[17,24,768]{2,1,0:T(8,128)} custom-call(s32[1]{0:T(128)} %bitcast.core_ref, f32[16,2,24,768]{3,2,1,0:T(8,128)} %bitcast.19, f32[1,768]{1,0:T(1,128)} %vector_ref.6, f32[1,24]{1,0:T(1,128)} %bitcast.25), custom_call_target="tpu_custom_call" | custom-call | tf_op jit(solution)/shard_map/pick/pallas_call | solution.py:81
  3.3 8.7 %collective-permute-start.1 = (f32[17,24,768]{2,1,0:T(8,128)}, f32[17,24,768]{2,1,0:T(8,128)}, u32[]{:S(2)}, u32[]{:S(2)}) collective-permute-start(f32[17,24,768]{2,1,0:T(8,128)} %pick.3), channel_id=1, source_target_pairs={{0,4},{4,0},{1,5},{5,1},{2,6},{6,2},{3,7},{7,3},{8,12},{12,8},{9,1... | collective-permute-start | bytes 3760136 | tf_op jit(solution)/shard_map/ppermute | solution.py:253
  12.0 0.0 copy-start.3
  12.1 0.0 copy-start.5
  12.1 2.0 %copy.17 = f32[768,768]{1,0:T(8,128)S(1)} copy(f32[768,768]{0,1:T(8,128)} %bitcast.27) | data formatting | bytes 4718592 | tf_op jit(solution)/shard_map/transpose | solution.py:250
  14.1 0.0 copy-done.3
  14.1 0.0 copy-done.5
  14.1 0.0 copy-start
  14.2 0.0 copy-start.4
  14.2 0.0 copy-start.6
  14.2 0.5 pick.2
  14.7 2.1 %collective-permute-start = (f32[17,24,768]{2,1,0:T(8,128)S(1)}, f32[17,24,768]{2,1,0:T(8,128)S(1)}, u32[]{:S(2)}, u32[]{:S(2)}) collective-permute-start(f32[17,24,768]{2,1,0:T(8,128)S(1)} %pick.2), channel_id=1, source_target_pairs={{0,4},{4,0},{1,5},{5,1},{2,6},{6,2},{3,7},{7,3},{8,12},{12,8},{9,1... | collective-permute-start | bytes 3760136 | tf_op jit(solution)/shard_map/ppermute | solution.py:253
  16.7 0.0 collective-permute-done.1.got_ref.small_ref
  16.7 0.0 copy-done
  16.7 0.0 copy-done.4
  16.7 0.0 copy-done.6
  16.8 2.8 %encode.2.refs_0_ = bf16[4,192,896]{2,1,0:T(8,128)(2,1)S(1)} custom-call(s32[1]{0:T(128)} %bitcast.core_ref, f32[4,4,2,24,768]{4,3,2,1,0:T(8,128)S(1)} %bitcast.20, f32[17,24,768]{2,1,0:T(8,128)} %collective-permute-done.1.got_ref.small_ref, f32[17,24,768]{2,1,0:T(8,128)} %collective-permute-done.1.got_ref.small_ref, f32[1,768]{1,0:T(1,128)S(1)} %copy-done.4, ...), custom_call_target="tpu_custom_call" | custom-call | tf_op jit(solution)/shard_map/encode/pallas_call | solution.py:121
  19.5 0.1 collective-permute-done.got_ref.small_ref
  19.6 1.0 encode.3
  20.7 20.4 %all_to_all.25.message_ref = bf16[4,192,896]{2,1,0:T(8,128)(2,1)S(1)} all-to-all(bf16[4,192,896]{2,1,0:T(8,128)(2,1)S(1)} %encode.3), channel_id=1, replica_groups=mesh['ens'=4,'y'=4,'x'=4,'core'=2,'mz'=2,'my'=2] {'x'}, dimensions={0} | all-to-all | bytes 2752512 | tf_op jit(solution)/shard_map/all_to_all | solution.py:241
  41.1 0.0 copy-start.1
  41.1 0.0 copy-start.2
  41.1 1.3 %shard_map.143 = bf16[4,48,896]{2,1,0:T(8,128)(2,1)S(1)} custom-call(bf16[4,192,896]{2,1,0:T(8,128)(2,1)S(1)} %all_to_all.25.message_ref), custom_call_target="tpu_custom_call" | custom-call | tf_op jit(solution)/shard_map/pallas_call | solution.py:255
  42.4 11.5 %all_to_all.26.message_ref = bf16[4,48,896]{2,1,0:T(8,128)(2,1)S(1)} all-to-all(bf16[4,48,896]{2,1,0:T(8,128)(2,1)S(1)} %shard_map.143), channel_id=1, replica_groups=mesh['ens'=4,'y'=4,'x'=4,'core'=2,'mz'=2,'my'=2] {'y'}, dimensions={0} | all-to-all | bytes 688128 | tf_op jit(solution)/shard_map/all_to_all | solution.py:241
  53.9 0.0 copy-done.1
  53.9 0.0 copy-done.2
  53.9 0.3 shard_map.144
  54.2 23.0 %all_to_all.27.sizes_ref = f32[4,48,128]{2,1,0:T(8,128)S(1)} all-to-all(f32[4,48,128]{2,1,0:T(8,128)S(1)} %get-tuple-element.18), channel_id=1, replica_groups=mesh['ens'=4,'y'=4,'x'=4,'core'=2,'mz'=2,'my'=2] {'mz','my'}, dimensions={0} | all-to-all | bytes 196608 | tf_op jit(solution)/shard_map/all_to_all | solution.py:241
  77.2 0.8 shard_map.145
  78.0 10.2 %all_to_all.28 = bf16[4,48,768]{2,1,0:T(8,128)(2,1)S(1)} all-to-all(bf16[4,48,768]{2,1,0:T(8,128)(2,1)S(1)} %get-tuple-element.19), channel_id=1, replica_groups=mesh['ens'=4,'y'=4,'x'=4,'core'=2,'mz'=2,'my'=2] {'y'}, dimensions={0} | all-to-all | bytes 589824 | tf_op jit(solution)/shard_map/all_to_all | solution.py:241
  88.2 0.1 broadcast_in_dim.2
  88.3 15.1 %all_to_all.29.plane_ref = bf16[4,4,48,768]{3,2,1,0:T(8,128)(2,1)S(1)} all-to-all(bf16[4,4,48,768]{3,2,1,0:T(8,128)(2,1)S(1)} %broadcast_in_dim.2), channel_id=1, replica_groups=mesh['ens'=4,'y'=4,'x'=4,'core'=2,'mz'=2,'my'=2] {'x'}, dimensions={0} | all-to-all | bytes 2359296 | tf_op jit(solution)/shard_map/all_to_all | solution.py:241
  103.4 6.7 %collective-permute-start.2 = (bf16[4,4,48,768]{3,2,1,0:T(8,128)(2,1)S(1)}, bf16[4,4,48,768]{3,2,1,0:T(8,128)(2,1)S(1)}, u32[]{:S(2)}, u32[]{:S(2)}) collective-permute-start(bf16[4,4,48,768]{3,2,1,0:T(8,128)(2,1)S(1)} %all_to_all.29.plane_ref), channel_id=1, source_target_pairs={{0,4},{4,0},{1,5},{5,1},{2,6},{6,2},{3,7},{7,3},{8,12},{12,8},{9,1... | collective-permute-start | bytes 3538952 | tf_op jit(solution)/shard_map/ppermute | solution.py:264
  110.1 0.1 shard_map.146
  110.3 0.6 dynamic-slice_bitcast_fusion
  110.9 0.6 convert_reduce_fusion
  111.5 1.1 collective-permute-done.2.got_ref
  112.5 1.8 %merge.1 = (bf16[4,4,2,24,768]{4,3,2,1,0:T(8,128)(2,1)}, bf16[768,768]{1,0:T(8,128)(2,1)}) custom-call(s32[1]{0:T(128)} %bitcast.core_ref, bf16[4,4,48,768]{3,2,1,0:T(8,128)(2,1)S(1)} %all_to_all.29.plane_ref, bf16[4,4,48,768]{3,2,1,0:T(8,128)(2,1)S(1)} %collective-permute-done.2.got_ref), custom_call_target="tpu_custom_call" | custom-call | tf_op jit(solution)/shard_map/merge/pallas_call | solution.py:211
  (1 shorter events, 0.0 us)
Async XLA Ops:
  3.3 13.4 %collective-permute-start.1 = (f32[17,24,768]{2,1,0:T(8,128)}, f32[17,24,768]{2,1,0:T(8,128)}, u32[]{:S(2)}, u32[]{:S(2)}) collective-permute-start(f32[17,24,768]{2,1,0:T(8,128)} %pick.3), channel_id=1, source_target_pairs={{0,4},{4,0},{1,5},{5,1},{2,6},{6,2},{3,7},{7,3},{8,12},{12,8},{9,1... | collective-permute-start | bytes 3760136 | tf_op jit(solution)/shard_map/ppermute | solution.py:253
  12.0 2.1 %copy-start.3 = (f32[1,768]{1,0:T(1,128)S(1)}, f32[1,768]{1,0:T(1,128)}, u32[]{:S(2)}) copy-start(f32[1,768]{1,0:T(1,128)} %vector_ref.7) | copy-start | bytes 9220
  12.1 2.1 %copy-start.5 = (f32[24]{0:T(128)S(1)}, f32[24]{0:T(128)}, u32[]{:S(2)}) copy-start(f32[24]{0:T(128)} %param.15) | copy-start | bytes 292
  14.1 2.6 %copy-start = (f32[1,768,768]{2,1,0:T(8,128)S(1)}, f32[1,768,768]{2,1,0:T(8,128)}, u32[]{:S(2)}) copy-start(f32[1,768,768]{2,1,0:T(8,128)} %param.8) | copy-start | bytes 7077892
  14.2 2.6 %copy-start.4 = (f32[1,768]{1,0:T(1,128)S(1)}, f32[1,768]{1,0:T(1,128)}, u32[]{:S(2)}) copy-start(f32[1,768]{1,0:T(1,128)} %vector_ref.6) | copy-start | bytes 9220
  14.2 2.6 %copy-start.6 = (f32[24]{0:T(128)S(1)}, f32[24]{0:T(128)}, u32[]{:S(2)}) copy-start(f32[24]{0:T(128)} %param.14) | copy-start | bytes 292
  14.7 5.0 %collective-permute-start = (f32[17,24,768]{2,1,0:T(8,128)S(1)}, f32[17,24,768]{2,1,0:T(8,128)S(1)}, u32[]{:S(2)}, u32[]{:S(2)}) collective-permute-start(f32[17,24,768]{2,1,0:T(8,128)S(1)} %pick.2), channel_id=1, source_target_pairs={{0,4},{4,0},{1,5},{5,1},{2,6},{6,2},{3,7},{7,3},{8,12},{12,8},{9,1... | collective-permute-start | bytes 3760136 | tf_op jit(solution)/shard_map/ppermute | solution.py:253
  41.1 12.8 %copy-start.1 = (f32[24,768]{1,0:T(8,128)S(1)}, f32[24,768]{1,0:T(8,128)}, u32[]{:S(2)}) copy-start(f32[24,768]{1,0:T(8,128)} %up_ref.3) | copy-start | bytes 221188
  41.1 12.8 %copy-start.2 = (f32[768,24]{0,1:T(8,128)S(1)}, f32[768,24]{0,1:T(8,128)}, u32[]{:S(2)}) copy-start(f32[768,24]{0,1:T(8,128)} %param.13) | copy-start | bytes 221188
  103.4 9.2 %collective-permute-start.2 = (bf16[4,4,48,768]{3,2,1,0:T(8,128)(2,1)S(1)}, bf16[4,4,48,768]{3,2,1,0:T(8,128)(2,1)S(1)}, u32[]{:S(2)}, u32[]{:S(2)}) collective-permute-start(bf16[4,4,48,768]{3,2,1,0:T(8,128)(2,1)S(1)} %all_to_all.29.plane_ref), channel_id=1, source_target_pairs={{0,4},{4,0},{1,5},{5,1},{2,6},{6,2},{3,7},{7,3},{8,12},{12,8},{9,1... | collective-permute-start | bytes 3538952 | tf_op jit(solution)/shard_map/ppermute | solution.py:264

commit v5 on v4

v5 whole, which is shorter than its diff:
```python
import jax
import jax.numpy as jnp
from jax import lax
from jax.experimental import pallas as pl
from jax.experimental.pallas import tpu as pltpu
from jax.sharding import Mesh
from jax.sharding import PartitionSpec as P

ENS_REPLICA = ("ens", "y", "x", "core")
MODEL = ("mz", "my")
SWAP = [(0, 1), (1, 0)]

learn_rate = 0.4
f32 = jnp.float32
bf16 = jnp.bfloat16
SPAN = 173.25
VMEM = pl.BlockSpec(memory_space=pltpu.VMEM)
PARAMS = pltpu.CompilerParams(vmem_limit_bytes=12 << 20)


def in_hbm(*arrays):
    return [pltpu.with_memory_space_constraint(a, pltpu.HBM) for a in arrays]


def shape(*dims, dtype=f32):
    return jax.ShapeDtypeStruct(dims, dtype)


def call(kernel, out_shape, count):
    return pl.pallas_call(
        kernel,
        in_specs=[VMEM] * count,
        out_specs=jax.tree.map(lambda _: VMEM, out_shape),
        out_shape=out_shape,
        compiler_params=PARAMS,
    )


def pieces(a):
    high = a.astype(bf16).astype(f32)
    rest = a - high
    middle = rest.astype(bf16).astype(f32)
    return high, middle, rest - middle


def encode_rows(part):
    size = jnp.abs(part)
    top = jnp.max(size, axis=1, keepdims=True)
    top = (jnp.maximum(top, 1e-30) * (1 + 2.0**-7)).astype(bf16).astype(f32)
    code = jnp.exp(size * (SPAN / top) - SPAN / 2)
    return jnp.where(part < 0, -code, code).astype(bf16), top


def decode_rows(code, top):
    code = code.astype(f32)
    size = (jnp.log(jnp.abs(code)) + SPAN / 2) * (top * (1 / SPAN))
    return jnp.where(code < 0, -size, size)


def diagonal(width, first):
    row, lane = (lax.broadcasted_iota(jnp.int32, (24, width), d) for d in (0, 1))
    return lane == row + first


def laid(top, width, first):
    return jnp.sum(jnp.where(diagonal(width, first), top, 0.0), axis=0, keepdims=True)


def stood(lanes, first):
    return jnp.sum(jnp.where(diagonal(lanes.shape[1], first), lanes, 0.0), axis=1, keepdims=True)


def padded(before, a, width):
    parts = [jnp.zeros((1, before), f32)] * (before > 0) + [a]
    after = width - before - a.shape[1]
    return jnp.concatenate(parts + [jnp.zeros((1, after), f32)] * (after > 0), axis=1)


def pick_up_kernel(core_ref, tiles_ref, vector_ref, param_ref, out_ref):
    i = pl.program_id(0)

    @pl.when(i < 2)
    def _():
        out_ref[...] = tiles_ref[:, 0]

    @pl.when(i == 2)
    def _():
        out_ref[0, 0:8, :] = jnp.broadcast_to(vector_ref[...], (8, 768))
        out_ref[0, 8:16, :] = jnp.broadcast_to(padded(0, param_ref[...], 768), (8, 768))


def pick_down_kernel(core_ref, tiles_ref, vector_ref, param_ref, out_ref, mine_ref):
    i = pl.program_id(0)

    @pl.when(i < 2)
    def _():
        rows = tiles_ref[...].T
        even = core_ref[0] == 0
        for o in range(8):
            first, second = rows[48 * o : 48 * o + 24], rows[48 * o + 24 : 48 * o + 48]
            mine_ref[o] = jnp.where(even, first, second)
            out_ref[o] = jnp.where(even, second, first)

    @pl.when(i == 2)
    def _():
        out_ref[0, 0:8, :] = jnp.broadcast_to(vector_ref[...], (8, 768))
        out_ref[0, 8:16, :] = jnp.broadcast_to(padded(0, param_ref[...], 768), (8, 768))


VECTOR_SPECS = [pl.BlockSpec((1, 768), lambda i, c: (0, 0)), pl.BlockSpec((1, 24), lambda i, c: (0, 0))]


def pick_up(core, tiles, vector, param):
    return pl.pallas_call(
        pick_up_kernel,
        grid_spec=pltpu.PrefetchScalarGridSpec(
            num_scalar_prefetch=1,
            grid=(3,),
            in_specs=[pl.BlockSpec((8, 1, 24, 768), lambda i, c: (jnp.minimum(i, 1), 1 - c[0], 0, 0)), *VECTOR_SPECS],
            out_specs=pl.BlockSpec((8, 24, 768), lambda i, c: (i, 0, 0)),
        ),
        out_shape=pltpu.VMEM((17, 24, 768), f32),
        compiler_params=PARAMS,
        name="pick_up",
    )(core, tiles, vector, param)


def pick_down(core, grad, vector, param):
    return pl.pallas_call(
        pick_down_kernel,
        grid_spec=pltpu.PrefetchScalarGridSpec(
            num_scalar_prefetch=1,
            grid=(3,),
            in_specs=[pl.BlockSpec((768, 384), lambda i, c: (0, jnp.minimum(i, 1))), *VECTOR_SPECS],
            out_specs=(
                pl.BlockSpec((8, 24, 768), lambda i, c: (i, 0, 0)),
                pl.BlockSpec((8, 24, 768), lambda i, c: (jnp.minimum(i, 1), 0, 0)),
            ),
        ),
        out_shape=(pltpu.VMEM((17, 24, 768), f32), pltpu.VMEM((16, 24, 768), f32)),
        compiler_params=PARAMS,
        name="pick_down",
    )(core, grad, vector, param)


def vector_rows(t, core, small_ref, vector_ref, param_ref):
    parts = pieces(vector_ref[...] + small_ref[0, 0:1, :])
    mine, theirs = param_ref[...], small_ref[0, 8:9, 0:24]
    pairs = (jnp.where(core == 0, mine, theirs), jnp.where(core == 0, theirs, mine))
    listed = padded(144 * t, jnp.concatenate([p for pair in pairs for p in pieces(pair)], axis=1), 768)
    row = lax.broadcasted_iota(jnp.int32, (8, 768), 0)
    rows = jnp.where(row == 7, listed, 0.0)
    for k in range(3):
        rows = jnp.where(row == 1 + 3 * t + k, parts[k], rows)
    return rows


def encode_up_kernel(core_ref, mine_ref, got_ref, small_ref, vector_ref, param_ref, out_ref, rows_ref):
    y = pl.program_id(0)

    @pl.when(y == 0)
    def _():
        rows = vector_rows(0, core_ref[0], small_ref, vector_ref, param_ref)
        for x in range(4):
            rows_ref[x] = rows

    for x in range(4):
        out_ref[x], top = encode_rows(mine_ref[0, x, 0] + got_ref[x])
        rows_ref[x, 0:1, 0:256] += laid(top, 256, 48 * y)


def encode_down_kernel(core_ref, mine_ref, got_ref, small_ref, vector_ref, param_ref, before_ref, message_ref, out_ref, rows_ref):
    y = pl.program_id(0)

    @pl.when(y == 0)
    def _():
        rows = vector_rows(1, core_ref[0], small_ref, vector_ref, param_ref)
        for x in range(4):
            rows_ref[x] = before_ref[x] + rows

    @pl.when(y < 4)
    def _():
        for x in range(4):
            out_ref[x], top = encode_rows(mine_ref[x] + got_ref[x])
            rows_ref[x, 0:1, 0:256] += laid(top, 256, 48 * y + 24)

    @pl.when(y == 4)
    def _():
        for x in range(4):
            out_ref[x, 0:8] = rows_ref[x].astype(bf16)


SMALL_SPECS = [
    pl.BlockSpec((4, 24, 768), lambda i, c: (jnp.minimum(i, 3), 0, 0)),
    pl.BlockSpec((1, 24, 768), lambda i, c: (16, 0, 0)),
    *VECTOR_SPECS,
]


def encode_up(core, grad, got, vector, param):
    return pl.pallas_call(
        encode_up_kernel,
        grid_spec=pltpu.PrefetchScalarGridSpec(
            num_scalar_prefetch=1,
            grid=(4,),
            in_specs=[pl.BlockSpec((1, 4, 1, 24, 768), lambda i, c: (i, 0, c[0], 0, 0)), *SMALL_SPECS],
            out_specs=(
                pl.BlockSpec((4, 24, 768), lambda i, c: (0, 2 * i, 0)),
                pl.BlockSpec((4, 8, 768), lambda i, c: (0, 0, 0)),
            ),
        ),
        out_shape=(shape(4, 200, 768, dtype=bf16), shape(4, 8, 768)),
        compiler_params=PARAMS,
        name="encode_up",
    )(core, grad.reshape(4, 4, 2, 24, 768), got, got, vector, param)


def encode_down(core, mine, got, vector, param, before, message):
    return pl.pallas_call(
        encode_down_kernel,
        grid_spec=pltpu.PrefetchScalarGridSpec(
            num_scalar_prefetch=1,
            grid=(5,),
            in_specs=[
                pl.BlockSpec((4, 24, 768), lambda i, c: (jnp.minimum(i, 3), 0, 0)),
                *SMALL_SPECS,
                pl.BlockSpec((4, 8, 768), lambda i, c: (0, 0, 0)),
                pl.BlockSpec(memory_space=pl.ANY),
            ],
            out_specs=pl.BlockSpec((4, 24, 768), lambda i, c: (0, jnp.minimum(2 * i + 1, 8), 0)),
            scratch_shapes=[pltpu.VMEM((4, 8, 768), f32)],
        ),
        out_shape=shape(4, 200, 768, dtype=bf16),
        input_output_aliases={7: 0},
        compiler_params=PARAMS,
        name="encode_down",
    )(core, mine, got, got, vector, param, before, message)


def recode_kernel(message_ref, out_ref):
    beside = [message_ref[x, 192:200, :].astype(f32) for x in range(4)]
    total = (beside[0] + beside[1]) + (beside[2] + beside[3])
    row = lax.broadcasted_iota(jnp.int32, (8, 768), 0)
    chips = [b[7:8, 0:288] for b in beside]
    rows = jnp.where(row == 7, padded(0, jnp.concatenate(chips[0:2], axis=1), 768), 0.0)
    rows = jnp.where(row == 0, padded(128, jnp.concatenate(chips[2:4], axis=1), 768), rows)
    for t in range(2):
        parts = pieces(total[1 + 3 * t : 2 + 3 * t] + total[2 + 3 * t : 3 + 3 * t] + total[3 + 3 * t : 4 + 3 * t])
        for k in range(3):
            rows = jnp.where(row == 1 + 3 * t + k, parts[k], rows)
    for y in range(4):
        tops = jnp.zeros((1, 128), f32)
        for t in range(2):
            at = 48 * y + 24 * t
            part = jnp.zeros((24, 768), f32)
            for x in range(4):
                part = part + decode_rows(message_ref[x, at : at + 24, :], stood(beside[x][0:1, 0:256], at))
            out_ref[y, 24 * t : 24 * t + 24, :], top = encode_rows(part)
            tops = tops + laid(top, 128, 24 * t)
        out_ref[y, 48:56, :] = (rows + jnp.where(row == 0, padded(0, tops, 768), 0.0)).astype(bf16)


def decode_kernel(message_ref, up_ref, down_ref, mean_ref, sizes_ref, vector_ref, params_ref):
    lane = lax.broadcasted_iota(jnp.int32, (24, 128), 1)
    beside = [message_ref[y, 48:56, :].astype(f32) for y in range(4)]
    total = (beside[0] + beside[1]) + (beside[2] + beside[3])
    for y in range(4):
        params_ref[y] = beside[y]
    for t, param_ref in enumerate((up_ref, down_ref)):
        rows = slice(24 * t, 24 * t + 24)
        mean = jnp.zeros((24, 768), f32)
        for y in range(4):
            mean = mean + decode_rows(message_ref[y, rows, :], stood(beside[y][0:1, 0:128], 24 * t))
        mean = mean * 32**-0.5
        mean_ref[rows] = mean
        vector_ref[t : t + 1] = total[1 + 3 * t : 2 + 3 * t] + total[2 + 3 * t : 3 + 3 * t] + total[3 + 3 * t : 4 + 3 * t]
        param = param_ref[...]
        own = jnp.sum(param * param, axis=1, keepdims=True)
        size = jnp.sum(mean * mean, axis=1, keepdims=True)
        both = jnp.where(lane < 64, own, size)
        for m in range(4):
            sizes_ref[m, rows] = both


def step_kernel(up_ref, down_ref, mean_ref, sizes_ref, next_up_ref, next_down_ref, copies_ref):
    for t, (param_ref, next_ref) in enumerate(((up_ref, next_up_ref), (down_ref, next_down_ref))):
        rows = slice(24 * t, 24 * t + 24)
        sizes = (sizes_ref[0, rows] + sizes_ref[1, rows]) + (sizes_ref[2, rows] + sizes_ref[3, rows])
        ratio = jnp.sqrt(sizes[:, 0:1]) * lax.rsqrt(sizes[:, 64:65] + 1e-06)
        after = param_ref[...] - learn_rate * (mean_ref[rows] * ratio)
        next_ref[...] = after
        half = after.astype(bf16)
        for y in range(4):
            copies_ref[y, rows] = half


def merge_kernel(core_ref, plane_ref, got_ref, up_ref, down_ref):
    even = core_ref[0] == 0
    columns = []
    for y in range(2):
        for x in range(4):
            mine, other = plane_ref[x, y], got_ref[x, y]
            for c, pair in enumerate((jnp.where(even, mine, other), jnp.where(even, other, mine))):
                up_ref[y, x, c] = pair[0:24]
                columns.append(pair.astype(f32)[24:48])
    down_ref[...] = jnp.concatenate(columns, axis=0).T.astype(bf16)


def merge(core, plane, got):
    up, down = pl.pallas_call(
        merge_kernel,
        grid_spec=pltpu.PrefetchScalarGridSpec(
            num_scalar_prefetch=1,
            grid=(2,),
            in_specs=[pl.BlockSpec((4, 2, 48, 768), lambda i, c: (0, i, 0, 0))] * 2,
            out_specs=(
                pl.BlockSpec((2, 4, 2, 24, 768), lambda i, c: (i, 0, 0, 0, 0)),
                pl.BlockSpec((768, 384), lambda i, c: (0, i)),
            ),
        ),
        out_shape=(shape(4, 4, 2, 24, 768, dtype=bf16), shape(768, 768, dtype=bf16)),
        compiler_params=PARAMS,
        name="merge",
    )(core, plane, got)
    return up.reshape(768, 768), down


def vector_kernel(vectors_ref, params_ref, out_ref):
    for t in range(2):
        listed = []
        for y in range(4):
            for x in range(4):
                row, first = (7, 288 * x) if x < 2 else (0, 128 + 288 * (x - 2))
                for c in range(2):
                    at = first + 144 * t + 72 * c
                    lanes = params_ref[y, row : row + 1, at : at + 72]
                    listed.append(lanes[:, 0:24] + lanes[:, 24:48] + lanes[:, 48:72])
        out_ref[t : t + 1] = jnp.concatenate(listed, axis=1) - learn_rate * (vectors_ref[t : t + 1] * 32**-0.5)


def exchange(a, axis):
    return lax.all_to_all(a, axis, 0, 0, tiled=True)


def on_device(
    slope_up, slope_down, slope_norm, slope_bias, param_up, param_down, param_norm, param_bias
):
    cores = lax.axis_index("core").astype(jnp.int32).reshape(1)
    turned = param_down.T
    norms = (slope_norm, param_norm.reshape(1, 24))
    biases = (slope_bias, param_bias.reshape(1, 24))
    sent_up = pick_up(cores, *in_hbm(slope_up[0].reshape(16, 2, 24, 768), *norms))
    got_up = lax.ppermute(sent_up, "core", SWAP)
    sent_down, mine_down = pick_down(cores, slope_down[0], *biases)
    got_down = lax.ppermute(sent_down, "core", SWAP)
    message, rows = encode_up(cores, slope_up[0], got_up, *norms)
    message = encode_down(cores, mine_down, got_down, *biases, rows, message)
    recoded = call(recode_kernel, shape(4, 56, 768, dtype=bf16), 1)(exchange(message, "x"))
    outs = (shape(48, 768), shape(4, 48, 128), shape(2, 768), shape(4, 8, 768))
    mean, sizes, vectors, params = call(decode_kernel, outs, 3)(exchange(recoded, "y"), param_up, turned)
    outs = (shape(24, 768), shape(24, 768), shape(4, 48, 768, dtype=bf16))
    next_up, next_down, copies = call(step_kernel, outs, 4)(param_up, turned, mean, exchange(sizes, MODEL))
    rows = exchange(copies, "y")
    norm, bias = call(vector_kernel, shape(2, 768), 2)(vectors, params)
    at = 24 * lax.axis_index(("y", "x", "core"))
    plane = exchange(jnp.broadcast_to(rows[None], (4, 4, 48, 768)), "x")
    half_up, half_down = merge(cores, plane, lax.ppermute(plane, "core", SWAP))
    return (
        half_up, half_down, norm.astype(bf16), bias.astype(bf16), next_up, next_down.T,
        lax.dynamic_slice_in_dim(norm, at, 24), lax.dynamic_slice_in_dim(bias, at, 24),
    )


def solution(mesh):
    split = Mesh(
        mesh.devices.reshape(mesh.shape["ens"], 4, 4, 2, 2, 2),
        ("ens", "y", "x", "core", "mz", "my"),
    )
    return jax.shard_map(
        on_device,
        mesh=split,
        in_specs=(
            P(ENS_REPLICA, None, MODEL),
            P(ENS_REPLICA, MODEL, None),
            P(ENS_REPLICA, None),
            P(ENS_REPLICA, None),
            P(ENS_REPLICA, MODEL),
            P(("ens", *MODEL), ("y", "x", "core")),
            P(ENS_REPLICA),
            P(ENS_REPLICA),
        ),
        out_specs=(
            P("ens", MODEL),
            P(("ens", *MODEL), None),
            P("ens"),
            P("ens"),
            P(ENS_REPLICA, MODEL),
            P(("ens", *MODEL), ("y", "x", "core")),
            P(ENS_REPLICA),
            P(ENS_REPLICA),
        ),
        check_vma=False,
    )
```

time: 115 us -> 111 us (0.965)
  local copies, waits for them, and re-layouts: 3.37 us -> 1.32 us
  Pallas kernels: 11.4 us -> 9.81 us
  blocking collectives: 80.1 us -> 78.7 us
  waiting for transfers between devices: 1.16 us -> 2.54 us
    transpose x1 -> x0, local copies, waits for them, and re-layouts: 2.04 us -> none  [on_device(): slope_down[0]]
    pallas_call x5, Pallas kernels: 8.27 us -> 6.5 us  [the longest x1 1.66 us: pick_up(): pl.pallas_call(pick_up_kernel, grid_spec=pltpu.PrefetchScalarGridSpec(num...]
    ppermute x2, waiting for transfers between devices: 0.09 us -> 1.65 us  [the longest x1 1.65 us: on_device(): got_down = lax.ppermute(sent_down, 'core', SWAP)]
    all_to_all x5, blocking collectives: 80.1 us -> 78.7 us  [exchange(): return lax.all_to_all(a, axis, 0, 0, tiled=True)]
  transfers between devices with their start and end apart: 3 -> 3, of which waited for: 2 -> 2; matrix products, arithmetic and copies ran while one was open for 3% -> 1% of each run, Pallas kernels for 3% -> 2%
where the time goes in v5:
time: 111 us
  blocking collectives  78.7 us (71%)
  starting transfers between devices  17.5 us (16%)
  Pallas kernels  9.81 us (9%)
  waiting for transfers between devices  2.54 us (2%)
  local copies, waits for them, and re-layouts  1.32 us (1%)
    all_to_all x5, blocking collectives, exchange(): return lax.all_to_all(a, axis, 0, 0, tiled=True)  78.7 us
    ppermute x1, starting transfers between devices, on_device(): got_up = lax.ppermute(sent_up, 'core', SWAP)  8.88 us
    ppermute x1, starting transfers between devices, on_device(): half_up, half_down = merge(cores, plane, lax.ppermute(plane, 'core', SWAP))  6.72 us
  transfers between devices with their start and end apart: 3, of which 2 were waited for; matrix products, arithmetic and copies ran while one was open for 1% of the time, Pallas kernels for 2%

profile of v5, /device:TPU:1, one launch (start us, length us, event | category | flops | bytes accessed | tf_op | source)
XLA Modules:
  0.0 110.7 jit_solution(16049591631075158123)
XLA Ops:
  0.6 0.0 copy-start.1
  0.6 0.0 copy-start.5
  0.7 0.0 copy-start.7
  0.7 1.7 %pick_up.1 = f32[17,24,768]{2,1,0:T(8,128)S(1)} custom-call(s32[1]{0:T(128)} %bitcast.core_ref, f32[16,2,24,768]{3,2,1,0:T(8,128)} %bitcast.13, f32[1,768]{1,0:T(1,128)} %vector_ref.6, f32[1,24]{1,0:T(1,128)} %bitcast.18), custom_call_target="tpu_custom_call" | custom-call | tf_op jit(solution)/shard_map/pick_up/pallas_call | solution.py:114
  2.3 0.0 copy-start
  2.3 0.0 copy-start.4
  2.4 0.0 copy-start.6
  2.4 8.9 %collective-permute-start.1 = (f32[17,24,768]{2,1,0:T(8,128)S(1)}, f32[17,24,768]{2,1,0:T(8,128)S(1)}, u32[]{:S(2)}, u32[]{:S(2)}) collective-permute-start(f32[17,24,768]{2,1,0:T(8,128)S(1)} %pick_up.1), channel_id=1, source_target_pairs={{0,4},{4,0},{1,5},{5,1},{2,6},{6,2},{3,7},{7,3},{8,12},{12,8},{9,1... | collective-permute-start | bytes 3760136 | tf_op jit(solution)/shard_map/ppermute | solution.py:353
  11.3 0.0 copy-done.1
  11.3 0.0 copy-done.5
  11.3 0.0 copy-done.7
  11.3 1.2 %pick_down.1 = (f32[17,24,768]{2,1,0:T(8,128)S(1)}, f32[16,24,768]{2,1,0:T(8,128)S(1)}) custom-call(s32[1]{0:T(128)} %bitcast.core_ref, f32[768,768]{1,0:T(8,128)S(1)} %bitcast.15, f32[1,768]{1,0:T(1,128)S(1)} %copy-done.5, f32[1,24]{1,0:T(1,128)S(1)} %bitcast.20), custom_call_target="tpu_custom_call" | custom-call | tf_op jit(solution)/shard_map/pick_down/pallas_call | solution.py:129
  12.5 1.9 %collective-permute-start = (f32[17,24,768]{2,1,0:T(8,128)S(1)}, f32[17,24,768]{2,1,0:T(8,128)S(1)}, u32[]{:S(2)}, u32[]{:S(2)}) collective-permute-start(f32[17,24,768]{2,1,0:T(8,128)S(1)} %get-tuple-element.22), channel_id=1, source_target_pairs={{0,4},{4,0},{1,5},{5,1},{2,6},{6,2},{3,7},{7,3},{8,12},{12,8},{9,1... | collective-permute-start | bytes 3760136 | tf_op jit(solution)/shard_map/ppermute | solution.py:355
  14.4 0.0 collective-permute-done.1.got_ref.small_ref
  14.4 0.0 copy-done
  14.4 0.0 copy-done.4
  14.4 0.0 copy-done.6
  14.4 1.2 %encode_up.1 = (bf16[4,200,768]{2,1,0:T(8,128)(2,1)S(1)}, f32[4,8,768]{2,1,0:T(8,128)S(1)}) custom-call(s32[1]{0:T(128)} %bitcast.core_ref, f32[4,4,2,24,768]{4,3,2,1,0:T(8,128)S(1)} %bitcast.14, f32[17,24,768]{2,1,0:T(8,128)S(1)} %collective-permute-done.1.got_ref.small_ref, f32[17,24,768]{2,1,0:T(8,128)S(1)} %collective-permute-done.1.got_ref.small_ref, ...), custom_call_target="tpu_custom_call" | custom-call | tf_op jit(solution)/shard_map/encode_up/pallas_call | solution.py:201
  15.7 1.6 %collective-permute-done.got_ref.small_ref = f32[17,24,768]{2,1,0:T(8,128)S(1)} collective-permute-done((f32[17,24,768]{2,1,0:T(8,128)S(1)}, f32[17,24,768]{2,1,0:T(8,128)S(1)}, u32[]{:S(2)}, u32[]{:S(2)}) %collective-permute-start) | collective-permute-done | bytes 1253408 | tf_op jit(solution)/shard_map/ppermute | solution.py:355
  17.3 1.2 %encode_down.1 = bf16[4,200,768]{2,1,0:T(8,128)(2,1)S(1)} custom-call(s32[1]{0:T(128)} %bitcast.core_ref, f32[16,24,768]{2,1,0:T(8,128)S(1)} %get-tuple-element.21.mine_ref, f32[17,24,768]{2,1,0:T(8,128)S(1)} %collective-permute-done.got_ref.small_ref, f32[17,24,768]{2,1,0:T(8,128)S(1)} %collective-permute-done.got_ref.small_ref, ...), custom_call_target="tpu_custom_call", output_to_operand_aliasing={{}: (7, {})} | custom-call | tf_op jit(solution)/shard_map/encode_down/pallas_call | solution.py:219
  18.6 19.4 %all_to_all.25.message_ref = bf16[4,200,768]{2,1,0:T(8,128)(2,1)S(1)} all-to-all(bf16[4,200,768]{2,1,0:T(8,128)(2,1)S(1)} %encode_down.1), channel_id=1, replica_groups=mesh['ens'=4,'y'=4,'x'=4,'core'=2,'mz'=2,'my'=2] {'x'}, dimensions={0} | all-to-all | bytes 2457600 | tf_op jit(solution)/shard_map/all_to_all | solution.py:342
  38.0 0.0 copy-start.2
  38.0 0.0 copy-start.3
  38.0 1.2 %shard_map.143 = bf16[4,56,768]{2,1,0:T(8,128)(2,1)S(1)} custom-call(bf16[4,200,768]{2,1,0:T(8,128)(2,1)S(1)} %all_to_all.25.message_ref), custom_call_target="tpu_custom_call" | custom-call | tf_op jit(solution)/shard_map/pallas_call | solution.py:358
  39.2 12.2 %all_to_all.26.message_ref = bf16[4,56,768]{2,1,0:T(8,128)(2,1)S(1)} all-to-all(bf16[4,56,768]{2,1,0:T(8,128)(2,1)S(1)} %shard_map.143), channel_id=1, replica_groups=mesh['ens'=4,'y'=4,'x'=4,'core'=2,'mz'=2,'my'=2] {'y'}, dimensions={0} | all-to-all | bytes 688128 | tf_op jit(solution)/shard_map/all_to_all | solution.py:342
  51.4 0.0 copy-done.2
  51.4 0.0 copy-done.3
  51.4 0.3 shard_map.144
  51.7 21.8 %all_to_all.27.sizes_ref = f32[4,48,128]{2,1,0:T(8,128)S(1)} all-to-all(f32[4,48,128]{2,1,0:T(8,128)S(1)} %get-tuple-element.26), channel_id=1, replica_groups=mesh['ens'=4,'y'=4,'x'=4,'core'=2,'mz'=2,'my'=2] {'mz','my'}, dimensions={0} | all-to-all | bytes 196608 | tf_op jit(solution)/shard_map/all_to_all | solution.py:342
  73.6 0.8 shard_map.145
  74.4 10.2 %all_to_all.28 = bf16[4,48,768]{2,1,0:T(8,128)(2,1)S(1)} all-to-all(bf16[4,48,768]{2,1,0:T(8,128)(2,1)S(1)} %get-tuple-element.27), channel_id=1, replica_groups=mesh['ens'=4,'y'=4,'x'=4,'core'=2,'mz'=2,'my'=2] {'y'}, dimensions={0} | all-to-all | bytes 589824 | tf_op jit(solution)/shard_map/all_to_all | solution.py:342
  84.6 0.1 broadcast_in_dim.2
  84.7 15.1 %all_to_all.29.plane_ref = bf16[4,4,48,768]{3,2,1,0:T(8,128)(2,1)S(1)} all-to-all(bf16[4,4,48,768]{3,2,1,0:T(8,128)(2,1)S(1)} %broadcast_in_dim.2), channel_id=1, replica_groups=mesh['ens'=4,'y'=4,'x'=4,'core'=2,'mz'=2,'my'=2] {'x'}, dimensions={0} | all-to-all | bytes 2359296 | tf_op jit(solution)/shard_map/all_to_all | solution.py:342
  99.7 6.7 %collective-permute-start.2 = (bf16[4,4,48,768]{3,2,1,0:T(8,128)(2,1)S(1)}, bf16[4,4,48,768]{3,2,1,0:T(8,128)(2,1)S(1)}, u32[]{:S(2)}, u32[]{:S(2)}) collective-permute-start(bf16[4,4,48,768]{3,2,1,0:T(8,128)(2,1)S(1)} %all_to_all.29.plane_ref), channel_id=1, source_target_pairs={{0,4},{4,0},{1,5},{5,1},{2,6},{6,2},{3,7},{7,3},{8,12},{12,8},{9,1... | collective-permute-start | bytes 3538952 | tf_op jit(solution)/shard_map/ppermute | solution.py:367
  106.4 0.3 shard_map.146
  106.8 0.6 dynamic-slice_bitcast_fusion
  107.4 0.6 convert_reduce_fusion
  108.0 0.9 collective-permute-done.2.got_ref
  108.9 1.8 %merge.1 = (bf16[4,4,2,24,768]{4,3,2,1,0:T(8,128)(2,1)}, bf16[768,768]{1,0:T(8,128)(2,1)}) custom-call(s32[1]{0:T(128)} %bitcast.core_ref, bf16[4,4,48,768]{3,2,1,0:T(8,128)(2,1)S(1)} %all_to_all.29.plane_ref, bf16[4,4,48,768]{3,2,1,0:T(8,128)(2,1)S(1)} %collective-permute-done.2.got_ref), custom_call_target="tpu_custom_call" | custom-call | tf_op jit(solution)/shard_map/merge/pallas_call | solution.py:310
  (1 shorter events, 0.0 us)
Async XLA Ops:
  0.6 10.6 %copy-start.1 = (f32[1,768,768]{2,1,0:T(8,128)S(1)}, f32[1,768,768]{2,1,0:T(8,128)}, u32[]{:S(2)}) copy-start(f32[1,768,768]{2,1,0:T(8,128)} %param.9) | copy-start | bytes 7077892
  0.6 10.6 %copy-start.5 = (f32[1,768]{1,0:T(1,128)S(1)}, f32[1,768]{1,0:T(1,128)}, u32[]{:S(2)}) copy-start(f32[1,768]{1,0:T(1,128)} %vector_ref.7) | copy-start | bytes 9220
  0.7 10.6 %copy-start.7 = (f32[24]{0:T(128)S(1)}, f32[24]{0:T(128)}, u32[]{:S(2)}) copy-start(f32[24]{0:T(128)} %param.15) | copy-start | bytes 292
  2.3 12.1 %copy-start = (f32[1,768,768]{2,1,0:T(8,128)S(1)}, f32[1,768,768]{2,1,0:T(8,128)}, u32[]{:S(2)}) copy-start(f32[1,768,768]{2,1,0:T(8,128)} %param.8) | copy-start | bytes 7077892
  2.3 12.1 %copy-start.4 = (f32[1,768]{1,0:T(1,128)S(1)}, f32[1,768]{1,0:T(1,128)}, u32[]{:S(2)}) copy-start(f32[1,768]{1,0:T(1,128)} %vector_ref.6) | copy-start | bytes 9220
  2.4 12.1 %copy-start.6 = (f32[24]{0:T(128)S(1)}, f32[24]{0:T(128)}, u32[]{:S(2)}) copy-start(f32[24]{0:T(128)} %param.14) | copy-start | bytes 292
  2.4 12.0 %collective-permute-start.1 = (f32[17,24,768]{2,1,0:T(8,128)S(1)}, f32[17,24,768]{2,1,0:T(8,128)S(1)}, u32[]{:S(2)}, u32[]{:S(2)}) collective-permute-start(f32[17,24,768]{2,1,0:T(8,128)S(1)} %pick_up.1), channel_id=1, source_target_pairs={{0,4},{4,0},{1,5},{5,1},{2,6},{6,2},{3,7},{7,3},{8,12},{12,8},{9,1... | collective-permute-start | bytes 3760136 | tf_op jit(solution)/shard_map/ppermute | solution.py:353
  12.5 4.8 %collective-permute-start = (f32[17,24,768]{2,1,0:T(8,128)S(1)}, f32[17,24,768]{2,1,0:T(8,128)S(1)}, u32[]{:S(2)}, u32[]{:S(2)}) collective-permute-start(f32[17,24,768]{2,1,0:T(8,128)S(1)} %get-tuple-element.22), channel_id=1, source_target_pairs={{0,4},{4,0},{1,5},{5,1},{2,6},{6,2},{3,7},{7,3},{8,12},{12,8},{9,1... | collective-permute-start | bytes 3760136 | tf_op jit(solution)/shard_map/ppermute | solution.py:355
  38.0 13.4 %copy-start.2 = (f32[24,768]{1,0:T(8,128)S(1)}, f32[24,768]{1,0:T(8,128)}, u32[]{:S(2)}) copy-start(f32[24,768]{1,0:T(8,128)} %up_ref.3) | copy-start | bytes 221188
  38.0 13.4 %copy-start.3 = (f32[768,24]{0,1:T(8,128)S(1)}, f32[768,24]{0,1:T(8,128)}, u32[]{:S(2)}) copy-start(f32[768,24]{0,1:T(8,128)} %param.13) | copy-start | bytes 221188
  99.7 9.2 %collective-permute-start.2 = (bf16[4,4,48,768]{3,2,1,0:T(8,128)(2,1)S(1)}, bf16[4,4,48,768]{3,2,1,0:T(8,128)(2,1)S(1)}, u32[]{:S(2)}, u32[]{:S(2)}) collective-permute-start(bf16[4,4,48,768]{3,2,1,0:T(8,128)(2,1)S(1)} %all_to_all.29.plane_ref), channel_id=1, source_target_pairs={{0,4},{4,0},{1,5},{5,1},{2,6},{6,2},{3,7},{7,3},{8,12},{12,8},{9,1... | collective-permute-start | bytes 3538952 | tf_op jit(solution)/shard_map/ppermute | solution.py:367

commit v6 on v5

--- a/solution.py
+++ b/solution.py
@@ -6,7 +6,8 @@
 from jax.sharding import Mesh
 from jax.sharding import PartitionSpec as P
 
-ENS_REPLICA = ("ens", "y", "x", "core")
+REPLICA = ("ya", "yb", "x", "core")
+ENS_REPLICA = ("ens", *REPLICA)
 MODEL = ("mz", "my")
 SWAP = [(0, 1), (1, 0)]
 
@@ -161,12 +162,12 @@
     @pl.when(y == 0)
     def _():
         rows = vector_rows(0, core_ref[0], small_ref, vector_ref, param_ref)
-        for x in range(4):
-            rows_ref[x] = rows
+        for d in range(8):
+            rows_ref[d] = rows
 
     for x in range(4):
         out_ref[x], top = encode_rows(mine_ref[0, x, 0] + got_ref[x])
-        rows_ref[x, 0:1, 0:256] += laid(top, 256, 48 * y)
+        rows_ref[4 * (y % 2) + x, 0:1, 0:128] += laid(top, 128, 48 * (y // 2))
 
 
 def encode_down_kernel(core_ref, mine_ref, got_ref, small_ref, vector_ref, param_ref, before_ref, message_ref, out_ref, rows_ref):
@@ -175,19 +176,19 @@
     @pl.when(y == 0)
     def _():
         rows = vector_rows(1, core_ref[0], small_ref, vector_ref, param_ref)
-        for x in range(4):
-            rows_ref[x] = before_ref[x] + rows
+        for d in range(8):
+            rows_ref[d] = before_ref[d] + rows
 
     @pl.when(y < 4)
     def _():
         for x in range(4):
             out_ref[x], top = encode_rows(mine_ref[x] + got_ref[x])
-            rows_ref[x, 0:1, 0:256] += laid(top, 256, 48 * y + 24)
-
-    @pl.when(y == 4)
+            rows_ref[4 * (y % 2) + x, 0:1, 0:128] += laid(top, 128, 48 * (y // 2) + 24)
+
+    @pl.when(y >= 4)
     def _():
         for x in range(4):
-            out_ref[x, 0:8] = rows_ref[x].astype(bf16)
+            out_ref[x, 0:8] = rows_ref[4 * (y - 4) + x].astype(bf16)
 
 
 SMALL_SPECS = [
@@ -205,11 +206,11 @@
             grid=(4,),
             in_specs=[pl.BlockSpec((1, 4, 1, 24, 768), lambda i, c: (i, 0, c[0], 0, 0)), *SMALL_SPECS],
             out_specs=(
-                pl.BlockSpec((4, 24, 768), lambda i, c: (0, 2 * i, 0)),
-                pl.BlockSpec((4, 8, 768), lambda i, c: (0, 0, 0)),
+                pl.BlockSpec((4, 24, 768), lambda i, c: (i % 2, 2 * (i // 2), 0)),
+                pl.BlockSpec((8, 8, 768), lambda i, c: (0, 0, 0)),
             ),
         ),
-        out_shape=(shape(4, 200, 768, dtype=bf16), shape(4, 8, 768)),
+        out_shape=(shape(8, 104, 768, dtype=bf16), shape(8, 8, 768)),
         compiler_params=PARAMS,
         name="encode_up",
     )(core, grad.reshape(4, 4, 2, 24, 768), got, got, vector, param)
@@ -220,58 +221,62 @@
         encode_down_kernel,
         grid_spec=pltpu.PrefetchScalarGridSpec(
             num_scalar_prefetch=1,
-            grid=(5,),
+            grid=(6,),
             in_specs=[
                 pl.BlockSpec((4, 24, 768), lambda i, c: (jnp.minimum(i, 3), 0, 0)),
                 *SMALL_SPECS,
-                pl.BlockSpec((4, 8, 768), lambda i, c: (0, 0, 0)),
+                pl.BlockSpec((8, 8, 768), lambda i, c: (0, 0, 0)),
                 pl.BlockSpec(memory_space=pl.ANY),
             ],
-            out_specs=pl.BlockSpec((4, 24, 768), lambda i, c: (0, jnp.minimum(2 * i + 1, 8), 0)),
-            scratch_shapes=[pltpu.VMEM((4, 8, 768), f32)],
-        ),
-        out_shape=shape(4, 200, 768, dtype=bf16),
+            out_specs=pl.BlockSpec((4, 24, 768), lambda i, c: (i % 2, jnp.where(i < 4, 2 * (i // 2) + 1, 4), 0)),
+            scratch_shapes=[pltpu.VMEM((8, 8, 768), f32)],
+        ),
+        out_shape=shape(8, 104, 768, dtype=bf16),
         input_output_aliases={7: 0},
         compiler_params=PARAMS,
         name="encode_down",
     )(core, mine, got, got, vector, param, before, message)
 
 
-def recode_kernel(message_ref, out_ref):
-    beside = [message_ref[x, 192:200, :].astype(f32) for x in range(4)]
-    total = (beside[0] + beside[1]) + (beside[2] + beside[3])
-    row = lax.broadcasted_iota(jnp.int32, (8, 768), 0)
-    chips = [b[7:8, 0:288] for b in beside]
-    rows = jnp.where(row == 7, padded(0, jnp.concatenate(chips[0:2], axis=1), 768), 0.0)
-    rows = jnp.where(row == 0, padded(128, jnp.concatenate(chips[2:4], axis=1), 768), rows)
+def recode_kernel(message_ref, kept_ref, rows_ref, out_ref):
+    near = lax.axis_index("ya") == 0
+    beside = [message_ref[d, 96:104, :].astype(f32) for d in range(8)]
+    total = ((beside[0] + beside[1]) + (beside[2] + beside[3])) + ((beside[4] + beside[5]) + (beside[6] + beside[7]))
+    row = lax.broadcasted_iota(jnp.int32, (16, 768), 0)
+    rows = jnp.zeros((16, 768), f32)
+    for k in range(4):
+        pair = jnp.concatenate([beside[2 * k][7:8, 0:288], beside[2 * k + 1][7:8, 0:288]], axis=1)
+        rows = jnp.where(row == 8 + k, padded(0, pair, 768), rows)
     for t in range(2):
         parts = pieces(total[1 + 3 * t : 2 + 3 * t] + total[2 + 3 * t : 3 + 3 * t] + total[3 + 3 * t : 4 + 3 * t])
         for k in range(3):
             rows = jnp.where(row == 1 + 3 * t + k, parts[k], rows)
-    for y in range(4):
-        tops = jnp.zeros((1, 128), f32)
-        for t in range(2):
-            at = 48 * y + 24 * t
+    rows_ref[...] = rows
+    tops = jnp.zeros((1, 128), f32)
+    for t in range(2):
+        sums = []
+        for at in (24 * t, 48 + 24 * t):
             part = jnp.zeros((24, 768), f32)
-            for x in range(4):
-                part = part + decode_rows(message_ref[x, at : at + 24, :], stood(beside[x][0:1, 0:256], at))
-            out_ref[y, 24 * t : 24 * t + 24, :], top = encode_rows(part)
-            tops = tops + laid(top, 128, 24 * t)
-        out_ref[y, 48:56, :] = (rows + jnp.where(row == 0, padded(0, tops, 768), 0.0)).astype(bf16)
-
-
-def decode_kernel(message_ref, up_ref, down_ref, mean_ref, sizes_ref, vector_ref, params_ref):
+            for d in range(8):
+                part = part + decode_rows(message_ref[d, at : at + 24, :], stood(beside[d][0:1, 0:128], at))
+            sums.append(part)
+        kept_ref[24 * t : 24 * t + 24] = jnp.where(near, sums[0], sums[1])
+        out_ref[24 * t : 24 * t + 24, :], top = encode_rows(jnp.where(near, sums[1], sums[0]))
+        tops = tops + laid(top, 128, 24 * t)
+    out_ref[48:64, :] = (rows + jnp.where(row == 0, padded(0, tops, 768), 0.0)).astype(bf16)
+
+
+def decode_kernel(kept_ref, rows_ref, message_ref, up_ref, down_ref, mean_ref, sizes_ref, vector_ref, params_ref):
+    near = lax.axis_index("ya") == 0
     lane = lax.broadcasted_iota(jnp.int32, (24, 128), 1)
-    beside = [message_ref[y, 48:56, :].astype(f32) for y in range(4)]
-    total = (beside[0] + beside[1]) + (beside[2] + beside[3])
-    for y in range(4):
-        params_ref[y] = beside[y]
+    here = rows_ref[...]
+    there = message_ref[48:64, :].astype(f32)
+    total = here + there
+    params_ref[0] = jnp.where(near, here, there)[8:16]
+    params_ref[1] = jnp.where(near, there, here)[8:16]
     for t, param_ref in enumerate((up_ref, down_ref)):
         rows = slice(24 * t, 24 * t + 24)
-        mean = jnp.zeros((24, 768), f32)
-        for y in range(4):
-            mean = mean + decode_rows(message_ref[y, rows, :], stood(beside[y][0:1, 0:128], 24 * t))
-        mean = mean * 32**-0.5
+        mean = (kept_ref[rows] + decode_rows(message_ref[rows, :], stood(there[0:1, 0:128], 24 * t))) * 32**-0.5
         mean_ref[rows] = mean
         vector_ref[t : t + 1] = total[1 + 3 * t : 2 + 3 * t] + total[2 + 3 * t : 3 + 3 * t] + total[3 + 3 * t : 4 + 3 * t]
         param = param_ref[...]
@@ -330,10 +335,10 @@
         listed = []
         for y in range(4):
             for x in range(4):
-                row, first = (7, 288 * x) if x < 2 else (0, 128 + 288 * (x - 2))
+                row, first = 2 * (y % 2) + x // 2, 288 * (x % 2)
                 for c in range(2):
                     at = first + 144 * t + 72 * c
-                    lanes = params_ref[y, row : row + 1, at : at + 72]
+                    lanes = params_ref[y // 2, row : row + 1, at : at + 72]
                     listed.append(lanes[:, 0:24] + lanes[:, 24:48] + lanes[:, 48:72])
         out_ref[t : t + 1] = jnp.concatenate(listed, axis=1) - learn_rate * (vectors_ref[t : t + 1] * 32**-0.5)
 
@@ -355,14 +360,16 @@
     got_down = lax.ppermute(sent_down, "core", SWAP)
     message, rows = encode_up(cores, slope_up[0], got_up, *norms)
     message = encode_down(cores, mine_down, got_down, *biases, rows, message)
-    recoded = call(recode_kernel, shape(4, 56, 768, dtype=bf16), 1)(exchange(message, "x"))
-    outs = (shape(48, 768), shape(4, 48, 128), shape(2, 768), shape(4, 8, 768))
-    mean, sizes, vectors, params = call(decode_kernel, outs, 3)(exchange(recoded, "y"), param_up, turned)
+    outs = (shape(48, 768), shape(16, 768), shape(64, 768, dtype=bf16))
+    kept, rows, recoded = call(recode_kernel, outs, 1)(exchange(message, ("yb", "x")))
+    across = lax.ppermute(recoded, "ya", SWAP)
+    outs = (shape(48, 768), shape(4, 48, 128), shape(2, 768), shape(2, 8, 768))
+    mean, sizes, vectors, params = call(decode_kernel, outs, 5)(kept, rows, across, param_up, turned)
     outs = (shape(24, 768), shape(24, 768), shape(4, 48, 768, dtype=bf16))
     next_up, next_down, copies = call(step_kernel, outs, 4)(param_up, turned, mean, exchange(sizes, MODEL))
-    rows = exchange(copies, "y")
+    rows = exchange(copies, ("ya", "yb"))
     norm, bias = call(vector_kernel, shape(2, 768), 2)(vectors, params)
-    at = 24 * lax.axis_index(("y", "x", "core"))
+    at = 24 * lax.axis_index(REPLICA)
     plane = exchange(jnp.broadcast_to(rows[None], (4, 4, 48, 768)), "x")
     half_up, half_down = merge(cores, plane, lax.ppermute(plane, "core", SWAP))
     return (
@@ -373,8 +380,8 @@
 
 def solution(mesh):
     split = Mesh(
-        mesh.devices.reshape(mesh.shape["ens"], 4, 4, 2, 2, 2),
-        ("ens", "y", "x", "core", "mz", "my"),
+        mesh.devices.reshape(mesh.shape["ens"], 2, 2, 4, 2, 2, 2),
+        ("ens", *REPLICA, "mz", "my"),
     )
     return jax.shard_map(
         on_device,
@@ -385,7 +392,7 @@
             P(ENS_REPLICA, None),
             P(ENS_REPLICA, None),
             P(ENS_REPLICA, MODEL),
-            P(("ens", *MODEL), ("y", "x", "core")),
+            P(("ens", *MODEL), REPLICA),
             P(ENS_REPLICA),
             P(ENS_REPLICA),
         ),
@@ -395,7 +402,7 @@
             P("ens"),
             P("ens"),
             P(ENS_REPLICA, MODEL),
-            P(("ens", *MODEL), ("y", "x", "core")),
+            P(("ens", *MODEL), REPLICA),
             P(ENS_REPLICA),
             P(ENS_REPLICA),
         ),

time: 111 us -> 108 us (0.973)
  blocking collectives: 78.7 us -> 68.2 us
  waiting for transfers between devices: 2.54 us -> 7.88 us
  starting transfers between devices: 17.5 us -> 20 us
    all_to_all x5 -> x4, blocking collectives: 78.7 us -> 68.2 us  [exchange(): return lax.all_to_all(a, axis, 0, 0, tiled=True)]
    ppermute x0 -> x1, waiting for transfers between devices: none -> 5.38 us  [on_device(): across = lax.ppermute(recoded, 'ya', SWAP)]
    ppermute x0 -> x1, starting transfers between devices: none -> 1.92 us  [on_device(): across = lax.ppermute(recoded, 'ya', SWAP)]
  transfers between devices with their start and end apart: 3 -> 4, of which waited for: 2 -> 3; matrix products, arithmetic and copies ran while one was open for 1% -> 1% of each run, Pallas kernels for 2% -> 3%
where the time goes in v6:
time: 108 us
  blocking collectives  68.2 us (63%)
  starting transfers between devices  20 us (19%)
  Pallas kernels  9.71 us (9%)
  waiting for transfers between devices  7.88 us (7%)
  local copies, waits for them, and re-layouts  1.32 us (1%)
    all_to_all x4, blocking collectives, exchange(): return lax.all_to_all(a, axis, 0, 0, tiled=True)  68.2 us
    ppermute x1, starting transfers between devices, on_device(): got_up = lax.ppermute(sent_up, 'core', SWAP)  8.88 us
    ppermute x1, starting transfers between devices, on_device(): half_up, half_down = merge(cores, plane, lax.ppermute(plane, 'core', SWAP))  7.26 us
    ppermute x1, waiting for transfers between devices, on_device(): across = lax.ppermute(recoded, 'ya', SWAP)  5.38 us
  transfers between devices with their start and end apart: 4, of which 3 were waited for; matrix products, arithmetic and copies ran while one was open for 1% of the time, Pallas kernels for 3%

profile of v6, /device:TPU:1, one launch (start us, length us, event | category | flops | bytes accessed | tf_op | source)
XLA Modules:
  0.0 108.0 jit_solution(5151647339173837252)
XLA Ops:
  0.6 0.0 copy-start.1
  0.6 0.0 copy-start.5
  0.7 0.0 copy-start.7
  0.7 1.7 %pick_up.1 = f32[17,24,768]{2,1,0:T(8,128)S(1)} custom-call(s32[1]{0:T(128)} %bitcast.core_ref, f32[16,2,24,768]{3,2,1,0:T(8,128)} %bitcast.13, f32[1,768]{1,0:T(1,128)} %vector_ref.6, f32[1,24]{1,0:T(1,128)} %bitcast.18), custom_call_target="tpu_custom_call" | custom-call | tf_op jit(solution)/shard_map/pick_up/pallas_call | solution.py:115
  2.3 0.0 copy-start
  2.3 0.0 copy-start.4
  2.4 0.0 copy-start.6
  2.4 8.9 %collective-permute-start.1 = (f32[17,24,768]{2,1,0:T(8,128)S(1)}, f32[17,24,768]{2,1,0:T(8,128)S(1)}, u32[]{:S(2)}, u32[]{:S(2)}) collective-permute-start(f32[17,24,768]{2,1,0:T(8,128)S(1)} %pick_up.1), channel_id=1, source_target_pairs={{0,4},{4,0},{1,5},{5,1},{2,6},{6,2},{3,7},{7,3},{8,12},{12,8},{9,1... | collective-permute-start | bytes 3760136 | tf_op jit(solution)/shard_map/ppermute | solution.py:358
  11.3 0.0 copy-done.1
  11.3 0.0 copy-done.5
  11.3 0.0 copy-done.7
  11.3 1.2 %pick_down.1 = (f32[17,24,768]{2,1,0:T(8,128)S(1)}, f32[16,24,768]{2,1,0:T(8,128)S(1)}) custom-call(s32[1]{0:T(128)} %bitcast.core_ref, f32[768,768]{1,0:T(8,128)S(1)} %bitcast.15, f32[1,768]{1,0:T(1,128)S(1)} %copy-done.5, f32[1,24]{1,0:T(1,128)S(1)} %bitcast.20), custom_call_target="tpu_custom_call" | custom-call | tf_op jit(solution)/shard_map/pick_down/pallas_call | solution.py:130
  12.5 1.9 %collective-permute-start = (f32[17,24,768]{2,1,0:T(8,128)S(1)}, f32[17,24,768]{2,1,0:T(8,128)S(1)}, u32[]{:S(2)}, u32[]{:S(2)}) collective-permute-start(f32[17,24,768]{2,1,0:T(8,128)S(1)} %get-tuple-element.25), channel_id=1, source_target_pairs={{0,4},{4,0},{1,5},{5,1},{2,6},{6,2},{3,7},{7,3},{8,12},{12,8},{9,1... | collective-permute-start | bytes 3760136 | tf_op jit(solution)/shard_map/ppermute | solution.py:360
  14.4 0.0 collective-permute-done.1.got_ref.small_ref
  14.4 0.0 copy-done
  14.4 0.0 copy-done.4
  14.4 0.0 copy-done.6
  14.4 1.3 %encode_up.1 = (bf16[8,104,768]{2,1,0:T(8,128)(2,1)S(1)}, f32[8,8,768]{2,1,0:T(8,128)S(1)}) custom-call(s32[1]{0:T(128)} %bitcast.core_ref, f32[4,4,2,24,768]{4,3,2,1,0:T(8,128)S(1)} %bitcast.14, f32[17,24,768]{2,1,0:T(8,128)S(1)} %collective-permute-done.1.got_ref.small_ref, f32[17,24,768]{2,1,0:T(8,128)S(1)} %collective-permute-done.1.got_ref.small_ref, ...), custom_call_target="tpu_custom_call" | custom-call | tf_op jit(solution)/shard_map/encode_up/pallas_call | solution.py:202
  15.7 1.6 %collective-permute-done.got_ref.small_ref = f32[17,24,768]{2,1,0:T(8,128)S(1)} collective-permute-done((f32[17,24,768]{2,1,0:T(8,128)S(1)}, f32[17,24,768]{2,1,0:T(8,128)S(1)}, u32[]{:S(2)}, u32[]{:S(2)}) %collective-permute-start) | collective-permute-done | bytes 1253408 | tf_op jit(solution)/shard_map/ppermute | solution.py:360
  17.3 1.4 %encode_down.1 = bf16[8,104,768]{2,1,0:T(8,128)(2,1)S(1)} custom-call(s32[1]{0:T(128)} %bitcast.core_ref, f32[16,24,768]{2,1,0:T(8,128)S(1)} %get-tuple-element.24.mine_ref, f32[17,24,768]{2,1,0:T(8,128)S(1)} %collective-permute-done.got_ref.small_ref, f32[17,24,768]{2,1,0:T(8,128)S(1)} %collective-permute-done.got_ref.small_ref, ...), custom_call_target="tpu_custom_call", output_to_operand_aliasing={{}: (7, {})} | custom-call | tf_op jit(solution)/shard_map/encode_down/pallas_call | solution.py:220
  18.7 19.6 %all_to_all.20.message_ref = bf16[8,104,768]{2,1,0:T(8,128)(2,1)S(1)} all-to-all(bf16[8,104,768]{2,1,0:T(8,128)(2,1)S(1)} %encode_down.1), channel_id=1, replica_groups=mesh['ens'=4,'ya'=2,'yb'=2,'x'=4,'core'=2,'mz'=2,'my'=2] {'yb','x'}, dimensions={0} | all-to-all | bytes 2555904 | tf_op jit(solution)/shard_map/all_to_all | solution.py:347
  38.3 0.0 copy-start.2
  38.3 0.0 copy-start.3
  38.3 1.1 shard_map.143
  39.4 1.9 %collective-permute-start.2 = (bf16[64,768]{1,0:T(8,128)(2,1)S(1)}, bf16[64,768]{1,0:T(8,128)(2,1)S(1)}, u32[]{:S(2)}, u32[]{:S(2)}) collective-permute-start(bf16[64,768]{1,0:T(8,128)(2,1)S(1)} %get-tuple-element.30), channel_id=1, source_target_pairs={{0,64},{64,0},{1,65},{65,1},{2,66},{66,2},{3,67},{67,3},{4,68},{68... | collective-permute-start | bytes 294920 | tf_op jit(solution)/shard_map/ppermute | solution.py:365
  41.3 5.4 %collective-permute-done.2.message_ref = bf16[64,768]{1,0:T(8,128)(2,1)S(1)} collective-permute-done((bf16[64,768]{1,0:T(8,128)(2,1)S(1)}, bf16[64,768]{1,0:T(8,128)(2,1)S(1)}, u32[]{:S(2)}, u32[]{:S(2)}) %collective-permute-start.2) | collective-permute-done | bytes 98336 | tf_op jit(solution)/shard_map/ppermute | solution.py:365
  46.7 0.0 copy-done.2
  46.7 0.0 copy-done.3
  46.7 0.2 shard_map.144
  46.9 22.8 %all_to_all.21.sizes_ref = f32[4,48,128]{2,1,0:T(8,128)S(1)} all-to-all(f32[4,48,128]{2,1,0:T(8,128)S(1)} %get-tuple-element.32), channel_id=1, replica_groups=mesh['ens'=4,'ya'=2,'yb'=2,'x'=4,'core'=2,'mz'=2,'my'=2] {'mz','my'}, dimensions={0} | all-to-all | bytes 196608 | tf_op jit(solution)/shard_map/all_to_all | solution.py:347
  69.7 0.8 shard_map.145
  70.6 9.0 %all_to_all.22 = bf16[4,48,768]{2,1,0:T(8,128)(2,1)S(1)} all-to-all(bf16[4,48,768]{2,1,0:T(8,128)(2,1)S(1)} %get-tuple-element.33), channel_id=1, replica_groups=mesh['ens'=4,'ya'=2,'yb'=2,'x'=4,'core'=2,'mz'=2,'my'=2] {'ya','yb'}, dimensions={0} | all-to-all | bytes 589824 | tf_op jit(solution)/shard_map/all_to_all | solution.py:347
  79.5 0.1 broadcast_in_dim.2
  79.6 16.8 %all_to_all.23.plane_ref = bf16[4,4,48,768]{3,2,1,0:T(8,128)(2,1)S(1)} all-to-all(bf16[4,4,48,768]{3,2,1,0:T(8,128)(2,1)S(1)} %broadcast_in_dim.2), channel_id=1, replica_groups=mesh['ens'=4,'ya'=2,'yb'=2,'x'=4,'core'=2,'mz'=2,'my'=2] {'x'}, dimensions={0} | all-to-all | bytes 2359296 | tf_op jit(solution)/shard_map/all_to_all | solution.py:347
  96.4 7.3 %collective-permute-start.3 = (bf16[4,4,48,768]{3,2,1,0:T(8,128)(2,1)S(1)}, bf16[4,4,48,768]{3,2,1,0:T(8,128)(2,1)S(1)}, u32[]{:S(2)}, u32[]{:S(2)}) collective-permute-start(bf16[4,4,48,768]{3,2,1,0:T(8,128)(2,1)S(1)} %all_to_all.23.plane_ref), channel_id=1, source_target_pairs={{0,4},{4,0},{1,5},{5,1},{2,6},{6,2},{3,7},{7,3},{8,12},{12,8},{9,1... | collective-permute-start | bytes 3538952 | tf_op jit(solution)/shard_map/ppermute | solution.py:374
  103.7 0.3 shard_map.146
  104.1 0.6 dynamic-slice_bitcast_fusion
  104.7 0.6 convert_reduce_fusion
  105.3 0.9 collective-permute-done.3.got_ref
  106.2 1.8 %merge.1 = (bf16[4,4,2,24,768]{4,3,2,1,0:T(8,128)(2,1)}, bf16[768,768]{1,0:T(8,128)(2,1)}) custom-call(s32[1]{0:T(128)} %bitcast.core_ref, bf16[4,4,48,768]{3,2,1,0:T(8,128)(2,1)S(1)} %all_to_all.23.plane_ref, bf16[4,4,48,768]{3,2,1,0:T(8,128)(2,1)S(1)} %collective-permute-done.3.got_ref), custom_call_target="tpu_custom_call" | custom-call | tf_op jit(solution)/shard_map/merge/pallas_call | solution.py:315
  (1 shorter events, 0.0 us)
Async XLA Ops:
  0.6 10.6 %copy-start.1 = (f32[1,768,768]{2,1,0:T(8,128)S(1)}, f32[1,768,768]{2,1,0:T(8,128)}, u32[]{:S(2)}) copy-start(f32[1,768,768]{2,1,0:T(8,128)} %param.9) | copy-start | bytes 7077892
  0.6 10.6 %copy-start.5 = (f32[1,768]{1,0:T(1,128)S(1)}, f32[1,768]{1,0:T(1,128)}, u32[]{:S(2)}) copy-start(f32[1,768]{1,0:T(1,128)} %vector_ref.7) | copy-start | bytes 9220
  0.7 10.6 %copy-start.7 = (f32[24]{0:T(128)S(1)}, f32[24]{0:T(128)}, u32[]{:S(2)}) copy-start(f32[24]{0:T(128)} %param.15) | copy-start | bytes 292
  2.3 12.1 %copy-start = (f32[1,768,768]{2,1,0:T(8,128)S(1)}, f32[1,768,768]{2,1,0:T(8,128)}, u32[]{:S(2)}) copy-start(f32[1,768,768]{2,1,0:T(8,128)} %param.8) | copy-start | bytes 7077892
  2.3 12.1 %copy-start.4 = (f32[1,768]{1,0:T(1,128)S(1)}, f32[1,768]{1,0:T(1,128)}, u32[]{:S(2)}) copy-start(f32[1,768]{1,0:T(1,128)} %vector_ref.6) | copy-start | bytes 9220
  2.4 12.1 %copy-start.6 = (f32[24]{0:T(128)S(1)}, f32[24]{0:T(128)}, u32[]{:S(2)}) copy-start(f32[24]{0:T(128)} %param.14) | copy-start | bytes 292
  2.4 12.0 %collective-permute-start.1 = (f32[17,24,768]{2,1,0:T(8,128)S(1)}, f32[17,24,768]{2,1,0:T(8,128)S(1)}, u32[]{:S(2)}, u32[]{:S(2)}) collective-permute-start(f32[17,24,768]{2,1,0:T(8,128)S(1)} %pick_up.1), channel_id=1, source_target_pairs={{0,4},{4,0},{1,5},{5,1},{2,6},{6,2},{3,7},{7,3},{8,12},{12,8},{9,1... | collective-permute-start | bytes 3760136 | tf_op jit(solution)/shard_map/ppermute | solution.py:358
  12.5 4.8 %collective-permute-start = (f32[17,24,768]{2,1,0:T(8,128)S(1)}, f32[17,24,768]{2,1,0:T(8,128)S(1)}, u32[]{:S(2)}, u32[]{:S(2)}) collective-permute-start(f32[17,24,768]{2,1,0:T(8,128)S(1)} %get-tuple-element.25), channel_id=1, source_target_pairs={{0,4},{4,0},{1,5},{5,1},{2,6},{6,2},{3,7},{7,3},{8,12},{12,8},{9,1... | collective-permute-start | bytes 3760136 | tf_op jit(solution)/shard_map/ppermute | solution.py:360
  38.3 8.4 %copy-start.2 = (f32[24,768]{1,0:T(8,128)S(1)}, f32[24,768]{1,0:T(8,128)}, u32[]{:S(2)}) copy-start(f32[24,768]{1,0:T(8,128)} %up_ref.3) | copy-start | bytes 221188
  38.3 8.4 %copy-start.3 = (f32[768,24]{0,1:T(8,128)S(1)}, f32[768,24]{0,1:T(8,128)}, u32[]{:S(2)}) copy-start(f32[768,24]{0,1:T(8,128)} %param.13) | copy-start | bytes 221188
  39.4 7.3 %collective-permute-start.2 = (bf16[64,768]{1,0:T(8,128)(2,1)S(1)}, bf16[64,768]{1,0:T(8,128)(2,1)S(1)}, u32[]{:S(2)}, u32[]{:S(2)}) collective-permute-start(bf16[64,768]{1,0:T(8,128)(2,1)S(1)} %get-tuple-element.30), channel_id=1, source_target_pairs={{0,64},{64,0},{1,65},{65,1},{2,66},{66,2},{3,67},{67,3},{4,68},{68... | collective-permute-start | bytes 294920 | tf_op jit(solution)/shard_map/ppermute | solution.py:365
  96.4 9.7 %collective-permute-start.3 = (bf16[4,4,48,768]{3,2,1,0:T(8,128)(2,1)S(1)}, bf16[4,4,48,768]{3,2,1,0:T(8,128)(2,1)S(1)}, u32[]{:S(2)}, u32[]{:S(2)}) collective-permute-start(bf16[4,4,48,768]{3,2,1,0:T(8,128)(2,1)S(1)} %all_to_all.23.plane_ref), channel_id=1, source_target_pairs={{0,4},{4,0},{1,5},{5,1},{2,6},{6,2},{3,7},{7,3},{8,12},{12,8},{9,1... | collective-permute-start | bytes 3538952 | tf_op jit(solution)/shard_map/ppermute | solution.py:374

commit v7 on v6

--- a/solution.py
+++ b/solution.py
@@ -287,16 +287,23 @@
             sizes_ref[m, rows] = both
 
 
-def step_kernel(up_ref, down_ref, mean_ref, sizes_ref, next_up_ref, next_down_ref, copies_ref):
+def step_kernel(up_ref, down_ref, mean_ref, sizes_ref, next_up_ref, next_down_ref, half_ref):
     for t, (param_ref, next_ref) in enumerate(((up_ref, next_up_ref), (down_ref, next_down_ref))):
         rows = slice(24 * t, 24 * t + 24)
         sizes = (sizes_ref[0, rows] + sizes_ref[1, rows]) + (sizes_ref[2, rows] + sizes_ref[3, rows])
         ratio = jnp.sqrt(sizes[:, 0:1]) * lax.rsqrt(sizes[:, 64:65] + 1e-06)
         after = param_ref[...] - learn_rate * (mean_ref[rows] * ratio)
         next_ref[...] = after
-        half = after.astype(bf16)
-        for y in range(4):
-            copies_ref[y, rows] = half
+        half_ref[rows] = after.astype(bf16)
+
+
+def copies_kernel(own_ref, other_ref, out_ref):
+    near = lax.axis_index("ya") == 0
+    own, other = own_ref[...], other_ref[...]
+    first, second = jnp.where(near, own, other), jnp.where(near, other, own)
+    for d in range(8):
+        out_ref[d, 0] = first
+        out_ref[d, 1] = second
 
 
 def merge_kernel(core_ref, plane_ref, got_ref, up_ref, down_ref):
@@ -304,7 +311,7 @@
     columns = []
     for y in range(2):
         for x in range(4):
-            mine, other = plane_ref[x, y], got_ref[x, y]
+            mine, other = plane_ref[4 * y + x, 0], got_ref[4 * y + x, 0]
             for c, pair in enumerate((jnp.where(even, mine, other), jnp.where(even, other, mine))):
                 up_ref[y, x, c] = pair[0:24]
                 columns.append(pair.astype(f32)[24:48])
@@ -317,7 +324,7 @@
         grid_spec=pltpu.PrefetchScalarGridSpec(
             num_scalar_prefetch=1,
             grid=(2,),
-            in_specs=[pl.BlockSpec((4, 2, 48, 768), lambda i, c: (0, i, 0, 0))] * 2,
+            in_specs=[pl.BlockSpec((8, 1, 48, 768), lambda i, c: (0, i, 0, 0))] * 2,
             out_specs=(
                 pl.BlockSpec((2, 4, 2, 24, 768), lambda i, c: (i, 0, 0, 0, 0)),
                 pl.BlockSpec((768, 384), lambda i, c: (0, i)),
@@ -365,12 +372,12 @@
     across = lax.ppermute(recoded, "ya", SWAP)
     outs = (shape(48, 768), shape(4, 48, 128), shape(2, 768), shape(2, 8, 768))
     mean, sizes, vectors, params = call(decode_kernel, outs, 5)(kept, rows, across, param_up, turned)
-    outs = (shape(24, 768), shape(24, 768), shape(4, 48, 768, dtype=bf16))
-    next_up, next_down, copies = call(step_kernel, outs, 4)(param_up, turned, mean, exchange(sizes, MODEL))
-    rows = exchange(copies, ("ya", "yb"))
+    outs = (shape(24, 768), shape(24, 768), shape(48, 768, dtype=bf16))
+    next_up, next_down, half = call(step_kernel, outs, 4)(param_up, turned, mean, exchange(sizes, MODEL))
+    copies = call(copies_kernel, shape(8, 2, 48, 768, dtype=bf16), 2)(half, lax.ppermute(half, "ya", SWAP))
     norm, bias = call(vector_kernel, shape(2, 768), 2)(vectors, params)
     at = 24 * lax.axis_index(REPLICA)
-    plane = exchange(jnp.broadcast_to(rows[None], (4, 4, 48, 768)), "x")
+    plane = exchange(copies, ("yb", "x"))
     half_up, half_down = merge(cores, plane, lax.ppermute(plane, "core", SWAP))
     return (
         half_up, half_down, norm.astype(bf16), bias.astype(bf16), next_up, next_down.T,

time: 108 us -> 106 us (0.981)
  blocking collectives: 68.2 us -> 59.3 us
  waiting for transfers between devices: 7.88 us -> 12.4 us
  starting transfers between devices: 20 us -> 21.8 us
    all_to_all x4 -> x3, blocking collectives: 68.2 us -> 59.3 us  [exchange(): return lax.all_to_all(a, axis, 0, 0, tiled=True)]
    ppermute x0 -> x1, waiting for transfers between devices: none -> 4.47 us  [on_device(): lax.ppermute(half, 'ya', SWAP)]
    ppermute x0 -> x1, starting transfers between devices: none -> 1.91 us  [on_device(): lax.ppermute(half, 'ya', SWAP)]
  transfers between devices with their start and end apart: 4 -> 5, of which waited for: 3 -> 4; matrix products, arithmetic and copies ran while one was open for 1% -> 1% of each run, Pallas kernels for 3% -> 3%
where the time goes in v7:
time: 106 us; the launch traced here: 105 us
  blocking collectives  59.3 us (56%)
  starting transfers between devices  21.8 us (21%)
  waiting for transfers between devices  12.4 us (12%)
  Pallas kernels  9.79 us (9%)
  local copies, waits for them, and re-layouts  1.25 us (1%)
    all_to_all x3, blocking collectives, exchange(): return lax.all_to_all(a, axis, 0, 0, tiled=True)  59.3 us
    ppermute x1, starting transfers between devices, on_device(): got_up = lax.ppermute(sent_up, 'core', SWAP)  8.88 us
    ppermute x1, starting transfers between devices, on_device(): half_up, half_down = merge(cores, plane, lax.ppermute(plane, 'core', SWAP))  7.17 us
    ppermute x1, waiting for transfers between devices, on_device(): across = lax.ppermute(recoded, 'ya', SWAP)  5.38 us
    ppermute x1, waiting for transfers between devices, on_device(): lax.ppermute(half, 'ya', SWAP)  4.47 us
  transfers between devices with their start and end apart: 5, of which 4 were waited for; matrix products, arithmetic and copies ran while one was open for 1% of the time, Pallas kernels for 3%

profile of v7, /device:TPU:1, one launch (start us, length us, event | category | flops | bytes accessed | tf_op | source)
XLA Modules:
  0.0 105.4 jit_solution(9925133424058285987)
XLA Ops:
  0.6 0.0 copy-start.1
  0.6 0.0 copy-start.5
  0.7 0.0 copy-start.7
  0.7 1.7 %pick_up.1 = f32[17,24,768]{2,1,0:T(8,128)S(1)} custom-call(s32[1]{0:T(128)} %bitcast.core_ref, f32[16,2,24,768]{3,2,1,0:T(8,128)} %bitcast.13, f32[1,768]{1,0:T(1,128)} %vector_ref.6, f32[1,24]{1,0:T(1,128)} %bitcast.18), custom_call_target="tpu_custom_call" | custom-call | tf_op jit(solution)/shard_map/pick_up/pallas_call | solution.py:115
  2.3 0.0 copy-start
  2.3 0.0 copy-start.4
  2.4 0.0 copy-start.6
  2.4 8.9 %collective-permute-start.1 = (f32[17,24,768]{2,1,0:T(8,128)S(1)}, f32[17,24,768]{2,1,0:T(8,128)S(1)}, u32[]{:S(2)}, u32[]{:S(2)}) collective-permute-start(f32[17,24,768]{2,1,0:T(8,128)S(1)} %pick_up.1), channel_id=1, source_target_pairs={{0,4},{4,0},{1,5},{5,1},{2,6},{6,2},{3,7},{7,3},{8,12},{12,8},{9,1... | collective-permute-start | bytes 3760136 | tf_op jit(solution)/shard_map/ppermute | solution.py:365
  11.3 0.0 copy-done.1
  11.3 0.0 copy-done.5
  11.3 0.0 copy-done.7
  11.3 1.2 %pick_down.1 = (f32[17,24,768]{2,1,0:T(8,128)S(1)}, f32[16,24,768]{2,1,0:T(8,128)S(1)}) custom-call(s32[1]{0:T(128)} %bitcast.core_ref, f32[768,768]{1,0:T(8,128)S(1)} %bitcast.15, f32[1,768]{1,0:T(1,128)S(1)} %copy-done.5, f32[1,24]{1,0:T(1,128)S(1)} %bitcast.20), custom_call_target="tpu_custom_call" | custom-call | tf_op jit(solution)/shard_map/pick_down/pallas_call | solution.py:130
  12.5 1.9 %collective-permute-start = (f32[17,24,768]{2,1,0:T(8,128)S(1)}, f32[17,24,768]{2,1,0:T(8,128)S(1)}, u32[]{:S(2)}, u32[]{:S(2)}) collective-permute-start(f32[17,24,768]{2,1,0:T(8,128)S(1)} %get-tuple-element.25), channel_id=1, source_target_pairs={{0,4},{4,0},{1,5},{5,1},{2,6},{6,2},{3,7},{7,3},{8,12},{12,8},{9,1... | collective-permute-start | bytes 3760136 | tf_op jit(solution)/shard_map/ppermute | solution.py:367
  14.4 0.0 collective-permute-done.1.got_ref.small_ref
  14.4 0.0 copy-done
  14.4 0.0 copy-done.4
  14.4 0.0 copy-done.6
  14.4 1.3 %encode_up.1 = (bf16[8,104,768]{2,1,0:T(8,128)(2,1)S(1)}, f32[8,8,768]{2,1,0:T(8,128)S(1)}) custom-call(s32[1]{0:T(128)} %bitcast.core_ref, f32[4,4,2,24,768]{4,3,2,1,0:T(8,128)S(1)} %bitcast.14, f32[17,24,768]{2,1,0:T(8,128)S(1)} %collective-permute-done.1.got_ref.small_ref, f32[17,24,768]{2,1,0:T(8,128)S(1)} %collective-permute-done.1.got_ref.small_ref, ...), custom_call_target="tpu_custom_call" | custom-call | tf_op jit(solution)/shard_map/encode_up/pallas_call | solution.py:202
  15.7 1.6 %collective-permute-done.got_ref.small_ref = f32[17,24,768]{2,1,0:T(8,128)S(1)} collective-permute-done((f32[17,24,768]{2,1,0:T(8,128)S(1)}, f32[17,24,768]{2,1,0:T(8,128)S(1)}, u32[]{:S(2)}, u32[]{:S(2)}) %collective-permute-start) | collective-permute-done | bytes 1253408 | tf_op jit(solution)/shard_map/ppermute | solution.py:367
  17.3 1.4 %encode_down.1 = bf16[8,104,768]{2,1,0:T(8,128)(2,1)S(1)} custom-call(s32[1]{0:T(128)} %bitcast.core_ref, f32[16,24,768]{2,1,0:T(8,128)S(1)} %get-tuple-element.24.mine_ref, f32[17,24,768]{2,1,0:T(8,128)S(1)} %collective-permute-done.got_ref.small_ref, f32[17,24,768]{2,1,0:T(8,128)S(1)} %collective-permute-done.got_ref.small_ref, ...), custom_call_target="tpu_custom_call", output_to_operand_aliasing={{}: (7, {})} | custom-call | tf_op jit(solution)/shard_map/encode_down/pallas_call | solution.py:220
  18.7 19.6 %all_to_all.15.message_ref = bf16[8,104,768]{2,1,0:T(8,128)(2,1)S(1)} all-to-all(bf16[8,104,768]{2,1,0:T(8,128)(2,1)S(1)} %encode_down.1), channel_id=1, replica_groups=mesh['ens'=4,'ya'=2,'yb'=2,'x'=4,'core'=2,'mz'=2,'my'=2] {'yb','x'}, dimensions={0} | all-to-all | bytes 2555904 | tf_op jit(solution)/shard_map/all_to_all | solution.py:354
  38.3 0.0 copy-start.2
  38.3 0.0 copy-start.3
  38.3 1.1 %shard_map.143 = (f32[48,768]{1,0:T(8,128)S(1)}, f32[16,768]{1,0:T(8,128)S(1)}, bf16[64,768]{1,0:T(8,128)(2,1)S(1)}) custom-call(bf16[8,104,768]{2,1,0:T(8,128)(2,1)S(1)} %all_to_all.15.message_ref), custom_call_target="tpu_custom_call" | custom-call | tf_op jit(solution)/shard_map/pallas_call | solution.py:371
  39.4 1.9 %collective-permute-start.2 = (bf16[64,768]{1,0:T(8,128)(2,1)S(1)}, bf16[64,768]{1,0:T(8,128)(2,1)S(1)}, u32[]{:S(2)}, u32[]{:S(2)}) collective-permute-start(bf16[64,768]{1,0:T(8,128)(2,1)S(1)} %get-tuple-element.30), channel_id=1, source_target_pairs={{0,64},{64,0},{1,65},{65,1},{2,66},{66,2},{3,67},{67,3},{4,68},{68... | collective-permute-start | bytes 294920 | tf_op jit(solution)/shard_map/ppermute | solution.py:372
  41.3 5.4 %collective-permute-done.2.message_ref = bf16[64,768]{1,0:T(8,128)(2,1)S(1)} collective-permute-done((bf16[64,768]{1,0:T(8,128)(2,1)S(1)}, bf16[64,768]{1,0:T(8,128)(2,1)S(1)}, u32[]{:S(2)}, u32[]{:S(2)}) %collective-permute-start.2) | collective-permute-done | bytes 98336 | tf_op jit(solution)/shard_map/ppermute | solution.py:372
  46.7 0.0 copy-done.2
  46.7 0.0 copy-done.3
  46.7 0.2 shard_map.144
  46.9 22.8 %all_to_all.16.sizes_ref = f32[4,48,128]{2,1,0:T(8,128)S(1)} all-to-all(f32[4,48,128]{2,1,0:T(8,128)S(1)} %get-tuple-element.32), channel_id=1, replica_groups=mesh['ens'=4,'ya'=2,'yb'=2,'x'=4,'core'=2,'mz'=2,'my'=2] {'mz','my'}, dimensions={0} | all-to-all | bytes 196608 | tf_op jit(solution)/shard_map/all_to_all | solution.py:354
  69.7 0.8 shard_map.145
  70.6 1.9 %collective-permute-start.3 = (bf16[48,768]{1,0:T(8,128)(2,1)S(1)}, bf16[48,768]{1,0:T(8,128)(2,1)S(1)}, u32[]{:S(2)}, u32[]{:S(2)}) collective-permute-start(bf16[48,768]{1,0:T(8,128)(2,1)S(1)} %get-tuple-element.33.own_ref), channel_id=1, source_target_pairs={{0,64},{64,0},{1,65},{65,1},{2,66},{66,2},{3,67},{67,3},{4,68},{68... | collective-permute-start | bytes 221192 | tf_op jit(solution)/shard_map/ppermute | solution.py:377
  72.5 4.5 %collective-permute-done.3.other_ref = bf16[48,768]{1,0:T(8,128)(2,1)S(1)} collective-permute-done((bf16[48,768]{1,0:T(8,128)(2,1)S(1)}, bf16[48,768]{1,0:T(8,128)(2,1)S(1)}, u32[]{:S(2)}, u32[]{:S(2)}) %collective-permute-start.3) | collective-permute-done | bytes 73760 | tf_op jit(solution)/shard_map/ppermute | solution.py:377
  76.9 0.1 shard_map.146
  77.0 16.9 %all_to_all.17.plane_ref = bf16[8,2,48,768]{3,2,1,0:T(8,128)(2,1)S(1)} all-to-all(bf16[8,2,48,768]{3,2,1,0:T(8,128)(2,1)S(1)} %shard_map.146), channel_id=1, replica_groups=mesh['ens'=4,'ya'=2,'yb'=2,'x'=4,'core'=2,'mz'=2,'my'=2] {'yb','x'}, dimensions={0} | all-to-all | bytes 2359296 | tf_op jit(solution)/shard_map/all_to_all | solution.py:354
  93.9 7.2 %collective-permute-start.4 = (bf16[8,2,48,768]{3,2,1,0:T(8,128)(2,1)S(1)}, bf16[8,2,48,768]{3,2,1,0:T(8,128)(2,1)S(1)}, u32[]{:S(2)}, u32[]{:S(2)}) collective-permute-start(bf16[8,2,48,768]{3,2,1,0:T(8,128)(2,1)S(1)} %all_to_all.17.plane_ref), channel_id=1, source_target_pairs={{0,4},{4,0},{1,5},{5,1},{2,6},{6,2},{3,7},{7,3},{8,12},{12,8},{9,1... | collective-permute-start | bytes 3538952 | tf_op jit(solution)/shard_map/ppermute | solution.py:381
  101.1 0.3 shard_map.147
  101.5 0.6 dynamic-slice_bitcast_fusion
  102.1 0.6 convert_reduce_fusion
  102.7 0.9 collective-permute-done.4.got_ref
  103.6 1.8 %merge.1 = (bf16[4,4,2,24,768]{4,3,2,1,0:T(8,128)(2,1)}, bf16[768,768]{1,0:T(8,128)(2,1)}) custom-call(s32[1]{0:T(128)} %bitcast.core_ref, bf16[8,2,48,768]{3,2,1,0:T(8,128)(2,1)S(1)} %all_to_all.17.plane_ref, bf16[8,2,48,768]{3,2,1,0:T(8,128)(2,1)S(1)} %collective-permute-done.4.got_ref), custom_call_target="tpu_custom_call" | custom-call | tf_op jit(solution)/shard_map/merge/pallas_call | solution.py:322
  (1 shorter events, 0.0 us)
Async XLA Ops:
  0.6 10.6 %copy-start.1 = (f32[1,768,768]{2,1,0:T(8,128)S(1)}, f32[1,768,768]{2,1,0:T(8,128)}, u32[]{:S(2)}) copy-start(f32[1,768,768]{2,1,0:T(8,128)} %param.9) | copy-start | bytes 7077892
  0.6 10.6 %copy-start.5 = (f32[1,768]{1,0:T(1,128)S(1)}, f32[1,768]{1,0:T(1,128)}, u32[]{:S(2)}) copy-start(f32[1,768]{1,0:T(1,128)} %vector_ref.7) | copy-start | bytes 9220
  0.7 10.6 %copy-start.7 = (f32[24]{0:T(128)S(1)}, f32[24]{0:T(128)}, u32[]{:S(2)}) copy-start(f32[24]{0:T(128)} %param.15) | copy-start | bytes 292
  2.3 12.1 %copy-start = (f32[1,768,768]{2,1,0:T(8,128)S(1)}, f32[1,768,768]{2,1,0:T(8,128)}, u32[]{:S(2)}) copy-start(f32[1,768,768]{2,1,0:T(8,128)} %param.8) | copy-start | bytes 7077892
  2.3 12.1 %copy-start.4 = (f32[1,768]{1,0:T(1,128)S(1)}, f32[1,768]{1,0:T(1,128)}, u32[]{:S(2)}) copy-start(f32[1,768]{1,0:T(1,128)} %vector_ref.6) | copy-start | bytes 9220
  2.4 12.1 %copy-start.6 = (f32[24]{0:T(128)S(1)}, f32[24]{0:T(128)}, u32[]{:S(2)}) copy-start(f32[24]{0:T(128)} %param.14) | copy-start | bytes 292
  2.4 12.0 %collective-permute-start.1 = (f32[17,24,768]{2,1,0:T(8,128)S(1)}, f32[17,24,768]{2,1,0:T(8,128)S(1)}, u32[]{:S(2)}, u32[]{:S(2)}) collective-permute-start(f32[17,24,768]{2,1,0:T(8,128)S(1)} %pick_up.1), channel_id=1, source_target_pairs={{0,4},{4,0},{1,5},{5,1},{2,6},{6,2},{3,7},{7,3},{8,12},{12,8},{9,1... | collective-permute-start | bytes 3760136 | tf_op jit(solution)/shard_map/ppermute | solution.py:365
  12.5 4.8 %collective-permute-start = (f32[17,24,768]{2,1,0:T(8,128)S(1)}, f32[17,24,768]{2,1,0:T(8,128)S(1)}, u32[]{:S(2)}, u32[]{:S(2)}) collective-permute-start(f32[17,24,768]{2,1,0:T(8,128)S(1)} %get-tuple-element.25), channel_id=1, source_target_pairs={{0,4},{4,0},{1,5},{5,1},{2,6},{6,2},{3,7},{7,3},{8,12},{12,8},{9,1... | collective-permute-start | bytes 3760136 | tf_op jit(solution)/shard_map/ppermute | solution.py:367
  38.3 8.4 %copy-start.2 = (f32[24,768]{1,0:T(8,128)S(1)}, f32[24,768]{1,0:T(8,128)}, u32[]{:S(2)}) copy-start(f32[24,768]{1,0:T(8,128)} %up_ref.3) | copy-start | bytes 221188
  38.3 8.4 %copy-start.3 = (f32[768,24]{0,1:T(8,128)S(1)}, f32[768,24]{0,1:T(8,128)}, u32[]{:S(2)}) copy-start(f32[768,24]{0,1:T(8,128)} %param.13) | copy-start | bytes 221188
  39.4 7.3 %collective-permute-start.2 = (bf16[64,768]{1,0:T(8,128)(2,1)S(1)}, bf16[64,768]{1,0:T(8,128)(2,1)S(1)}, u32[]{:S(2)}, u32[]{:S(2)}) collective-permute-start(bf16[64,768]{1,0:T(8,128)(2,1)S(1)} %get-tuple-element.30), channel_id=1, source_target_pairs={{0,64},{64,0},{1,65},{65,1},{2,66},{66,2},{3,67},{67,3},{4,68},{68... | collective-permute-start | bytes 294920 | tf_op jit(solution)/shard_map/ppermute | solution.py:372
  70.6 6.4 %collective-permute-start.3 = (bf16[48,768]{1,0:T(8,128)(2,1)S(1)}, bf16[48,768]{1,0:T(8,128)(2,1)S(1)}, u32[]{:S(2)}, u32[]{:S(2)}) collective-permute-start(bf16[48,768]{1,0:T(8,128)(2,1)S(1)} %get-tuple-element.33.own_ref), channel_id=1, source_target_pairs={{0,64},{64,0},{1,65},{65,1},{2,66},{66,2},{3,67},{67,3},{4,68},{68... | collective-permute-start | bytes 221192 | tf_op jit(solution)/shard_map/ppermute | solution.py:377
  93.9 9.6 %collective-permute-start.4 = (bf16[8,2,48,768]{3,2,1,0:T(8,128)(2,1)S(1)}, bf16[8,2,48,768]{3,2,1,0:T(8,128)(2,1)S(1)}, u32[]{:S(2)}, u32[]{:S(2)}) collective-permute-start(bf16[8,2,48,768]{3,2,1,0:T(8,128)(2,1)S(1)} %all_to_all.17.plane_ref), channel_id=1, source_target_pairs={{0,4},{4,0},{1,5},{5,1},{2,6},{6,2},{3,7},{7,3},{8,12},{12,8},{9,1... | collective-permute-start | bytes 3538952 | tf_op jit(solution)/shard_map/ppermute | solution.py:381
